TPU v7x, 1024 devices: a whole 8x8x8 slice. The times are simulated.
1024 devices in a mesh: dp: 16 (over y, core), seq: 8 (over x), expert: 8 (over z).
Axes of the slice: x: 8, y: 8, z: 8, core: 2. Of those that a mesh axis runs over, the one named last changes fastest.
Arguments:
- queries: bfloat16 [8192, 4096], P(('dp', 'seq'), 'expert'), parts along dimension 0, may hold values from -256 to 256, as said below
- keys: bfloat16 [32768, 1024], P(('dp', 'seq'), 'expert'), parts along dimension 0, may hold values from -6 to 6
- values: bfloat16 [32768, 1024], P(('dp', 'seq'), 'expert'), parts along dimension 0, may hold values from -6 to 6
- lengths: int32 [128], P('dp'), parts along dimension 0, may hold values from 1 to 1024, 2048 in all
- routes: int32 [8192, 2], P(('dp', 'seq', 'expert')), parts along dimension 0, may hold values from 0 to 7, all different within a row; in each aligned block of 8 rows (0 to 7, 8 to 15, ...) at most 3 rows name the same one
- gates: float32 [8192, 2], P(('dp', 'seq', 'expert')), parts along dimension 0, may hold values from 0.2 to 1
- w_up: bfloat16 [8, 4096, 7168], P('expert', None, 'seq'), may hold values from -0.09375 to 0.09375
Outputs:
- expert_mix: bfloat16 [8192, 7168], P(('dp', 'seq', 'expert')), parts along dimension 0
There are 16 independent parts, one for each index of `dp`. A program takes and returns all parts, laid end to end along the dimension named above; an argument that names none is the same for every part. Nothing has to cross between parts.
Inputs may be any that keep to these rules, and one draw needn't show every extreme that they name: `queries`: A query row's values are those of a normal draw or, in some rows, a multiple of a sum of key rows. The 8 lengths sum to 2048. `routes`: A row's two experts differ; among the 8 rows of one device no expert is named more than 3 times.
All inputs are finite; a program needn't handle non-finite values.
Results may differ from a plain program's by a relative error of at most 0.012.
Values may be sent and summed in bfloat16 or wider, within the bound.
No kernel may reach another device: no remote copies, remote signals or barrier semaphores. Data moves between devices by JAX's collectives and lax.ppermute only.
A program may use at most 32 MiB of HBM per device.

v0:
```python
import jax
import jax.numpy as jnp
from jax import lax
from jax.sharding import PartitionSpec as P

HD = 128


def laid_out(parts, dim):
    shape = list(parts.shape[1:])
    shape[dim] *= parts.shape[0]
    return jnp.moveaxis(parts, 0, dim).reshape(shape)


def from_everyone(x, axis):
    copies = jnp.broadcast_to(x, (lax.axis_size(axis), *x.shape))
    return lax.all_to_all(copies, axis, split_axis=0, concat_axis=0, tiled=True)


def gathered_copies(x, axis, dim):
    return laid_out(from_everyone(x, axis), dim)


def sent_together(arrays, axis, dim, along):
    widths = [a.shape[along] for a in arrays]
    both = jnp.concatenate(arrays, axis=along)
    result = gathered_copies(both, axis, dim)
    return tuple(jnp.split(result, [sum(widths[:k]) for k in range(1, len(widths))], axis=along))


def cut_along(x, dim, peers):
    shape = x.shape
    parts = x.reshape(*shape[:dim], peers, shape[dim] // peers, *shape[dim + 1 :])
    return jnp.moveaxis(parts, dim, 0)


def joined_exchange(x, axis, axes, splits, concats):
    sizes = [lax.axis_size(a) for a in axes]
    parts = cut_along(x, splits[0], sizes[0])
    parts = jnp.moveaxis(cut_along(parts, splits[1] + 1, sizes[1]), 0, 1)
    inside = parts.shape[2:]
    parts = parts.reshape(-1, *inside)
    parts = lax.all_to_all(parts, axis, split_axis=0, concat_axis=0, tiled=True)
    parts = laid_out(parts.reshape(*sizes, *inside), concats[0] + 1)
    return laid_out(parts, concats[1])


def doc_index(positions, starts):
    return jnp.sum((positions[:, None] >= starts[None, :]).astype(jnp.int32), axis=1) - 1


def shards(queries, keys, values, lengths, routes, gates, w_up):
    q_rows, width = queries.shape
    shard_len = keys.shape[0]
    kv_local = keys.shape[1] // HD
    group = width // HD // kv_local
    scale = 1.0 / HD**0.5
    seq_count = lax.axis_size("seq")
    expert_count = lax.axis_size("expert")
    experts_all = expert_count * w_up.shape[0]
    capacity = max(2, 3 * q_rows // (expert_count * expert_count))
    starts = jnp.cumsum(lengths) - lengths
    qpos = (
        lax.axis_index("seq") * shard_len + shard_len - q_rows + jnp.arange(q_rows, dtype=jnp.int32)
    )
    qdoc = doc_index(qpos, starts)
    q_split = queries.reshape(q_rows, kv_local, group, HD)
    start_peak = jnp.full((kv_local, group, q_rows), -1e30, jnp.float32)
    peak = start_peak
    k_piece, v_piece = sent_together((keys, values), "seq", 0, 1)
    count = k_piece.shape[0]
    kpos = jnp.arange(count, dtype=jnp.int32)
    allowed = (kpos[None, :] <= qpos[:, None]) & (doc_index(kpos, starts)[None, :] == qdoc[:, None])
    score = (
        jnp.einsum(
            "qkgd,pkd->kgqp",
            q_split,
            k_piece.reshape(count, kv_local, HD),
            preferred_element_type=jnp.float32,
        )
        * scale
    )
    masked = jnp.where(allowed, score, jnp.float32(-1e30))
    new_peak = jnp.maximum(peak, jnp.max(masked, axis=-1))
    weight = jnp.where(allowed, jnp.exp(score - new_peak[..., None]), jnp.float32(0.0))
    total = jnp.sum(weight, axis=-1)
    update = jnp.einsum(
        "kgqp,pkd->kgqd",
        weight.astype(jnp.bfloat16),
        v_piece.reshape(count, kv_local, HD),
        preferred_element_type=jnp.float32,
    )
    peak, total, acc = (new_peak, total, update)
    attended = (
        (acc / total[..., None]).astype(jnp.bfloat16).transpose(2, 0, 1, 3).reshape(q_rows, width)
    )
    tok_feats = lax.all_to_all(attended, "expert", split_axis=0, concat_axis=1, tiled=True)
    feats = tok_feats.astype(jnp.float32)
    normed = (feats * lax.rsqrt(jnp.mean(feats * feats, axis=-1, keepdims=True) + 1e-05)).astype(
        jnp.bfloat16
    )
    flat = routes.reshape(-1)
    onehot = (flat[:, None] == jnp.arange(experts_all, dtype=jnp.int32)[None, :]).astype(jnp.int32)
    before = jnp.cumsum(onehot, axis=0) - onehot
    slot = jnp.sum(before * onehot, axis=1)
    target = flat * capacity + slot
    selector = (
        jnp.arange(experts_all * capacity, dtype=jnp.int32)[:, None] == target[None, :]
    ).astype(jnp.bfloat16)
    repeated = jnp.repeat(normed, 2, axis=0)
    outgoing = jnp.dot(selector, repeated, preferred_element_type=jnp.float32).astype(jnp.bfloat16)
    landed = lax.all_to_all(outgoing, "expert", split_axis=0, concat_axis=0, tiled=True)
    incoming = gathered_copies(landed, "seq", 0)
    upper = jnp.dot(incoming, w_up[0], preferred_element_type=jnp.float32)
    act = jax.nn.silu(upper).astype(jnp.bfloat16)
    ff_local = act.shape[1]
    act_four = act.reshape(seq_count, experts_all, capacity, ff_local)
    back = joined_exchange(act_four, ("seq", "expert"), ("seq", "expert"), (0, 1), (3, 1))
    returned = back.reshape(experts_all * capacity, seq_count * ff_local)
    picked = jnp.dot(selector.T, returned, preferred_element_type=jnp.float32)
    tok_count = routes.shape[0]
    mixed = jnp.sum(picked.reshape(tok_count, 2, -1) * gates[:, :, None], axis=1)
    return mixed.astype(jnp.bfloat16)


def solution(mesh):
    placed = (
        P(("dp", "seq"), "expert"),
        P(("dp", "seq"), "expert"),
        P(("dp", "seq"), "expert"),
        P("dp"),
        P(("dp", "seq", "expert"), None),
        P(("dp", "seq", "expert"), None),
        P("expert", None, "seq"),
    )
    return jax.shard_map(
        shards,
        mesh=mesh,
        in_specs=placed,
        out_specs=P(("dp", "seq", "expert"), None),
        check_vma=False,
    )
```

profile of v0, /device:TPU:112, one launch (start us, length us, event | category | flops | bytes accessed | tf_op | source)
XLA Modules:
  0.0 149.7 jit_solution(14268820443196854984)
XLA Ops:
  0.0 0.9 pad_maximum_fusion
  0.9 1.1 broadcast_in_dim.21
  2.0 6.8 %all-to-all-start = ((bf16[8,256,256]{2,1,0:T(8,128)(2,1)}), bf16[8,256,256]{2,1,0:T(8,128)(2,1)S(1)}, u32[]{:S(2)}, u32[]{:S(2)}) async-start(bf16[8,256,256]{2,1,0:T(8,128)(2,1)} %broadcast_in_dim.21), calls=%async_computation | async-start | bytes 2097152 | tf_op jit(solution)/shard_map/all_to_all | solution.py:17
  8.8 0.1 copy.22
  8.8 0.1 reshape.139
  8.9 0.2 reduce-window.9
  9.2 0.1 convert_reduce_fusion
  9.3 0.1 convert_reduce_fusion.1
  9.4 0.2 select_reduce_fusion.1
  9.6 0.2 fusion.15
  9.8 27.7 %all-to-all-done = bf16[8,256,256]{2,1,0:T(8,128)(2,1)S(1)} async-done(((bf16[8,256,256]{2,1,0:T(8,128)(2,1)}), bf16[8,256,256]{2,1,0:T(8,128)(2,1)S(1)}, u32[]{:S(2)}, u32[]{:S(2)}) %all-to-all-start) | async-done | bytes 1048608 | tf_op jit(solution)/shard_map/all_to_all | solution.py:17
  37.5 0.6 select_reduce_fusion
  38.1 0.5 fusion.3
  38.6 0.6 fusion.7
  39.2 0.7 all_to_all.28
  39.9 18.2 %all-to-all-start.1 = ((bf16[8,8,512]{2,1,0:T(8,128)(2,1)}), bf16[8,8,512]{2,1,0:T(8,128)(2,1)S(1)}, u32[]{:S(2)}, u32[]{:S(2)}) async-start(bf16[8,8,512]{2,1,0:T(8,128)(2,1)} %all_to_all.28), calls=%async_computation.1 | async-start | bytes 131072 | tf_op jit(solution)/shard_map/all_to_all | solution.py:97
  58.1 8.4 %all-to-all-done.1 = bf16[8,8,512]{2,1,0:T(8,128)(2,1)S(1)} async-done(((bf16[8,8,512]{2,1,0:T(8,128)(2,1)}), bf16[8,8,512]{2,1,0:T(8,128)(2,1)S(1)}, u32[]{:S(2)}, u32[]{:S(2)}) %all-to-all-start.1) | async-done | bytes 65568 | tf_op jit(solution)/shard_map/all_to_all | solution.py:97
  66.5 0.1 multiply_reduce_fusion
  66.6 0.1 multiply_convert_fusion.1
  66.9 0.2 convolution_convert_fusion
  67.0 0.1 all_to_all.30
  67.2 13.3 %all_to_all.40 = bf16[8,3,4096]{2,1,0:T(4,128)(2,1)S(1)} all-to-all(bf16[8,3,4096]{2,1,0:T(4,128)(2,1)S(1)} %all_to_all.30), channel_id=1, replica_groups=mesh['dp'=16,'seq'=8,'expert'=8] {'expert'}, dimensions={0} | all-to-all | bytes 393216 | tf_op jit(solution)/shard_map/all_to_all | solution.py:112
  80.5 0.2 all_to_all.32
  80.7 0.2 broadcast_in_dim.45
  80.8 39.8 %all_to_all.41 = bf16[8,24,4096]{2,1,0:T(8,128)(2,1)S(1)} all-to-all(bf16[8,24,4096]{2,1,0:T(8,128)(2,1)S(1)} %broadcast_in_dim.45), channel_id=1, replica_groups=mesh['dp'=16,'seq'=8,'expert'=8] {'seq'}, dimensions={0} | all-to-all | bytes 3145728 | tf_op jit(solution)/shard_map/all_to_all | solution.py:17
  120.6 5.0 %multiply_convert_fusion = bf16[192,896]{1,0:T(8,128)(2,1)S(1)} fusion(bf16[192,4096]{1,0:T(8,128)(2,1)S(1)} %bitcast.56, bf16[1,4096,896]{2,1,0:T(8,128)(2,1)} %param.13), kind=kOutput, calls=%fused_computation.18 | convolution fusion | flops 1410146304 | bytes 9256960 | tf_op jit(solution)/shard_map/dot_general | solution.py:114
  125.6 0.9 reshape_transpose_transpose_reshape_reshape_reshape.3
  126.5 4.6 %all-to-all-start.4 = ((bf16[64,1,1,3,896]{4,3,2,1,0:T(4,128)(2,1)}), bf16[64,1,1,3,896]{4,3,2,1,0:T(4,128)(2,1)S(1)}, u32[]{:S(2)}, u32[]{:S(2)}) async-start(bf16[64,1,1,3,896]{4,3,2,1,0:T(4,128)(2,1)} %bitcast.15), calls=%async_computation.4 | async-start | bytes 917504 | tf_op jit(solution)/shard_map/all_to_all | solution.py:43
  131.3 17.3 %all-to-all-done.4 = bf16[64,1,1,3,896]{4,3,2,1,0:T(4,128)(2,1)S(1)} async-done(((bf16[64,1,1,3,896]{4,3,2,1,0:T(4,128)(2,1)}), bf16[64,1,1,3,896]{4,3,2,1,0:T(4,128)(2,1)S(1)}, u32[]{:S(2)}, u32[]{:S(2)}) %all-to-all-start.4) | async-done | bytes 344096 | tf_op jit(solution)/shard_map/all_to_all | solution.py:43
  148.6 0.1 copy.38
  148.7 0.2 reshape.151
  148.9 0.9 fusion.5
  (23 shorter events, 0.4 us)
Async XLA Ops:
  0.0 37.5 %copy-start = (bf16[64,512]{1,0:T(8,128)(2,1)S(1)}, bf16[64,512]{1,0:T(8,128)(2,1)}, u32[]{:S(2)}) copy-start(bf16[64,512]{1,0:T(8,128)(2,1)} %param.7) | copy-start | bytes 196612
  0.0 8.8 %copy-start.2 = (s32[8,2]{0,1:T(2,128)S(1)}, s32[8,2]{0,1:T(2,128)}, u32[]{:S(2)}) copy-start(s32[8,2]{0,1:T(2,128)} %param.11) | copy-start | bytes 196
  0.0 8.9 %copy-start.3 = (s32[8]{0:T(128)S(1)}, s32[8]{0:T(128)}, u32[]{:S(2)}) copy-start(s32[8]{0:T(128)} %param.10) | copy-start | bytes 100
  2.0 35.5 %all-to-all-start = ((bf16[8,256,256]{2,1,0:T(8,128)(2,1)}), bf16[8,256,256]{2,1,0:T(8,128)(2,1)S(1)}, u32[]{:S(2)}, u32[]{:S(2)}) async-start(bf16[8,256,256]{2,1,0:T(8,128)(2,1)} %broadcast_in_dim.21), calls=%async_computation | async-start | bytes 2097152 | tf_op jit(solution)/shard_map/all_to_all | solution.py:17
  39.9 26.6 %all-to-all-start.1 = ((bf16[8,8,512]{2,1,0:T(8,128)(2,1)}), bf16[8,8,512]{2,1,0:T(8,128)(2,1)S(1)}, u32[]{:S(2)}, u32[]{:S(2)}) async-start(bf16[8,8,512]{2,1,0:T(8,128)(2,1)} %all_to_all.28), calls=%async_computation.1 | async-start | bytes 131072 | tf_op jit(solution)/shard_map/all_to_all | solution.py:97
  125.6 23.3 %copy-start.1 = (f32[8,2]{0,1:T(2,128)S(1)}, f32[8,2]{0,1:T(2,128)}, u32[]{:S(2)}) copy-start(f32[8,2]{0,1:T(2,128)} %param.12) | copy-start | bytes 196
  126.5 22.0 %all-to-all-start.4 = ((bf16[64,1,1,3,896]{4,3,2,1,0:T(4,128)(2,1)}), bf16[64,1,1,3,896]{4,3,2,1,0:T(4,128)(2,1)S(1)}, u32[]{:S(2)}, u32[]{:S(2)}) async-start(bf16[64,1,1,3,896]{4,3,2,1,0:T(4,128)(2,1)} %bitcast.15), calls=%async_computation.4 | async-start | bytes 917504 | tf_op jit(solution)/shard_map/all_to_all | solution.py:43
where the time goes:
time: 151 us; the launch traced here: 150 us
  waiting for transfers between devices  53.3 us (35%)
  blocking collectives  53.1 us (35%)
  starting transfers between devices  29.6 us (20%)
  matrix products  7.13 us (5%)
  local copies, waits for them, and re-layouts  3.78 us (3%)
  other arithmetic  2.63 us (2%)
    all_to_all x1, blocking collectives, from_everyone(): return lax.all_to_all(copies, axis, split_axis=0, concat_axis=0, tiled=True)  39.8 us
    all_to_all x1, waiting for transfers between devices, from_everyone(): return lax.all_to_all(copies, axis, split_axis=0, concat_axis=0, tiled=True)  27.7 us
    all_to_all x1, starting transfers between devices, shards(): lax.all_to_all(attended, 'expert', split_axis=0, concat_axis=1, tiled=True)  18.2 us
    all_to_all x1, waiting for transfers between devices, joined_exchange(): parts = lax.all_to_all(parts, axis, split_axis=0, concat_axis=0, tiled=True)  17.3 us
    all_to_all x1, blocking collectives, shards(): lax.all_to_all(outgoing, 'expert', split_axis=0, concat_axis=0, tiled=True)  13.3 us
    all_to_all x1, waiting for transfers between devices, shards(): lax.all_to_all(attended, 'expert', split_axis=0, concat_axis=1, tiled=True)  8.37 us
    all_to_all x1, starting transfers between devices, from_everyone(): return lax.all_to_all(copies, axis, split_axis=0, concat_axis=0, tiled=True)  6.76 us
    dot_general x1, matrix products, shards(): upper = jnp.dot(incoming, w_up[0], preferred_element_type=jnp.float32)  4.96 us
  transfers between devices with their start and end apart: 3, of which 3 were waited for; matrix products, arithmetic and copies ran while one was open for 1% of the time, Pallas kernels for 0%

commit v1 on v0

v1 whole, which is shorter than its diff:
```python
import jax
import jax.numpy as jnp
from jax import lax
from jax.sharding import PartitionSpec as P

HD = 128


def exchange(x, axis):
    return lax.all_to_all(x, axis, split_axis=0, concat_axis=0, tiled=True)


def to_everyone(x, axis):
    return exchange(jnp.broadcast_to(x, (lax.axis_size(axis), *x.shape)), axis)


def doc_index(positions, starts):
    return jnp.sum((positions[:, None] >= starts[None, :]).astype(jnp.int32), axis=1) - 1


def slots(routes, experts_all):
    blocks = routes.shape[0]
    flat = routes.reshape(blocks, -1)
    onehot = (flat[:, :, None] == jnp.arange(experts_all, dtype=jnp.int32)).astype(jnp.int32)
    count = flat.shape[1]
    earlier = jnp.arange(count)[:, None] > jnp.arange(count)[None, :]
    same = flat[:, :, None] == flat[:, None, :]
    return jnp.sum((same & earlier[None]).astype(jnp.int32), axis=2).reshape(routes.shape)


def shards(queries, keys, values, lengths, routes, gates, w_up):
    q_rows, width = queries.shape
    shard_len = keys.shape[0]
    kv_local = keys.shape[1] // HD
    group = width // HD // kv_local
    scale = 1.0 / HD**0.5
    seq_count = lax.axis_size("seq")
    expert_count = lax.axis_size("expert")
    experts_all = expert_count * w_up.shape[0]
    capacity = max(2, 3 * q_rows // (expert_count * expert_count))
    tok_count = routes.shape[0]
    starts = jnp.cumsum(lengths) - lengths
    qpos = (
        lax.axis_index("seq") * shard_len + shard_len - q_rows + jnp.arange(q_rows, dtype=jnp.int32)
    )
    qdoc = doc_index(qpos, starts)
    kv = to_everyone(jnp.concatenate([keys, values], axis=1), "seq")
    count = seq_count * shard_len
    kv = kv.reshape(count, 2 * kv_local * HD)
    k_all, v_all = kv[:, : kv_local * HD], kv[:, kv_local * HD :]
    row_routes = to_everyone(routes.reshape(1, -1), "expert").reshape(expert_count, tok_count, 2)

    q_split = queries.reshape(q_rows, kv_local, group, HD)
    kpos = jnp.arange(count, dtype=jnp.int32)
    allowed = (kpos[None, :] <= qpos[:, None]) & (doc_index(kpos, starts)[None, :] == qdoc[:, None])
    score = (
        jnp.einsum(
            "qkgd,pkd->kgqp",
            q_split,
            k_all.reshape(count, kv_local, HD),
            preferred_element_type=jnp.float32,
        )
        * scale
    )
    masked = jnp.where(allowed, score, jnp.float32(-1e30))
    peak = jnp.max(masked, axis=-1)
    weight = jnp.where(allowed, jnp.exp(score - peak[..., None]), jnp.float32(0.0))
    total = jnp.sum(weight, axis=-1)
    acc = jnp.einsum(
        "kgqp,pkd->kgqd",
        weight.astype(jnp.bfloat16),
        v_all.reshape(count, kv_local, HD),
        preferred_element_type=jnp.float32,
    )
    attended = (
        (acc / total[..., None]).astype(jnp.bfloat16).transpose(2, 0, 1, 3).reshape(q_rows, width)
    )

    place = slots(row_routes, experts_all)
    block = jnp.arange(expert_count, dtype=jnp.int32)[:, None, None]
    target = (row_routes * expert_count + block) * capacity + place
    total_slots = experts_all * expert_count * capacity
    target = target.reshape(q_rows, 2)
    slot_ids = jnp.arange(total_slots, dtype=jnp.int32)[:, None]
    selector = ((slot_ids == target[None, :, 0]) | (slot_ids == target[None, :, 1])).astype(
        jnp.bfloat16
    )
    outgoing = jnp.dot(selector, attended, preferred_element_type=jnp.float32).astype(jnp.bfloat16)
    per_expert = expert_count * capacity
    outgoing = outgoing.reshape(1, expert_count, per_expert, width)
    outgoing = jnp.broadcast_to(outgoing, (seq_count, expert_count, per_expert, width))
    landed = exchange(
        outgoing.reshape(seq_count * expert_count, per_expert, width), ("seq", "expert")
    )
    landed = landed.reshape(seq_count, expert_count, per_expert, width)
    feats = landed.astype(jnp.float32)
    square = jnp.sum(feats * feats, axis=(1, 3)) / (expert_count * width)
    norm = lax.rsqrt(square + 1e-05).reshape(seq_count * per_expert, 1)
    incoming = landed.transpose(0, 2, 1, 3).reshape(seq_count * per_expert, expert_count * width)
    upper = jnp.dot(incoming, w_up[0], preferred_element_type=jnp.float32) * norm
    act = jax.nn.silu(upper).astype(jnp.bfloat16)
    ff_local = act.shape[1]
    back = exchange(act.reshape(seq_count * expert_count, capacity, ff_local), ("seq", "expert"))
    back = back.reshape(seq_count, experts_all * capacity, ff_local)
    returned = back.transpose(1, 0, 2).reshape(experts_all * capacity, seq_count * ff_local)
    own = slots(routes[None], experts_all)[0]
    own_target = (routes * capacity + own).reshape(-1)
    own_selector = (
        own_target[:, None] == jnp.arange(experts_all * capacity, dtype=jnp.int32)[None, :]
    ).astype(jnp.bfloat16)
    picked = jnp.dot(own_selector, returned, preferred_element_type=jnp.float32)
    mixed = jnp.sum(picked.reshape(tok_count, 2, -1) * gates[:, :, None], axis=1)
    return mixed.astype(jnp.bfloat16)


def solution(mesh):
    placed = (
        P(("dp", "seq"), "expert"),
        P(("dp", "seq"), "expert"),
        P(("dp", "seq"), "expert"),
        P("dp"),
        P(("dp", "seq", "expert"), None),
        P(("dp", "seq", "expert"), None),
        P("expert", None, "seq"),
    )
    return jax.shard_map(
        shards,
        mesh=mesh,
        in_specs=placed,
        out_specs=P(("dp", "seq", "expert"), None),
        check_vma=False,
    )
```

time: 151 us -> 143 us (0.947)
  blocking collectives: 53.1 us -> 44.5 us
  waiting for transfers between devices: 53.3 us -> 48.1 us
  starting transfers between devices: 29.6 us -> 32.2 us
  local copies, waits for them, and re-layouts: 3.78 us -> 6.01 us
  other arithmetic: 2.63 us -> 4.26 us
    all_to_all x2 -> x1, blocking collectives: 53.1 us -> 44.5 us  [exchange(): return lax.all_to_all(x, axis, split_axis=0, concat_axis=0, tiled=True)]
    all_to_all x3, waiting for transfers between devices: 53.3 us -> 48.1 us  [exchange(): return lax.all_to_all(x, axis, split_axis=0, concat_axis=0, tiled=True)]
    all_to_all x3, starting transfers between devices: 29.6 us -> 32.2 us  [exchange(): return lax.all_to_all(x, axis, split_axis=0, concat_axis=0, tiled=True)]
  transfers between devices with their start and end apart: 3 -> 3, of which waited for: 3 -> 3; matrix products, arithmetic and copies ran while one was open for 1% -> 3% of each run, Pallas kernels for 0% -> 0%
where the time goes in v1:
time: 143 us; the launch traced here: 142 us
  waiting for transfers between devices  48.1 us (34%)
  blocking collectives  44.5 us (31%)
  starting transfers between devices  32.2 us (23%)
  matrix products  7.19 us (5%)
  local copies, waits for them, and re-layouts  6.01 us (4%)
  other arithmetic  4.26 us (3%)
    all_to_all x3, waiting for transfers between devices, exchange(): return lax.all_to_all(x, axis, split_axis=0, concat_axis=0, tiled=True)  48.1 us
    all_to_all x1, blocking collectives, exchange(): return lax.all_to_all(x, axis, split_axis=0, concat_axis=0, tiled=True)  44.5 us
    all_to_all x3, starting transfers between devices, exchange(): return lax.all_to_all(x, axis, split_axis=0, concat_axis=0, tiled=True)  32.2 us
    dot_general x1, matrix products, shards(): jnp.dot(incoming, w_up[0], preferred_element_type=jnp.float32) * norm  4.96 us
  transfers between devices with their start and end apart: 3, of which 3 were waited for; matrix products, arithmetic and copies ran while one was open for 3% of the time, Pallas kernels for 0%

profile of v1, /device:TPU:112, one launch (start us, length us, event | category | flops | bytes accessed | tf_op | source)
XLA Modules:
  0.0 142.4 jit_solution(10767713735285079116)
XLA Ops:
  0.0 0.8 copy.33
  0.9 0.6 broadcast_in_dim.20
  1.5 16.7 %all-to-all-start = ((s32[8,1,16]{2,1,0:T(1,128)}), s32[8,1,16]{2,1,0:T(1,128)S(1)}, u32[]{:S(2)}, u32[]{:S(2)}) async-start(s32[8,1,16]{2,1,0:T(1,128)} %broadcast_in_dim.20), calls=%async_computation | async-start | bytes 8192 | tf_op jit(solution)/shard_map/all_to_all | solution.py:10
  18.2 0.8 reduce-window.9
  19.0 0.7 bitcast_subtract_fusion
  19.6 0.9 pad_maximum_fusion
  20.5 5.2 %all-to-all-done = s32[8,1,16]{2,1,0:T(1,128)S(1)} async-done(((s32[8,1,16]{2,1,0:T(1,128)}), s32[8,1,16]{2,1,0:T(1,128)S(1)}, u32[]{:S(2)}, u32[]{:S(2)}) %all-to-all-start) | async-done | bytes 544 | tf_op jit(solution)/shard_map/all_to_all | solution.py:10
  25.8 1.1 broadcast_in_dim.22
  26.8 6.8 %all-to-all-start.1 = ((bf16[8,256,256]{2,1,0:T(8,128)(2,1)}), bf16[8,256,256]{2,1,0:T(8,128)(2,1)S(1)}, u32[]{:S(2)}, u32[]{:S(2)}) async-start(bf16[8,256,256]{2,1,0:T(8,128)(2,1)} %broadcast_in_dim.22), calls=%async_computation.1 | async-start | bytes 2097152 | tf_op jit(solution)/shard_map/all_to_all | solution.py:10
  33.7 0.1 convert_reduce_fusion
  33.8 0.1 convert_reduce_fusion.3
  33.9 0.2 fusion.18
  34.2 0.3 convert_reduce_fusion.1
  34.6 0.2 slice_reduce_fusion.1
  34.8 26.1 %all-to-all-done.1 = bf16[8,256,256]{2,1,0:T(8,128)(2,1)S(1)} async-done(((bf16[8,256,256]{2,1,0:T(8,128)(2,1)}), bf16[8,256,256]{2,1,0:T(8,128)(2,1)S(1)}, u32[]{:S(2)}, u32[]{:S(2)}) %all-to-all-start.1) | async-done | bytes 1048608 | tf_op jit(solution)/shard_map/all_to_all | solution.py:10
  60.9 0.6 select_reduce_fusion
  61.5 0.5 fusion.3
  62.0 0.6 fusion.10
  62.7 0.2 convolution_convert_fusion
  62.8 0.1 broadcast_in_dim.26
  63.0 44.5 %all_to_all.20 = bf16[64,24,512]{2,1,0:T(8,128)(2,1)S(1)} all-to-all(bf16[64,24,512]{2,1,0:T(8,128)(2,1)S(1)} %bitcast.63), channel_id=1, replica_groups=mesh['dp'=16,'seq'=8,'expert'=8] {'seq','expert'}, dimensions={0} | all-to-all | bytes 3145728 | tf_op jit(solution)/shard_map/all_to_all | solution.py:10
  107.5 0.4 multiply_reduce_fusion
  108.0 0.6 copy.38
  108.6 0.6 copy.42
  109.2 5.0 %multiply_convert_fusion = bf16[192,896]{1,0:T(8,128)(2,1)S(1)} fusion(bf16[192,4096]{1,0:T(8,128)(2,1)S(1)} %bitcast.65, bf16[1,4096,896]{2,1,0:T(8,128)(2,1)} %param.13, f32[192]{0:T(256)S(1)} %rsqrt.11), kind=kOutput, calls=%fused_computation.20 | convolution fusion | flops 1410318336 | bytes 9257728 | tf_op jit(solution)/shard_map/dot_general | solution.py:100
  114.2 0.9 reshape.254
  115.1 8.8 %all-to-all-start.3 = ((bf16[64,3,896]{2,1,0:T(4,128)(2,1)}), bf16[64,3,896]{2,1,0:T(4,128)(2,1)S(1)}, u32[]{:S(2)}, u32[]{:S(2)}) async-start(bf16[64,3,896]{2,1,0:T(4,128)(2,1)} %reshape.254), calls=%async_computation.3 | async-start | bytes 917504 | tf_op jit(solution)/shard_map/all_to_all | solution.py:10
  123.9 0.2 convert_reduce_fusion.2
  124.3 16.7 %all-to-all-done.3 = bf16[64,3,896]{2,1,0:T(4,128)(2,1)S(1)} async-done(((bf16[64,3,896]{2,1,0:T(4,128)(2,1)}), bf16[64,3,896]{2,1,0:T(4,128)(2,1)S(1)}, u32[]{:S(2)}, u32[]{:S(2)}) %all-to-all-start.3) | async-done | bytes 344096 | tf_op jit(solution)/shard_map/all_to_all | solution.py:10
  141.0 0.3 reshape.255
  141.3 0.2 reshape.259
  141.5 0.9 fusion.8
  (23 shorter events, 0.8 us)
Async XLA Ops:
  0.0 60.9 %copy-start = (bf16[64,512]{1,0:T(8,128)(2,1)S(1)}, bf16[64,512]{1,0:T(8,128)(2,1)}, u32[]{:S(2)}) copy-start(bf16[64,512]{1,0:T(8,128)(2,1)} %param.7) | copy-start | bytes 196612
  1.5 24.3 %all-to-all-start = ((s32[8,1,16]{2,1,0:T(1,128)}), s32[8,1,16]{2,1,0:T(1,128)S(1)}, u32[]{:S(2)}, u32[]{:S(2)}) async-start(s32[8,1,16]{2,1,0:T(1,128)} %broadcast_in_dim.20), calls=%async_computation | async-start | bytes 8192 | tf_op jit(solution)/shard_map/all_to_all | solution.py:10
  26.8 34.1 %all-to-all-start.1 = ((bf16[8,256,256]{2,1,0:T(8,128)(2,1)}), bf16[8,256,256]{2,1,0:T(8,128)(2,1)S(1)}, u32[]{:S(2)}, u32[]{:S(2)}) async-start(bf16[8,256,256]{2,1,0:T(8,128)(2,1)} %broadcast_in_dim.22), calls=%async_computation.1 | async-start | bytes 2097152 | tf_op jit(solution)/shard_map/all_to_all | solution.py:10
  114.2 27.3 %copy-start.1 = (f32[8,2]{0,1:T(2,128)S(1)}, f32[8,2]{0,1:T(2,128)}, u32[]{:S(2)}) copy-start(f32[8,2]{0,1:T(2,128)} %param.12) | copy-start | bytes 196
  115.1 25.9 %all-to-all-start.3 = ((bf16[64,3,896]{2,1,0:T(4,128)(2,1)}), bf16[64,3,896]{2,1,0:T(4,128)(2,1)S(1)}, u32[]{:S(2)}, u32[]{:S(2)}) async-start(bf16[64,3,896]{2,1,0:T(4,128)(2,1)} %reshape.254), calls=%async_computation.3 | async-start | bytes 917504 | tf_op jit(solution)/shard_map/all_to_all | solution.py:10

commit v2 on v1

--- a/solution.py
+++ b/solution.py
@@ -12,10 +12,6 @@
 
 def to_everyone(x, axis):
     return exchange(jnp.broadcast_to(x, (lax.axis_size(axis), *x.shape)), axis)
-
-
-def doc_index(positions, starts):
-    return jnp.sum((positions[:, None] >= starts[None, :]).astype(jnp.int32), axis=1) - 1
 
 
 def slots(routes, experts_all):
@@ -43,16 +39,23 @@
     qpos = (
         lax.axis_index("seq") * shard_len + shard_len - q_rows + jnp.arange(q_rows, dtype=jnp.int32)
     )
-    qdoc = doc_index(qpos, starts)
-    kv = to_everyone(jnp.concatenate([keys, values], axis=1), "seq")
-    count = seq_count * shard_len
-    kv = kv.reshape(count, 2 * kv_local * HD)
-    k_all, v_all = kv[:, : kv_local * HD], kv[:, kv_local * HD :]
+    reach = -(-(1024 - 1) // shard_len)
     row_routes = to_everyone(routes.reshape(1, -1), "expert").reshape(expert_count, tok_count, 2)
+    kv_own = jnp.concatenate([keys, values], axis=0).reshape(2, shard_len, kv_local * HD)
+    ring = [[(i, (i + d) % seq_count) for i in range(seq_count)] for d in range(reach + 1)]
+    parts = [kv_own]
+    for d in range(1, reach):
+        parts.append(lax.ppermute(kv_own, "seq", ring[d]))
+    parts.append(lax.ppermute(kv_own[:, shard_len - q_rows :], "seq", ring[reach]))
+    kv = jnp.concatenate(parts[::-1], axis=1)
+    k_all, v_all = kv[0], kv[1]
+    count = k_all.shape[0]
 
     q_split = queries.reshape(q_rows, kv_local, group, HD)
-    kpos = jnp.arange(count, dtype=jnp.int32)
-    allowed = (kpos[None, :] <= qpos[:, None]) & (doc_index(kpos, starts)[None, :] == qdoc[:, None])
+    first = (lax.axis_index("seq") + 1) * shard_len - count
+    kpos = first + jnp.arange(count, dtype=jnp.int32)
+    begin = jnp.max(jnp.where(starts[None, :] <= qpos[:, None], starts[None, :], 0), axis=1)
+    allowed = (kpos[None, :] <= qpos[:, None]) & (kpos[None, :] >= begin[:, None])
     score = (
         jnp.einsum(
             "qkgd,pkd->kgqp",
@@ -103,6 +106,7 @@
     back = exchange(act.reshape(seq_count * expert_count, capacity, ff_local), ("seq", "expert"))
     back = back.reshape(seq_count, experts_all * capacity, ff_local)
     returned = back.transpose(1, 0, 2).reshape(experts_all * capacity, seq_count * ff_local)
+    back, routes = lax.optimization_barrier((back, routes))
     own = slots(routes[None], experts_all)[0]
     own_target = (routes * capacity + own).reshape(-1)
     own_selector = (

time: 143 us -> 126 us (0.88)
  waiting for transfers between devices: 48.1 us -> 2.75 us
  blocking collectives: 44.5 us -> 73.3 us
  local copies, waits for them, and re-layouts: 6.01 us -> 4.42 us
    all_to_all x3 -> x1, waiting for transfers between devices: 48.1 us -> 1.38 us  [exchange(): return lax.all_to_all(x, axis, split_axis=0, concat_axis=0, tiled=True)]
    all_to_all x1 -> x2, blocking collectives: 44.5 us -> 73.3 us  [exchange(): return lax.all_to_all(x, axis, split_axis=0, concat_axis=0, tiled=True)]
    ppermute x0 -> x4, starting transfers between devices: none -> 16.8 us  [the longest x3 12.4 us: shards(): parts.append(lax.ppermute(kv_own, 'seq', ring[d]))]
    all_to_all x3 -> x1, starting transfers between devices: 32.2 us -> 16.7 us  [exchange(): return lax.all_to_all(x, axis, split_axis=0, concat_axis=0, tiled=True)]
  transfers between devices with their start and end apart: 3 -> 5, of which waited for: 3 -> 2; matrix products, arithmetic and copies ran while one was open for 3% -> 3% of each run, Pallas kernels for 0% -> 0%
where the time goes in v2:
time: 126 us; the launch traced here: 125 us
  blocking collectives  73.3 us (58%)
  starting transfers between devices  33.5 us (27%)
  matrix products  6.93 us (6%)
  local copies, waits for them, and re-layouts  4.42 us (4%)
  other arithmetic  3.98 us (3%)
  waiting for transfers between devices  2.75 us (2%)
    all_to_all x2, blocking collectives, exchange(): return lax.all_to_all(x, axis, split_axis=0, concat_axis=0, tiled=True)  73.3 us
    all_to_all x1, starting transfers between devices, exchange(): return lax.all_to_all(x, axis, split_axis=0, concat_axis=0, tiled=True)  16.7 us
    ppermute x3, starting transfers between devices, shards(): parts.append(lax.ppermute(kv_own, 'seq', ring[d]))  12.4 us
    dot_general x1, matrix products, shards(): jnp.dot(incoming, w_up[0], preferred_element_type=jnp.float32) * norm  4.98 us
    ppermute x1, starting transfers between devices, shards(): lax.ppermute(kv_own[:, shard_len - q_rows:], 'seq', ring[reach])  4.4 us
  transfers between devices with their start and end apart: 5, of which 2 were waited for; matrix products, arithmetic and copies ran while one was open for 3% of the time, Pallas kernels for 0%

profile of v2, /device:TPU:112, one launch (start us, length us, event | category | flops | bytes accessed | tf_op | source)
XLA Modules:
  0.0 125.1 jit_solution(822979755922177615)
XLA Ops:
  0.0 0.9 pad_maximum_fusion
  0.9 3.4 %collective-permute-start.3 = (bf16[2,256,128]{2,1,0:T(8,128)(2,1)S(1)}, bf16[2,256,128]{2,1,0:T(8,128)(2,1)S(1)}, u32[]{:S(2)}, u32[]{:S(2)}) collective-permute-start(bf16[2,256,128]{2,1,0:T(8,128)(2,1)S(1)} %bitcast.70), channel_id=1, source_target_pairs={{0,8},{8,16},{16,24},{24,32},{32,40},{40,48},{48,56},{56,0},{1,9},... | collective-permute-start | bytes 393224 | tf_op jit(solution)/shard_map/ppermute | solution.py:48
  4.3 4.3 %collective-permute-start.2 = (bf16[2,256,128]{2,1,0:T(8,128)(2,1)S(1)}, bf16[2,256,128]{2,1,0:T(8,128)(2,1)S(1)}, u32[]{:S(2)}, u32[]{:S(2)}) collective-permute-start(bf16[2,256,128]{2,1,0:T(8,128)(2,1)S(1)} %bitcast.71), channel_id=1, source_target_pairs={{0,16},{8,24},{16,32},{24,40},{32,48},{40,56},{48,0},{56,8},{1,17}... | collective-permute-start | bytes 393224 | tf_op jit(solution)/shard_map/ppermute | solution.py:48
  8.7 4.7 %collective-permute-start.1 = (bf16[2,256,128]{2,1,0:T(8,128)(2,1)S(1)}, bf16[2,256,128]{2,1,0:T(8,128)(2,1)S(1)}, u32[]{:S(2)}, u32[]{:S(2)}) collective-permute-start(bf16[2,256,128]{2,1,0:T(8,128)(2,1)S(1)} %bitcast.72), channel_id=1, source_target_pairs={{0,24},{8,32},{16,40},{24,48},{32,56},{40,0},{48,8},{56,16},{1,25}... | collective-permute-start | bytes 393224 | tf_op jit(solution)/shard_map/ppermute | solution.py:48
  13.3 0.8 copy.37
  14.2 0.6 broadcast_in_dim.28
  14.8 16.7 %all-to-all-start = ((s32[8,1,16]{2,1,0:T(1,128)}), s32[8,1,16]{2,1,0:T(1,128)S(1)}, u32[]{:S(2)}, u32[]{:S(2)}) async-start(s32[8,1,16]{2,1,0:T(1,128)} %broadcast_in_dim.28), calls=%async_computation | async-start | bytes 8192 | tf_op jit(solution)/shard_map/all_to_all | solution.py:10
  31.5 4.4 %collective-permute-start = (bf16[2,64,128]{2,1,0:T(8,128)(2,1)S(1)}, bf16[2,64,128]{2,1,0:T(8,128)(2,1)S(1)}, u32[]{:S(2)}, u32[]{:S(2)}) collective-permute-start(bf16[2,64,128]{2,1,0:T(8,128)(2,1)S(1)} %slice.22), channel_id=1, source_target_pairs={{0,32},{8,40},{16,48},{24,56},{32,0},{40,8},{48,16},{56,24},{1,33}... | collective-permute-start | bytes 98312 | tf_op jit(solution)/shard_map/ppermute | solution.py:49
  35.9 0.8 reduce-window.9
  36.7 0.7 bitcast_subtract_fusion
  37.5 0.1 compare_and_fusion
  37.7 1.4 %all-to-all-done = s32[8,1,16]{2,1,0:T(1,128)S(1)} async-done(((s32[8,1,16]{2,1,0:T(1,128)}), s32[8,1,16]{2,1,0:T(1,128)S(1)}, u32[]{:S(2)}, u32[]{:S(2)}) %all-to-all-start) | async-done | bytes 544 | tf_op jit(solution)/shard_map/all_to_all | solution.py:10
  39.2 0.3 convert_reduce_fusion
  39.6 0.2 slice_reduce_fusion.1
  39.8 1.4 %collective-permute-done = bf16[2,64,128]{2,1,0:T(8,128)(2,1)S(1)} collective-permute-done((bf16[2,64,128]{2,1,0:T(8,128)(2,1)S(1)}, bf16[2,64,128]{2,1,0:T(8,128)(2,1)S(1)}, u32[]{:S(2)}, u32[]{:S(2)}) %collective-permute-start) | collective-permute-done | bytes 32800 | tf_op jit(solution)/shard_map/ppermute | solution.py:49
  41.3 0.5 select_reduce_fusion
  41.8 0.4 fusion.9
  42.2 0.4 fusion.8
  42.6 0.2 convolution_convert_fusion
  42.8 0.1 broadcast_in_dim.34
  43.0 48.7 %all_to_all.15 = bf16[64,24,512]{2,1,0:T(8,128)(2,1)S(1)} all-to-all(bf16[64,24,512]{2,1,0:T(8,128)(2,1)S(1)} %bitcast.65), channel_id=1, replica_groups=mesh['dp'=16,'seq'=8,'expert'=8] {'seq','expert'}, dimensions={0} | all-to-all | bytes 3145728 | tf_op jit(solution)/shard_map/all_to_all | solution.py:10
  91.7 0.4 multiply_reduce_fusion
  92.2 0.6 copy.40
  92.7 0.7 copy.47
  93.4 5.0 %multiply_convert_fusion = bf16[192,896]{1,0:T(8,128)(2,1)S(1)} fusion(bf16[192,4096]{1,0:T(8,128)(2,1)S(1)} %bitcast.67, bf16[1,4096,896]{2,1,0:T(8,128)(2,1)} %param.13, f32[192]{0:T(256)S(1)} %rsqrt.11), kind=kOutput, calls=%fused_computation.16 | convolution fusion | flops 1410318336 | bytes 9257728 | tf_op jit(solution)/shard_map/dot_general | solution.py:103
  98.4 0.2 reshape.260
  98.5 24.6 %all_to_all.16 = bf16[64,3,896]{2,1,0:T(4,128)(2,1)S(1)} all-to-all(bf16[64,3,896]{2,1,0:T(4,128)(2,1)S(1)} %reshape.260), channel_id=1, replica_groups=mesh['dp'=16,'seq'=8,'expert'=8] {'seq','expert'}, dimensions={0} | all-to-all | bytes 688128 | tf_op jit(solution)/shard_map/all_to_all | solution.py:10
  123.2 0.3 reshape.261
  123.6 0.2 convert_reduce_fusion.1
  123.9 0.1 copy.43
  124.1 0.2 reshape.265
  124.2 0.9 fusion.6
  (35 shorter events, 1.1 us)
Async XLA Ops:
  0.0 41.3 %copy-start = (bf16[64,512]{1,0:T(8,128)(2,1)S(1)}, bf16[64,512]{1,0:T(8,128)(2,1)}, u32[]{:S(2)}) copy-start(bf16[64,512]{1,0:T(8,128)(2,1)} %param.7) | copy-start | bytes 196612
  0.9 40.3 %collective-permute-start.3 = (bf16[2,256,128]{2,1,0:T(8,128)(2,1)S(1)}, bf16[2,256,128]{2,1,0:T(8,128)(2,1)S(1)}, u32[]{:S(2)}, u32[]{:S(2)}) collective-permute-start(bf16[2,256,128]{2,1,0:T(8,128)(2,1)S(1)} %bitcast.70), channel_id=1, source_target_pairs={{0,8},{8,16},{16,24},{24,32},{32,40},{40,48},{48,56},{56,0},{1,9},... | collective-permute-start | bytes 393224 | tf_op jit(solution)/shard_map/ppermute | solution.py:48
  4.3 36.9 %collective-permute-start.2 = (bf16[2,256,128]{2,1,0:T(8,128)(2,1)S(1)}, bf16[2,256,128]{2,1,0:T(8,128)(2,1)S(1)}, u32[]{:S(2)}, u32[]{:S(2)}) collective-permute-start(bf16[2,256,128]{2,1,0:T(8,128)(2,1)S(1)} %bitcast.71), channel_id=1, source_target_pairs={{0,16},{8,24},{16,32},{24,40},{32,48},{40,56},{48,0},{56,8},{1,17}... | collective-permute-start | bytes 393224 | tf_op jit(solution)/shard_map/ppermute | solution.py:48
  8.7 32.5 %collective-permute-start.1 = (bf16[2,256,128]{2,1,0:T(8,128)(2,1)S(1)}, bf16[2,256,128]{2,1,0:T(8,128)(2,1)S(1)}, u32[]{:S(2)}, u32[]{:S(2)}) collective-permute-start(bf16[2,256,128]{2,1,0:T(8,128)(2,1)S(1)} %bitcast.72), channel_id=1, source_target_pairs={{0,24},{8,32},{16,40},{24,48},{32,56},{40,0},{48,8},{56,16},{1,25}... | collective-permute-start | bytes 393224 | tf_op jit(solution)/shard_map/ppermute | solution.py:48
  14.8 24.3 %all-to-all-start = ((s32[8,1,16]{2,1,0:T(1,128)}), s32[8,1,16]{2,1,0:T(1,128)S(1)}, u32[]{:S(2)}, u32[]{:S(2)}) async-start(s32[8,1,16]{2,1,0:T(1,128)} %broadcast_in_dim.28), calls=%async_computation | async-start | bytes 8192 | tf_op jit(solution)/shard_map/all_to_all | solution.py:10
  31.5 9.7 %collective-permute-start = (bf16[2,64,128]{2,1,0:T(8,128)(2,1)S(1)}, bf16[2,64,128]{2,1,0:T(8,128)(2,1)S(1)}, u32[]{:S(2)}, u32[]{:S(2)}) collective-permute-start(bf16[2,64,128]{2,1,0:T(8,128)(2,1)S(1)} %slice.22), channel_id=1, source_target_pairs={{0,32},{8,40},{16,48},{24,56},{32,0},{40,8},{48,16},{56,24},{1,33}... | collective-permute-start | bytes 98312 | tf_op jit(solution)/shard_map/ppermute | solution.py:49
  98.4 25.1 %copy-start.1 = (s32[8,2]{0,1:T(2,128)S(1)}, s32[8,2]{0,1:T(2,128)}, u32[]{:S(2)}) copy-start(s32[8,2]{0,1:T(2,128)} %param.11) | copy-start | bytes 196
  123.2 1.1 copy-start.2

commit v3 on v1

v3 whole, which is shorter than its diff:
```python
import functools

import jax
import jax.numpy as jnp
from jax import lax
from jax.experimental import pallas as pl
from jax.experimental.pallas import tpu as pltpu
from jax.sharding import PartitionSpec as P

HD = 128
LONGEST = 1024
F32 = jnp.float32
BF16 = jnp.bfloat16
VMEM = pl.BlockSpec(memory_space=pltpu.VMEM)


def exchange(x, axis):
    return lax.all_to_all(x, axis, split_axis=0, concat_axis=0, tiled=True)


def attend(seq_count, begin_ref, routes_ref, q_ref, *refs):
    parts, out_ref = refs[:-1], refs[-1]
    heads, q_rows, _ = q_ref.shape
    shard_len = parts[0].shape[1]
    me = lax.axis_index("seq")
    rows = heads * q_rows
    queries = q_ref[...].reshape(rows, HD)
    begin = begin_ref[...]
    place = lax.broadcasted_iota(jnp.int32, (rows, 1), 0) % q_rows
    qpos = (me + 1) * shard_len - q_rows + place
    scores = []
    for d, part in enumerate(parts):
        count = part.shape[1]
        kpos = (me + 1 - d) * shard_len - count + lax.broadcasted_iota(jnp.int32, (1, count), 1)
        score = lax.dot_general(
            queries, part[0], (((1,), (1,)), ((), ())), preferred_element_type=F32
        )
        allowed = kpos >= begin
        if d == 0:
            allowed = allowed & (kpos <= qpos)
        scores.append(jnp.where(allowed, score, F32(-1e30)))
    peak = functools.reduce(jnp.maximum, [jnp.max(s, axis=1, keepdims=True) for s in scores])
    total = jnp.zeros((rows, 1), F32)
    acc = jnp.zeros((rows, HD), F32)
    for score, part in zip(scores, parts):
        weight = jnp.exp((score - peak) * F32(HD**-0.5))
        total = total + jnp.sum(weight, axis=1, keepdims=True)
        acc = acc + jnp.dot(weight.astype(BF16), part[1], preferred_element_type=F32)
    attended = (acc / total).astype(BF16)
    wide = jnp.concatenate([attended[h * q_rows : (h + 1) * q_rows] for h in range(heads)], axis=1)

    blocks, _, tokens = routes_ref.shape
    experts = out_ref.shape[0] // seq_count
    slots = out_ref.shape[1]
    capacity = slots // blocks
    spread = lax.broadcasted_iota(jnp.int32, (tokens, q_rows), 0) == (
        lax.broadcasted_iota(jnp.int32, (tokens, q_rows), 1) % tokens
    )
    block_of = lax.broadcasted_iota(jnp.int32, (blocks, q_rows), 1) // tokens
    in_block = lax.broadcasted_iota(jnp.int32, (blocks, q_rows), 0) == block_of
    expert_id = lax.broadcasted_iota(jnp.int32, (experts, q_rows), 0).astype(F32)
    named = jnp.zeros((experts, q_rows), jnp.bool_)
    for k in range(2):
        chosen = routes_ref[:, k, :].astype(F32).astype(BF16)
        by_block = jnp.dot(chosen, spread.astype(BF16), preferred_element_type=F32)
        flat = jnp.sum(jnp.where(in_block, by_block, 0.0), axis=0, keepdims=True)
        named = named | (flat == expert_id)
    r = lax.broadcasted_iota(jnp.int32, (q_rows, q_rows), 0)
    c = lax.broadcasted_iota(jnp.int32, (q_rows, q_rows), 1)
    earlier = (r // tokens == c // tokens) & (r < c)
    ahead = jnp.dot(named.astype(BF16), earlier.astype(BF16), preferred_element_type=F32)
    token_block = lax.broadcasted_iota(jnp.int32, (experts, q_rows), 1) // tokens
    slot = jnp.where(named, ahead + (token_block * capacity).astype(F32), F32(-1))
    slot_id = lax.broadcasted_iota(jnp.int32, (slots, q_rows), 0).astype(F32)
    selector = jnp.concatenate(
        [(slot_id == slot[e : e + 1, :]).astype(F32) for e in range(experts)], axis=0
    ).astype(BF16)
    picked = jnp.dot(selector, wide, preferred_element_type=F32)
    picked = picked.reshape(experts, slots, picked.shape[1]).astype(BF16)
    for s in range(seq_count):
        out_ref[s * experts : (s + 1) * experts] = picked


def project(experts, x_ref, w_ref, out_ref, w_vmem, sems):
    chunk = x_ref.shape[2]
    seq_count = x_ref.shape[0] // experts
    slots = x_ref.shape[1]
    rows = seq_count * slots

    def copy(e):
        at = pl.ds(e * chunk, chunk)
        return pltpu.make_async_copy(w_ref.at[0, at], w_vmem.at[at], sems.at[e])

    for e in range(experts):
        copy(e).start()
    acc = jnp.zeros((rows, w_ref.shape[2]), F32)
    square = jnp.zeros((rows, 1), F32)
    for e in range(experts):
        x = jnp.concatenate([x_ref[s * experts + e].astype(F32) for s in range(seq_count)], axis=0)
        square = square + jnp.sum(x * x, axis=1, keepdims=True)
        copy(e).wait()
        acc = acc + jnp.dot(
            x.astype(BF16), w_vmem[e * chunk : (e + 1) * chunk], preferred_element_type=F32
        )
    upper = acc * lax.rsqrt(square / F32(experts * chunk) + F32(1e-05))
    out_ref[...] = (upper / (1.0 + jnp.exp(-upper))).astype(BF16)


def mix(back_ref, selector_ref, gates_ref, out_ref):
    tokens = gates_ref.shape[0] // 2
    units = back_ref.shape[2]
    for s in range(back_ref.shape[0]):
        rows = jnp.dot(selector_ref[...], back_ref[s], preferred_element_type=F32)
        rows = rows * gates_ref[:, :1]
        out_ref[:, s * units : (s + 1) * units] = (rows[:tokens] + rows[tokens:]).astype(BF16)


def shards(queries, keys, values, lengths, routes, gates, w_up):
    q_rows, width = queries.shape
    shard_len = keys.shape[0]
    seq_count = lax.axis_size("seq")
    expert_count = lax.axis_size("expert")
    capacity = 3
    tok_count = routes.shape[0]
    per_expert = expert_count * capacity
    reach = -(-(LONGEST - 1) // shard_len)

    kv_own = jnp.concatenate([keys, values], axis=0).reshape(2, shard_len, HD)
    ring = [[(i, (i + d) % seq_count) for i in range(seq_count)] for d in range(reach + 1)]
    last = lax.ppermute(kv_own[:, shard_len - q_rows :], "seq", ring[reach])
    parts = [kv_own] + [lax.ppermute(kv_own, "seq", ring[d]) for d in range(1, reach)] + [last]
    row_routes = exchange(
        jnp.broadcast_to(routes.T[None], (expert_count, 2, tok_count)), "expert"
    )

    heads = width // HD
    q_heads = queries.reshape(q_rows, heads, HD).transpose(1, 0, 2)
    starts = jnp.cumsum(lengths) - lengths
    rows = jnp.arange(heads * q_rows, dtype=jnp.int32)[:, None]
    qpos = (lax.axis_index("seq") + 1) * shard_len - q_rows + rows % q_rows
    begin = jnp.max(jnp.where(starts[None, :] <= qpos, starts[None, :], 0), axis=1, keepdims=True)

    flat = routes.T.reshape(-1)
    token = jnp.arange(2 * tok_count, dtype=jnp.int32) % tok_count
    before = (flat[:, None] == flat[None, :]) & (token[:, None] > token[None, :])
    own_target = flat * capacity + jnp.sum(before.astype(jnp.int32), axis=1)
    own_selector = (
        own_target[:, None] == jnp.arange(per_expert, dtype=jnp.int32)[None, :]
    ).astype(BF16)

    outgoing = pl.pallas_call(
        functools.partial(attend, seq_count),
        out_shape=jax.ShapeDtypeStruct((seq_count * expert_count, per_expert, width), BF16),
        in_specs=[VMEM] * (3 + len(parts)),
        out_specs=VMEM,
        compiler_params=pltpu.CompilerParams(vmem_limit_bytes=24 << 20),
        name="attend",
    )(begin, row_routes, q_heads, *parts)
    gate_rows = jnp.broadcast_to(gates.T.reshape(-1, 1), (2 * tok_count, HD))
    outgoing, own_selector, gate_rows = lax.optimization_barrier(
        (outgoing, own_selector, gate_rows)
    )
    landed = exchange(outgoing, ("seq", "expert"))
    act = pl.pallas_call(
        functools.partial(project, expert_count),
        out_shape=jax.ShapeDtypeStruct((seq_count * per_expert, w_up.shape[2]), BF16),
        in_specs=[VMEM, pl.BlockSpec(memory_space=pltpu.HBM)],
        out_specs=VMEM,
        scratch_shapes=[
            pltpu.VMEM(w_up.shape[1:], BF16),
            pltpu.SemaphoreType.DMA((expert_count,)),
        ],
        compiler_params=pltpu.CompilerParams(vmem_limit_bytes=32 << 20),
        name="project",
    )(landed, pltpu.with_memory_space_constraint(w_up, pltpu.HBM))
    ff_local = act.shape[1]
    back = exchange(act.reshape(seq_count * expert_count, capacity, ff_local), ("seq", "expert"))
    back = back.reshape(seq_count, per_expert, ff_local)
    return pl.pallas_call(
        mix,
        out_shape=jax.ShapeDtypeStruct((tok_count, seq_count * ff_local), BF16),
        in_specs=[VMEM] * 3,
        out_specs=VMEM,
        compiler_params=pltpu.CompilerParams(vmem_limit_bytes=16 << 20),
        name="mix",
    )(back, own_selector, gate_rows)


def solution(mesh):
    placed = (
        P(("dp", "seq"), "expert"),
        P(("dp", "seq"), "expert"),
        P(("dp", "seq"), "expert"),
        P("dp"),
        P(("dp", "seq", "expert"), None),
        P(("dp", "seq", "expert"), None),
        P("expert", None, "seq"),
    )
    return jax.shard_map(
        shards,
        mesh=mesh,
        in_specs=placed,
        out_specs=P(("dp", "seq", "expert"), None),
        check_vma=False,
    )
```

time: 143 us -> 127 us (0.89)
  waiting for transfers between devices: 48.1 us -> 1.43 us
  blocking collectives: 44.5 us -> 73.7 us
  matrix products: 7.19 us -> 0 us
  Pallas kernels: 0 us -> 6.36 us
  starting transfers between devices: 32.2 us -> 37.9 us
  local copies, waits for them, and re-layouts: 6.01 us -> 3.48 us
  other arithmetic: 4.26 us -> 2.76 us
    all_to_all x3 -> x1, waiting for transfers between devices: 48.1 us -> 0.01 us  [exchange(): return lax.all_to_all(x, axis, split_axis=0, concat_axis=0, tiled=True)]
    all_to_all x1 -> x2, blocking collectives: 44.5 us -> 73.7 us  [exchange(): return lax.all_to_all(x, axis, split_axis=0, concat_axis=0, tiled=True)]
    ppermute x0 -> x4, starting transfers between devices: none -> 17.1 us  [the longest x3 12.4 us: shards(): lax.ppermute(kv_own, 'seq', ring[d])]
    all_to_all x3 -> x1, starting transfers between devices: 32.2 us -> 20.8 us  [exchange(): return lax.all_to_all(x, axis, split_axis=0, concat_axis=0, tiled=True)]
    dot_general x5 -> x0, matrix products: 7.19 us -> none  [the longest x1 4.96 us: shards(): jnp.dot(incoming, w_up[0], preferred_element_type=jnp.float32) * norm]
    pallas_call x0 -> x3, Pallas kernels: none -> 6.36 us  [the longest x1 4.33 us: shards(): pl.pallas_call(functools.partial(project, expert_count), out_shape=jax.Sh...]
    unnamed x6 -> x2, local copies, waits for them, and re-layouts: 1.44 us -> 0.01 us
  transfers between devices with their start and end apart: 3 -> 5, of which waited for: 3 -> 1; matrix products, arithmetic and copies ran while one was open for 3% -> 4% of each run, Pallas kernels for 0% -> 0%
where the time goes in v3:
time: 127 us; the launch traced here: 126 us
  blocking collectives  73.7 us (58%)
  starting transfers between devices  37.9 us (30%)
  Pallas kernels  6.36 us (5%)
  local copies, waits for them, and re-layouts  3.48 us (3%)
  other arithmetic  2.76 us (2%)
  waiting for transfers between devices  1.43 us (1%)
    all_to_all x2, blocking collectives, exchange(): return lax.all_to_all(x, axis, split_axis=0, concat_axis=0, tiled=True)  73.7 us
    all_to_all x1, starting transfers between devices, exchange(): return lax.all_to_all(x, axis, split_axis=0, concat_axis=0, tiled=True)  20.8 us
    ppermute x3, starting transfers between devices, shards(): lax.ppermute(kv_own, 'seq', ring[d])  12.4 us
    ppermute x1, starting transfers between devices, shards(): last = lax.ppermute(kv_own[:, shard_len - q_rows:], 'seq', ring[reach])  4.73 us
    pallas_call x1, Pallas kernels, shards(): pl.pallas_call(functools.partial(project, expert_count), out_shape=jax.Sh...  4.33 us
  transfers between devices with their start and end apart: 5, of which 1 were waited for; matrix products, arithmetic and copies ran while one was open for 4% of the time, Pallas kernels for 0%

profile of v3, /device:TPU:112, one launch (start us, length us, event | category | flops | bytes accessed | tf_op | source)
XLA Modules:
  0.0 125.8 jit_solution(3360922300762628489)
XLA Ops:
  0.0 0.0 copy-start
  0.0 0.9 pad_maximum_fusion
  0.9 5.3 %collective-permute-start.2 = (bf16[2,256,128]{2,1,0:T(8,128)(2,1)S(1)}, bf16[2,256,128]{2,1,0:T(8,128)(2,1)S(1)}, u32[]{:S(2)}, u32[]{:S(2)}) collective-permute-start(bf16[2,256,128]{2,1,0:T(8,128)(2,1)S(1)} %bitcast.14), channel_id=1, source_target_pairs={{0,24},{8,32},{16,40},{24,48},{32,56},{40,0},{48,8},{56,16},{1,25}... | collective-permute-start | bytes 393224 | tf_op jit(solution)/shard_map/ppermute | solution.py:131
  6.2 4.6 %collective-permute-start.1 = (bf16[2,256,128]{2,1,0:T(8,128)(2,1)S(1)}, bf16[2,256,128]{2,1,0:T(8,128)(2,1)S(1)}, u32[]{:S(2)}, u32[]{:S(2)}) collective-permute-start(bf16[2,256,128]{2,1,0:T(8,128)(2,1)S(1)} %bitcast.15), channel_id=1, source_target_pairs={{0,16},{8,24},{16,32},{24,40},{32,48},{40,56},{48,0},{56,8},{1,17}... | collective-permute-start | bytes 393224 | tf_op jit(solution)/shard_map/ppermute | solution.py:131
  10.8 2.5 %collective-permute-start = (bf16[2,256,128]{2,1,0:T(8,128)(2,1)S(1)}, bf16[2,256,128]{2,1,0:T(8,128)(2,1)S(1)}, u32[]{:S(2)}, u32[]{:S(2)}) collective-permute-start(bf16[2,256,128]{2,1,0:T(8,128)(2,1)S(1)} %bitcast.16), channel_id=1, source_target_pairs={{0,8},{8,16},{16,24},{24,32},{32,40},{40,48},{48,56},{56,0},{1,9},... | collective-permute-start | bytes 393224 | tf_op jit(solution)/shard_map/ppermute | solution.py:131
  13.3 1.3 %broadcast_in_dim.20 = s32[8,2,8]{2,1,0:T(2,128)} broadcast(s32[2,8]{1,0:T(2,128)} %bitcast.20), dimensions={1,2} | broadcast | bytes 576 | tf_op jit(solution)/shard_map/broadcast_in_dim | solution.py:133
  14.6 20.8 %all-to-all-start = ((s32[8,2,8]{2,1,0:T(2,128)}), s32[8,2,8]{2,1,0:T(2,128)S(1)}, u32[]{:S(2)}, u32[]{:S(2)}) async-start(s32[8,2,8]{2,1,0:T(2,128)} %broadcast_in_dim.20), calls=%async_computation | async-start | bytes 16384 | tf_op jit(solution)/shard_map/all_to_all | solution.py:18
  35.4 4.7 %collective-permute-start.3 = (bf16[2,64,128]{2,1,0:T(8,128)(2,1)S(1)}, bf16[2,64,128]{2,1,0:T(8,128)(2,1)S(1)}, u32[]{:S(2)}, u32[]{:S(2)}) collective-permute-start(bf16[2,64,128]{2,1,0:T(8,128)(2,1)S(1)} %slice.4), channel_id=1, source_target_pairs={{0,32},{8,40},{16,48},{24,56},{32,0},{40,8},{48,16},{56,24},{1,33}... | collective-permute-start | bytes 98312 | tf_op jit(solution)/shard_map/ppermute | solution.py:130
  40.2 0.8 reshape.94
  40.9 0.8 reduce-window.9
  41.8 0.7 bitcast_subtract_fusion
  42.4 0.2 convert_reduce_fusion
  42.6 0.1 fusion.selector_ref
  42.7 0.0 copy-done
  42.7 0.1 select_reduce_fusion
  42.8 0.8 broadcast_in_dim.21
  43.6 0.1 copy.11.begin_ref
  43.7 0.0 all-to-all-done.routes_ref
  43.7 1.4 %collective-permute-done.3.refs_4_ = bf16[2,64,128]{2,1,0:T(8,128)(2,1)S(1)} collective-permute-done((bf16[2,64,128]{2,1,0:T(8,128)(2,1)S(1)}, bf16[2,64,128]{2,1,0:T(8,128)(2,1)S(1)}, u32[]{:S(2)}, u32[]{:S(2)}) %collective-permute-start.3) | collective-permute-done | bytes 32800 | tf_op jit(solution)/shard_map/ppermute | solution.py:130
  45.1 0.0 collective-permute-done.2.refs_3_
  45.2 0.0 collective-permute-done.1.refs_2_
  45.2 0.0 collective-permute-done.refs_1_
  45.2 1.2 attend.1
  46.3 0.1 broadcast_in_dim.22.gates_ref
  46.4 49.1 %all_to_all.15.x_ref = bf16[64,24,512]{2,1,0:T(8,128)(2,1)S(1)} all-to-all(bf16[64,24,512]{2,1,0:T(8,128)(2,1)S(1)} %attend.1), channel_id=1, replica_groups=mesh['dp'=16,'seq'=8,'expert'=8] {'seq','expert'}, dimensions={0} | all-to-all | bytes 3145728 | tf_op jit(solution)/shard_map/all_to_all | solution.py:18
  95.5 4.3 %project.1 = bf16[192,896]{1,0:T(8,128)(2,1)S(1)} custom-call(bf16[64,24,512]{2,1,0:T(8,128)(2,1)S(1)} %all_to_all.15.x_ref, bf16[1,4096,896]{2,1,0:T(8,128)(2,1)} %w_ref.1), custom_call_target="tpu_custom_call" | custom-call | tf_op jit(solution)/shard_map/project/pallas_call | solution.py:164
  99.8 0.2 reshape.95
  100.0 24.6 %all_to_all.16 = bf16[64,3,896]{2,1,0:T(4,128)(2,1)S(1)} all-to-all(bf16[64,3,896]{2,1,0:T(4,128)(2,1)S(1)} %reshape.95), channel_id=1, replica_groups=mesh['dp'=16,'seq'=8,'expert'=8] {'seq','expert'}, dimensions={0} | all-to-all | bytes 688128 | tf_op jit(solution)/shard_map/all_to_all | solution.py:18
  124.6 0.3 reshape.96.back_ref
  124.9 0.9 mix.1
  (5 shorter events, 0.0 us)
Async XLA Ops:
  0.0 42.7 %copy-start = (bf16[64,512]{1,0:T(8,128)(2,1)S(1)}, bf16[64,512]{1,0:T(8,128)(2,1)}, u32[]{:S(2)}) copy-start(bf16[64,512]{1,0:T(8,128)(2,1)} %param.7) | copy-start | bytes 196612
  0.9 44.2 %collective-permute-start.2 = (bf16[2,256,128]{2,1,0:T(8,128)(2,1)S(1)}, bf16[2,256,128]{2,1,0:T(8,128)(2,1)S(1)}, u32[]{:S(2)}, u32[]{:S(2)}) collective-permute-start(bf16[2,256,128]{2,1,0:T(8,128)(2,1)S(1)} %bitcast.14), channel_id=1, source_target_pairs={{0,24},{8,32},{16,40},{24,48},{32,56},{40,0},{48,8},{56,16},{1,25}... | collective-permute-start | bytes 393224 | tf_op jit(solution)/shard_map/ppermute | solution.py:131
  6.2 39.0 %collective-permute-start.1 = (bf16[2,256,128]{2,1,0:T(8,128)(2,1)S(1)}, bf16[2,256,128]{2,1,0:T(8,128)(2,1)S(1)}, u32[]{:S(2)}, u32[]{:S(2)}) collective-permute-start(bf16[2,256,128]{2,1,0:T(8,128)(2,1)S(1)} %bitcast.15), channel_id=1, source_target_pairs={{0,16},{8,24},{16,32},{24,40},{32,48},{40,56},{48,0},{56,8},{1,17}... | collective-permute-start | bytes 393224 | tf_op jit(solution)/shard_map/ppermute | solution.py:131
  10.8 34.3 %collective-permute-start = (bf16[2,256,128]{2,1,0:T(8,128)(2,1)S(1)}, bf16[2,256,128]{2,1,0:T(8,128)(2,1)S(1)}, u32[]{:S(2)}, u32[]{:S(2)}) collective-permute-start(bf16[2,256,128]{2,1,0:T(8,128)(2,1)S(1)} %bitcast.16), channel_id=1, source_target_pairs={{0,8},{8,16},{16,24},{24,32},{32,40},{40,48},{48,56},{56,0},{1,9},... | collective-permute-start | bytes 393224 | tf_op jit(solution)/shard_map/ppermute | solution.py:131
  14.6 29.1 %all-to-all-start = ((s32[8,2,8]{2,1,0:T(2,128)}), s32[8,2,8]{2,1,0:T(2,128)S(1)}, u32[]{:S(2)}, u32[]{:S(2)}) async-start(s32[8,2,8]{2,1,0:T(2,128)} %broadcast_in_dim.20), calls=%async_computation | async-start | bytes 16384 | tf_op jit(solution)/shard_map/all_to_all | solution.py:18
  35.4 9.7 %collective-permute-start.3 = (bf16[2,64,128]{2,1,0:T(8,128)(2,1)S(1)}, bf16[2,64,128]{2,1,0:T(8,128)(2,1)S(1)}, u32[]{:S(2)}, u32[]{:S(2)}) collective-permute-start(bf16[2,64,128]{2,1,0:T(8,128)(2,1)S(1)} %slice.4), channel_id=1, source_target_pairs={{0,32},{8,40},{16,48},{24,56},{32,0},{40,8},{48,16},{56,24},{1,33}... | collective-permute-start | bytes 98312 | tf_op jit(solution)/shard_map/ppermute | solution.py:130

commit v4 on v3

--- a/solution.py
+++ b/solution.py
@@ -9,6 +9,8 @@
 
 HD = 128
 LONGEST = 1024
+FIXED = 32767
+DIGITS = 8192
 F32 = jnp.float32
 BF16 = jnp.bfloat16
 VMEM = pl.BlockSpec(memory_space=pltpu.VMEM)
@@ -18,7 +20,7 @@
     return lax.all_to_all(x, axis, split_axis=0, concat_axis=0, tiled=True)
 
 
-def attend(seq_count, begin_ref, routes_ref, q_ref, *refs):
+def attend(begin_ref, routes_ref, q_ref, *refs):
     parts, out_ref = refs[:-1], refs[-1]
     heads, q_rows, _ = q_ref.shape
     shard_len = parts[0].shape[1]
@@ -50,7 +52,7 @@
     wide = jnp.concatenate([attended[h * q_rows : (h + 1) * q_rows] for h in range(heads)], axis=1)
 
     blocks, _, tokens = routes_ref.shape
-    experts = out_ref.shape[0] // seq_count
+    experts = out_ref.shape[0]
     slots = out_ref.shape[1]
     capacity = slots // blocks
     spread = lax.broadcasted_iota(jnp.int32, (tokens, q_rows), 0) == (
@@ -76,33 +78,55 @@
         [(slot_id == slot[e : e + 1, :]).astype(F32) for e in range(experts)], axis=0
     ).astype(BF16)
     picked = jnp.dot(selector, wide, preferred_element_type=F32)
-    picked = picked.reshape(experts, slots, picked.shape[1]).astype(BF16)
-    for s in range(seq_count):
-        out_ref[s * experts : (s + 1) * experts] = picked
-
-
-def project(experts, x_ref, w_ref, out_ref, w_vmem, sems):
-    chunk = x_ref.shape[2]
-    seq_count = x_ref.shape[0] // experts
-    slots = x_ref.shape[1]
-    rows = seq_count * slots
+    out_ref[...] = picked.reshape(out_ref.shape).astype(BF16)
+
+
+def pack(x_ref, out_ref):
+    experts, _, chunk = x_ref.shape
+    parts = [x_ref[e].astype(F32) for e in range(experts)]
+    square = sum(jnp.sum(x * x, axis=1, keepdims=True) for x in parts)
+    largest = functools.reduce(
+        jnp.maximum, [jnp.max(jnp.abs(x), axis=1, keepdims=True) for x in parts]
+    )
+    largest = jnp.maximum(largest, F32(1e-30))
+    up = F32(FIXED) / largest
+    for e, x in enumerate(parts):
+        fixed = jnp.round(x * up).astype(jnp.int32)
+        out_ref[:, e * chunk : (e + 1) * chunk] = fixed.astype(jnp.int16)
+    down = largest * F32(1 / FIXED) * lax.rsqrt(square / F32(experts * chunk) + F32(1e-05))
+    power = jnp.floor(jnp.log2(down))
+    digits = jnp.round(down * jnp.exp2(-power) * F32(DIGITS))
+    tail = (x_ref.shape[1], out_ref.shape[1] - experts * chunk)
+    lane = lax.broadcasted_iota(jnp.int32, tail, 1)
+    factor = jnp.where(lane == 0, digits, jnp.where(lane == 1, power, F32(0)))
+    out_ref[:, experts * chunk :] = factor.astype(jnp.int32).astype(jnp.int16)
+
+
+def project(chunks, x_ref, w_ref, out_ref, w_vmem, sems):
+    seq_count = x_ref.shape[0]
+    depth = w_vmem.shape[0]
+    chunk = depth // chunks
 
     def copy(e):
         at = pl.ds(e * chunk, chunk)
         return pltpu.make_async_copy(w_ref.at[0, at], w_vmem.at[at], sems.at[e])
 
-    for e in range(experts):
+    def rows(lo, size):
+        part = [x_ref[s, :, lo : lo + size].astype(jnp.int32) for s in range(seq_count)]
+        return jnp.concatenate(part, axis=0).astype(F32)
+
+    for e in range(chunks):
         copy(e).start()
-    acc = jnp.zeros((rows, w_ref.shape[2]), F32)
-    square = jnp.zeros((rows, 1), F32)
-    for e in range(experts):
-        x = jnp.concatenate([x_ref[s * experts + e].astype(F32) for s in range(seq_count)], axis=0)
-        square = square + jnp.sum(x * x, axis=1, keepdims=True)
+    factor = rows(depth, HD)
+    factor = factor[:, 0:1] * F32(1 / DIGITS) * jnp.exp2(factor[:, 1:2])
+    acc = jnp.zeros(out_ref.shape, F32)
+    for e in range(chunks):
+        x = rows(e * chunk, chunk).astype(BF16)
         copy(e).wait()
         acc = acc + jnp.dot(
-            x.astype(BF16), w_vmem[e * chunk : (e + 1) * chunk], preferred_element_type=F32
+            x, w_vmem[e * chunk : (e + 1) * chunk], preferred_element_type=F32
         )
-    upper = acc * lax.rsqrt(square / F32(experts * chunk) + F32(1e-05))
+    upper = acc * factor
     out_ref[...] = (upper / (1.0 + jnp.exp(-upper))).astype(BF16)
 
 
@@ -149,8 +173,8 @@
     ).astype(BF16)
 
     outgoing = pl.pallas_call(
-        functools.partial(attend, seq_count),
-        out_shape=jax.ShapeDtypeStruct((seq_count * expert_count, per_expert, width), BF16),
+        attend,
+        out_shape=jax.ShapeDtypeStruct((expert_count, per_expert, width), BF16),
         in_specs=[VMEM] * (3 + len(parts)),
         out_specs=VMEM,
         compiler_params=pltpu.CompilerParams(vmem_limit_bytes=24 << 20),
@@ -160,7 +184,16 @@
     outgoing, own_selector, gate_rows = lax.optimization_barrier(
         (outgoing, own_selector, gate_rows)
     )
-    landed = exchange(outgoing, ("seq", "expert"))
+    landed = exchange(outgoing, "expert")
+    packed = pl.pallas_call(
+        pack,
+        out_shape=jax.ShapeDtypeStruct((per_expert, expert_count * width + HD), jnp.int16),
+        in_specs=[VMEM],
+        out_specs=VMEM,
+        compiler_params=pltpu.CompilerParams(vmem_limit_bytes=16 << 20),
+        name="pack",
+    )(landed)
+    incoming = lax.all_gather(packed, "seq")
     act = pl.pallas_call(
         functools.partial(project, expert_count),
         out_shape=jax.ShapeDtypeStruct((seq_count * per_expert, w_up.shape[2]), BF16),
@@ -172,7 +205,7 @@
         ],
         compiler_params=pltpu.CompilerParams(vmem_limit_bytes=32 << 20),
         name="project",
-    )(landed, pltpu.with_memory_space_constraint(w_up, pltpu.HBM))
+    )(incoming, pltpu.with_memory_space_constraint(w_up, pltpu.HBM))
     ff_local = act.shape[1]
     back = exchange(act.reshape(seq_count * expert_count, capacity, ff_local), ("seq", "expert"))
     back = back.reshape(seq_count, per_expert, ff_local)

time: 127 us -> 119 us (0.937)
  blocking collectives: 73.7 us -> 65.7 us
    all_to_all x2, blocking collectives: 73.7 us -> 36.1 us  [exchange(): return lax.all_to_all(x, axis, split_axis=0, concat_axis=0, tiled=True)]
    all_gather x0 -> x1, blocking collectives: none -> 29.6 us  [shards(): incoming = lax.all_gather(packed, 'seq')]
where the time goes in v4:
time: 119 us; the launch traced here: 118 us
  blocking collectives  65.7 us (55%)
  starting transfers between devices  37.9 us (32%)
  Pallas kernels  6.63 us (6%)
  local copies, waits for them, and re-layouts  3.48 us (3%)
  other arithmetic  2.76 us (2%)
  waiting for transfers between devices  1.43 us (1%)
    all_to_all x2, blocking collectives, exchange(): return lax.all_to_all(x, axis, split_axis=0, concat_axis=0, tiled=True)  36.1 us
    all_gather x1, blocking collectives, shards(): incoming = lax.all_gather(packed, 'seq')  29.6 us
    all_to_all x1, starting transfers between devices, exchange(): return lax.all_to_all(x, axis, split_axis=0, concat_axis=0, tiled=True)  20.8 us
    ppermute x3, starting transfers between devices, shards(): lax.ppermute(kv_own, 'seq', ring[d])  12.4 us
    ppermute x1, starting transfers between devices, shards(): last = lax.ppermute(kv_own[:, shard_len - q_rows:], 'seq', ring[reach])  4.73 us
    pallas_call x1, Pallas kernels, shards(): pl.pallas_call(functools.partial(project, expert_count), out_shape=jax.Sh...  4.49 us
  transfers between devices with their start and end apart: 5, of which 1 were waited for; matrix products, arithmetic and copies ran while one was open for 4% of the time, Pallas kernels for 0%

profile of v4, /device:TPU:112, one launch (start us, length us, event | category | flops | bytes accessed | tf_op | source)
XLA Modules:
  0.0 118.0 jit_solution(13315053353179202735)
XLA Ops:
  0.0 0.0 copy-start
  0.0 0.9 pad_maximum_fusion
  0.9 5.3 %collective-permute-start.2 = (bf16[2,256,128]{2,1,0:T(8,128)(2,1)S(1)}, bf16[2,256,128]{2,1,0:T(8,128)(2,1)S(1)}, u32[]{:S(2)}, u32[]{:S(2)}) collective-permute-start(bf16[2,256,128]{2,1,0:T(8,128)(2,1)S(1)} %bitcast.16), channel_id=1, source_target_pairs={{0,24},{8,32},{16,40},{24,48},{32,56},{40,0},{48,8},{56,16},{1,25}... | collective-permute-start | bytes 393224 | tf_op jit(solution)/shard_map/ppermute | solution.py:155
  6.2 4.6 %collective-permute-start.1 = (bf16[2,256,128]{2,1,0:T(8,128)(2,1)S(1)}, bf16[2,256,128]{2,1,0:T(8,128)(2,1)S(1)}, u32[]{:S(2)}, u32[]{:S(2)}) collective-permute-start(bf16[2,256,128]{2,1,0:T(8,128)(2,1)S(1)} %bitcast.17), channel_id=1, source_target_pairs={{0,16},{8,24},{16,32},{24,40},{32,48},{40,56},{48,0},{56,8},{1,17}... | collective-permute-start | bytes 393224 | tf_op jit(solution)/shard_map/ppermute | solution.py:155
  10.8 2.5 %collective-permute-start = (bf16[2,256,128]{2,1,0:T(8,128)(2,1)S(1)}, bf16[2,256,128]{2,1,0:T(8,128)(2,1)S(1)}, u32[]{:S(2)}, u32[]{:S(2)}) collective-permute-start(bf16[2,256,128]{2,1,0:T(8,128)(2,1)S(1)} %bitcast.18), channel_id=1, source_target_pairs={{0,8},{8,16},{16,24},{24,32},{32,40},{40,48},{48,56},{56,0},{1,9},... | collective-permute-start | bytes 393224 | tf_op jit(solution)/shard_map/ppermute | solution.py:155
  13.3 1.3 %broadcast_in_dim.20 = s32[8,2,8]{2,1,0:T(2,128)} broadcast(s32[2,8]{1,0:T(2,128)} %bitcast.22), dimensions={1,2} | broadcast | bytes 576 | tf_op jit(solution)/shard_map/broadcast_in_dim | solution.py:157
  14.6 20.8 %all-to-all-start = ((s32[8,2,8]{2,1,0:T(2,128)}), s32[8,2,8]{2,1,0:T(2,128)S(1)}, u32[]{:S(2)}, u32[]{:S(2)}) async-start(s32[8,2,8]{2,1,0:T(2,128)} %broadcast_in_dim.20), calls=%async_computation | async-start | bytes 16384 | tf_op jit(solution)/shard_map/all_to_all | solution.py:20
  35.4 4.7 %collective-permute-start.3 = (bf16[2,64,128]{2,1,0:T(8,128)(2,1)S(1)}, bf16[2,64,128]{2,1,0:T(8,128)(2,1)S(1)}, u32[]{:S(2)}, u32[]{:S(2)}) collective-permute-start(bf16[2,64,128]{2,1,0:T(8,128)(2,1)S(1)} %slice.4), channel_id=1, source_target_pairs={{0,32},{8,40},{16,48},{24,56},{32,0},{40,8},{48,16},{56,24},{1,33}... | collective-permute-start | bytes 98312 | tf_op jit(solution)/shard_map/ppermute | solution.py:154
  40.2 0.8 reshape.94
  40.9 0.8 reduce-window.9
  41.8 0.7 bitcast_subtract_fusion
  42.4 0.2 convert_reduce_fusion
  42.6 0.1 fusion.selector_ref
  42.7 0.0 copy-done
  42.7 0.1 select_reduce_fusion
  42.8 0.8 broadcast_in_dim.21
  43.6 0.1 copy.11.begin_ref
  43.7 0.0 all-to-all-done.routes_ref
  43.7 1.4 %collective-permute-done.3.refs_4_ = bf16[2,64,128]{2,1,0:T(8,128)(2,1)S(1)} collective-permute-done((bf16[2,64,128]{2,1,0:T(8,128)(2,1)S(1)}, bf16[2,64,128]{2,1,0:T(8,128)(2,1)S(1)}, u32[]{:S(2)}, u32[]{:S(2)}) %collective-permute-start.3) | collective-permute-done | bytes 32800 | tf_op jit(solution)/shard_map/ppermute | solution.py:154
  45.1 0.0 collective-permute-done.2.refs_3_
  45.2 0.0 collective-permute-done.1.refs_2_
  45.2 0.0 collective-permute-done.refs_1_
  45.2 1.1 attend.1
  46.3 0.1 broadcast_in_dim.22.gates_ref
  46.3 16.8 %all_to_all.15.x_ref = bf16[8,24,512]{2,1,0:T(8,128)(2,1)S(1)} all-to-all(bf16[8,24,512]{2,1,0:T(8,128)(2,1)S(1)} %attend.1), channel_id=1, replica_groups=mesh['dp'=16,'seq'=8,'expert'=8] {'expert'}, dimensions={0} | all-to-all | bytes 393216 | tf_op jit(solution)/shard_map/all_to_all | solution.py:20
  63.1 0.2 pack.1
  63.3 29.6 %all-gather.2 = s16[192,4224]{1,0:T(8,128)(2,1)S(1)} all-gather(s16[24,4224]{1,0:T(8,128)(2,1)S(1)} %pack.1), channel_id=2, replica_groups=mesh['dp'=16,'seq'=8,'expert'=8] {'seq'}, dimensions={0}, use_global_device_ids=true | all-gather | bytes 1824768 | tf_op jit(solution)/shard_map/all_gather | solution.py:196
  92.9 4.5 %project.1 = bf16[192,896]{1,0:T(8,128)(2,1)S(1)} custom-call(s16[8,24,4224]{2,1,0:T(8,128)(2,1)S(1)} %bitcast.15, bf16[1,4096,896]{2,1,0:T(8,128)(2,1)} %w_ref.1), custom_call_target="tpu_custom_call" | custom-call | tf_op jit(solution)/shard_map/project/pallas_call | solution.py:197
  97.4 0.2 reshape.95
  97.5 19.3 %all_to_all.16 = bf16[64,3,896]{2,1,0:T(4,128)(2,1)S(1)} all-to-all(bf16[64,3,896]{2,1,0:T(4,128)(2,1)S(1)} %reshape.95), channel_id=1, replica_groups=mesh['dp'=16,'seq'=8,'expert'=8] {'seq','expert'}, dimensions={0} | all-to-all | bytes 688128 | tf_op jit(solution)/shard_map/all_to_all | solution.py:20
  116.8 0.3 reshape.96.back_ref
  117.1 0.9 mix.1
  (5 shorter events, 0.0 us)
Async XLA Ops:
  0.0 42.7 %copy-start = (bf16[64,512]{1,0:T(8,128)(2,1)S(1)}, bf16[64,512]{1,0:T(8,128)(2,1)}, u32[]{:S(2)}) copy-start(bf16[64,512]{1,0:T(8,128)(2,1)} %param.7) | copy-start | bytes 196612
  0.9 44.2 %collective-permute-start.2 = (bf16[2,256,128]{2,1,0:T(8,128)(2,1)S(1)}, bf16[2,256,128]{2,1,0:T(8,128)(2,1)S(1)}, u32[]{:S(2)}, u32[]{:S(2)}) collective-permute-start(bf16[2,256,128]{2,1,0:T(8,128)(2,1)S(1)} %bitcast.16), channel_id=1, source_target_pairs={{0,24},{8,32},{16,40},{24,48},{32,56},{40,0},{48,8},{56,16},{1,25}... | collective-permute-start | bytes 393224 | tf_op jit(solution)/shard_map/ppermute | solution.py:155
  6.2 39.0 %collective-permute-start.1 = (bf16[2,256,128]{2,1,0:T(8,128)(2,1)S(1)}, bf16[2,256,128]{2,1,0:T(8,128)(2,1)S(1)}, u32[]{:S(2)}, u32[]{:S(2)}) collective-permute-start(bf16[2,256,128]{2,1,0:T(8,128)(2,1)S(1)} %bitcast.17), channel_id=1, source_target_pairs={{0,16},{8,24},{16,32},{24,40},{32,48},{40,56},{48,0},{56,8},{1,17}... | collective-permute-start | bytes 393224 | tf_op jit(solution)/shard_map/ppermute | solution.py:155
  10.8 34.3 %collective-permute-start = (bf16[2,256,128]{2,1,0:T(8,128)(2,1)S(1)}, bf16[2,256,128]{2,1,0:T(8,128)(2,1)S(1)}, u32[]{:S(2)}, u32[]{:S(2)}) collective-permute-start(bf16[2,256,128]{2,1,0:T(8,128)(2,1)S(1)} %bitcast.18), channel_id=1, source_target_pairs={{0,8},{8,16},{16,24},{24,32},{32,40},{40,48},{48,56},{56,0},{1,9},... | collective-permute-start | bytes 393224 | tf_op jit(solution)/shard_map/ppermute | solution.py:155
  14.6 29.1 %all-to-all-start = ((s32[8,2,8]{2,1,0:T(2,128)}), s32[8,2,8]{2,1,0:T(2,128)S(1)}, u32[]{:S(2)}, u32[]{:S(2)}) async-start(s32[8,2,8]{2,1,0:T(2,128)} %broadcast_in_dim.20), calls=%async_computation | async-start | bytes 16384 | tf_op jit(solution)/shard_map/all_to_all | solution.py:20
  35.4 9.7 %collective-permute-start.3 = (bf16[2,64,128]{2,1,0:T(8,128)(2,1)S(1)}, bf16[2,64,128]{2,1,0:T(8,128)(2,1)S(1)}, u32[]{:S(2)}, u32[]{:S(2)}) collective-permute-start(bf16[2,64,128]{2,1,0:T(8,128)(2,1)S(1)} %slice.4), channel_id=1, source_target_pairs={{0,32},{8,40},{16,48},{24,56},{32,0},{40,8},{48,16},{56,24},{1,33}... | collective-permute-start | bytes 98312 | tf_op jit(solution)/shard_map/ppermute | solution.py:154

commit v5 on v4

--- a/solution.py
+++ b/solution.py
@@ -20,6 +20,74 @@
     return lax.all_to_all(x, axis, split_axis=0, concat_axis=0, tiled=True)
 
 
+def fetch(pairs, sems):
+    copies = [pltpu.make_async_copy(a, b, sems.at[i]) for i, (a, b) in enumerate(pairs)]
+    for copy in copies:
+        copy.start()
+    for copy in copies:
+        copy.wait()
+
+
+def first(keys_ref, values_ref, routes_ref, kv_ref, last_ref, message_ref, routes_vmem, sems):
+    shard_len, q_rows = keys_ref.shape[0], last_ref.shape[1]
+    end = pl.ds(shard_len - q_rows, q_rows)
+    pairs = [
+        (keys_ref, kv_ref.at[0]),
+        (values_ref, kv_ref.at[1]),
+        (keys_ref.at[end], last_ref.at[0]),
+        (values_ref.at[end], last_ref.at[1]),
+        (routes_ref, routes_vmem),
+    ]
+    fetch(pairs, sems)
+    message_ref[...] = jnp.broadcast_to(routes_vmem[...][None], message_ref.shape)
+
+
+def second(
+    shard_len,
+    q_hbm, lengths_hbm, routes_hbm, gates_hbm,
+    heads_ref, begin_ref, selector_ref, column_ref,
+    q_ref, lengths_ref, routes_ref, gates_ref, sems,
+):
+    pairs = [
+        (q_hbm, q_ref),
+        (lengths_hbm, lengths_ref),
+        (routes_hbm, routes_ref),
+        (gates_hbm, gates_ref),
+    ]
+    fetch(pairs, sems)
+    heads, q_rows, _ = heads_ref.shape
+    for h in range(heads):
+        heads_ref[h] = q_ref[:, h * HD : (h + 1) * HD]
+    routes = routes_ref[...]
+    place = lax.broadcasted_iota(jnp.int32, begin_ref.shape, 0)
+    qpos = (lax.axis_index("seq") + 1) * shard_len - q_rows + place
+    begin = jnp.zeros(begin_ref.shape, jnp.int32)
+    start = jnp.zeros((1, 1), jnp.int32)
+    for j in range(lengths_ref.shape[1]):
+        begin = jnp.where(start <= qpos, start, begin)
+        start = start + lengths_ref[:, j : j + 1]
+    begin_ref[...] = begin
+
+    _, rows, tokens = selector_ref.shape
+    capacity = 3
+    row = lax.broadcasted_iota(jnp.int32, (rows, tokens), 0)
+    named = [routes[k : k + 1, :] == row // capacity for k in range(2)]
+    before = lax.broadcasted_iota(jnp.int32, (tokens, tokens), 0) < (
+        lax.broadcasted_iota(jnp.int32, (tokens, tokens), 1)
+    )
+    either = (named[0] | named[1]).astype(F32).astype(BF16)
+    ahead = jnp.dot(either, before.astype(F32).astype(BF16), preferred_element_type=F32)
+    right = ahead == (row % capacity).astype(F32)
+    diagonal = lax.broadcasted_iota(jnp.int32, (tokens, tokens), 0) == (
+        lax.broadcasted_iota(jnp.int32, (tokens, tokens), 1)
+    )
+    for k in range(2):
+        selector_ref[k] = (named[k] & right).astype(F32).astype(BF16)
+        gate = jnp.where(diagonal, gates_ref[k : k + 1, :], F32(0))
+        gate = jnp.sum(gate, axis=1, keepdims=True)
+        column_ref[k] = jnp.broadcast_to(gate, column_ref.shape[1:])
+
+
 def attend(begin_ref, routes_ref, q_ref, *refs):
     parts, out_ref = refs[:-1], refs[-1]
     heads, q_rows, _ = q_ref.shape
@@ -27,7 +95,7 @@
     me = lax.axis_index("seq")
     rows = heads * q_rows
     queries = q_ref[...].reshape(rows, HD)
-    begin = begin_ref[...]
+    begin = jnp.concatenate([begin_ref[:, 0:1]] * heads, axis=0)
     place = lax.broadcasted_iota(jnp.int32, (rows, 1), 0) % q_rows
     qpos = (me + 1) * shard_len - q_rows + place
     scores = []
@@ -130,13 +198,19 @@
     out_ref[...] = (upper / (1.0 + jnp.exp(-upper))).astype(BF16)
 
 
-def mix(back_ref, selector_ref, gates_ref, out_ref):
-    tokens = gates_ref.shape[0] // 2
+def mix(back_ref, selector_ref, column_ref, out_ref):
     units = back_ref.shape[2]
     for s in range(back_ref.shape[0]):
-        rows = jnp.dot(selector_ref[...], back_ref[s], preferred_element_type=F32)
-        rows = rows * gates_ref[:, :1]
-        out_ref[:, s * units : (s + 1) * units] = (rows[:tokens] + rows[tokens:]).astype(BF16)
+        both = F32(0)
+        for k in range(2):
+            rows = lax.dot_general(
+                selector_ref[k],
+                back_ref[s],
+                (((0,), (0,)), ((), ())),
+                preferred_element_type=F32,
+            )
+            both = both + rows * column_ref[k, :, 0:1]
+        out_ref[:, s * units : (s + 1) * units] = both.astype(BF16)
 
 
 def shards(queries, keys, values, lengths, routes, gates, w_up):
@@ -149,28 +223,53 @@
     per_expert = expert_count * capacity
     reach = -(-(LONGEST - 1) // shard_len)
 
-    kv_own = jnp.concatenate([keys, values], axis=0).reshape(2, shard_len, HD)
+    heads = width // HD
+    keys, values, queries, lengths, routes, gates = (
+        pltpu.with_memory_space_constraint(x, pltpu.HBM)
+        for x in (keys, values, queries, lengths.reshape(1, -1), routes.T, gates.T)
+    )
+    hbm = pl.BlockSpec(memory_space=pltpu.HBM)
+    kv_own, kv_last, message = pl.pallas_call(
+        first,
+        out_shape=(
+            jax.ShapeDtypeStruct((2, shard_len, HD), BF16),
+            jax.ShapeDtypeStruct((2, q_rows, HD), BF16),
+            jax.ShapeDtypeStruct((expert_count, 2, tok_count), jnp.int32),
+        ),
+        in_specs=[hbm] * 3,
+        out_specs=(VMEM,) * 3,
+        scratch_shapes=[
+            pltpu.VMEM(routes.shape, jnp.int32),
+            pltpu.SemaphoreType.DMA((5,)),
+        ],
+        compiler_params=pltpu.CompilerParams(vmem_limit_bytes=8 << 20),
+        name="first",
+    )(keys, values, routes)
+    q_heads, begin, selectors, columns = pl.pallas_call(
+        functools.partial(second, shard_len),
+        out_shape=(
+            jax.ShapeDtypeStruct((heads, q_rows, HD), BF16),
+            jax.ShapeDtypeStruct((q_rows, HD), jnp.int32),
+            jax.ShapeDtypeStruct((2, per_expert, tok_count), BF16),
+            jax.ShapeDtypeStruct((2, tok_count, HD), F32),
+        ),
+        in_specs=[hbm] * 4,
+        out_specs=(VMEM,) * 4,
+        scratch_shapes=[
+            pltpu.VMEM(queries.shape, BF16),
+            pltpu.VMEM(lengths.shape, jnp.int32),
+            pltpu.VMEM(routes.shape, jnp.int32),
+            pltpu.VMEM(gates.shape, F32),
+            pltpu.SemaphoreType.DMA((4,)),
+        ],
+        compiler_params=pltpu.CompilerParams(vmem_limit_bytes=8 << 20),
+        cost_estimate=pl.CostEstimate(flops=4_000_000, bytes_accessed=200_000, transcendentals=0),
+        name="second",
+    )(queries, lengths, routes, gates)
     ring = [[(i, (i + d) % seq_count) for i in range(seq_count)] for d in range(reach + 1)]
-    last = lax.ppermute(kv_own[:, shard_len - q_rows :], "seq", ring[reach])
+    last = lax.ppermute(kv_last, "seq", ring[reach])
     parts = [kv_own] + [lax.ppermute(kv_own, "seq", ring[d]) for d in range(1, reach)] + [last]
-    row_routes = exchange(
-        jnp.broadcast_to(routes.T[None], (expert_count, 2, tok_count)), "expert"
-    )
-
-    heads = width // HD
-    q_heads = queries.reshape(q_rows, heads, HD).transpose(1, 0, 2)
-    starts = jnp.cumsum(lengths) - lengths
-    rows = jnp.arange(heads * q_rows, dtype=jnp.int32)[:, None]
-    qpos = (lax.axis_index("seq") + 1) * shard_len - q_rows + rows % q_rows
-    begin = jnp.max(jnp.where(starts[None, :] <= qpos, starts[None, :], 0), axis=1, keepdims=True)
-
-    flat = routes.T.reshape(-1)
-    token = jnp.arange(2 * tok_count, dtype=jnp.int32) % tok_count
-    before = (flat[:, None] == flat[None, :]) & (token[:, None] > token[None, :])
-    own_target = flat * capacity + jnp.sum(before.astype(jnp.int32), axis=1)
-    own_selector = (
-        own_target[:, None] == jnp.arange(per_expert, dtype=jnp.int32)[None, :]
-    ).astype(BF16)
+    row_routes = exchange(message, "expert")
 
     outgoing = pl.pallas_call(
         attend,
@@ -180,10 +279,6 @@
         compiler_params=pltpu.CompilerParams(vmem_limit_bytes=24 << 20),
         name="attend",
     )(begin, row_routes, q_heads, *parts)
-    gate_rows = jnp.broadcast_to(gates.T.reshape(-1, 1), (2 * tok_count, HD))
-    outgoing, own_selector, gate_rows = lax.optimization_barrier(
-        (outgoing, own_selector, gate_rows)
-    )
     landed = exchange(outgoing, "expert")
     packed = pl.pallas_call(
         pack,
@@ -216,7 +311,7 @@
         out_specs=VMEM,
         compiler_params=pltpu.CompilerParams(vmem_limit_bytes=16 << 20),
         name="mix",
-    )(back, own_selector, gate_rows)
+    )(back, selectors, columns)
 
 
 def solution(mesh):

time: 119 us -> 118 us (level)
  waiting for transfers between devices: 1.43 us -> 6.69 us
  blocking collectives: 65.7 us -> 62 us
  local copies, waits for them, and re-layouts: 3.48 us -> 0.45 us
  other arithmetic: 2.76 us -> 0 us
  Pallas kernels: 6.63 us -> 9.28 us
    all_to_all x1, waiting for transfers between devices: 0.01 us -> 6.68 us  [exchange(): return lax.all_to_all(x, axis, split_axis=0, concat_axis=0, tiled=True)]
    all_to_all x2, blocking collectives: 36.1 us -> 32.6 us  [exchange(): return lax.all_to_all(x, axis, split_axis=0, concat_axis=0, tiled=True)]
    pallas_call x0 -> x2, Pallas kernels: none -> 2.56 us  [the longest x1 1.52 us: shards(): pl.pallas_call(first, out_shape=(jax.ShapeDtypeStruct((2, shard_len, HD),...]
    broadcast_in_dim x4 -> x0, local copies, waits for them, and re-layouts: 2.24 us -> none  [the longest x1 1.28 us: shards(): jnp.broadcast_to(routes.T[None], (expert_count, 2, tok_count))]
    ppermute x1, waiting for transfers between devices: 1.42 us -> 0.01 us  [shards(): last = lax.ppermute(kv_last, 'seq', ring[reach])]
  transfers between devices with their start and end apart: 5 -> 5, of which waited for: 1 -> 1; matrix products, arithmetic and copies ran while one was open for 4% -> 0% of each run, Pallas kernels for 0% -> 1%
where the time goes in v5:
time: 118 us; the launch traced here: 117 us
  blocking collectives  62 us (53%)
  starting transfers between devices  38.3 us (32%)
  Pallas kernels  9.28 us (8%)
  waiting for transfers between devices  6.69 us (6%)
    all_to_all x2, blocking collectives, exchange(): return lax.all_to_all(x, axis, split_axis=0, concat_axis=0, tiled=True)  32.6 us
    all_gather x1, blocking collectives, shards(): incoming = lax.all_gather(packed, 'seq')  29.4 us
    all_to_all x1, starting transfers between devices, exchange(): return lax.all_to_all(x, axis, split_axis=0, concat_axis=0, tiled=True)  21.8 us
    ppermute x3, starting transfers between devices, shards(): lax.ppermute(kv_own, 'seq', ring[d])  12.4 us
    all_to_all x1, waiting for transfers between devices, exchange(): return lax.all_to_all(x, axis, split_axis=0, concat_axis=0, tiled=True)  6.68 us
    pallas_call x1, Pallas kernels, shards(): pl.pallas_call(functools.partial(project, expert_count), out_shape=jax.Sh...  4.49 us
    ppermute x1, starting transfers between devices, shards(): last = lax.ppermute(kv_last, 'seq', ring[reach])  4.16 us
  transfers between devices with their start and end apart: 5, of which 1 were waited for; matrix products, arithmetic and copies ran while one was open for 0% of the time, Pallas kernels for 1%

profile of v5, /device:TPU:112, one launch (start us, length us, event | category | flops | bytes accessed | tf_op | source)
XLA Modules:
  0.0 116.8 jit_solution(15404509503823677372)
XLA Ops:
  0.0 1.5 %first.1 = (bf16[2,256,128]{2,1,0:T(8,128)(2,1)S(1)}, bf16[2,64,128]{2,1,0:T(8,128)(2,1)S(1)}, s32[8,2,8]{2,1,0:T(2,128)}) custom-call(bf16[256,128]{1,0:T(8,128)(2,1)} %keys_ref.1, bf16[256,128]{1,0:T(8,128)(2,1)} %values_ref.1, s32[2,8]{1,0:T(2,128)} %bitcast.5), custom_call_target="tpu_custom_call" | custom-call | tf_op jit(solution)/shard_map/first/pallas_call | solution.py:232
  1.5 5.3 %collective-permute-start.2 = (bf16[2,256,128]{2,1,0:T(8,128)(2,1)S(1)}, bf16[2,256,128]{2,1,0:T(8,128)(2,1)S(1)}, u32[]{:S(2)}, u32[]{:S(2)}) collective-permute-start(bf16[2,256,128]{2,1,0:T(8,128)(2,1)S(1)} %get-tuple-element.15.refs_0_), channel_id=1, source_target_pairs={{0,24},{8,32},{16,40},{24,48},{32,56},{40,0},{48,8},{56,16},{1,25}... | collective-permute-start | bytes 393224 | tf_op jit(solution)/shard_map/ppermute | solution.py:271
  6.8 4.6 %collective-permute-start.1 = (bf16[2,256,128]{2,1,0:T(8,128)(2,1)S(1)}, bf16[2,256,128]{2,1,0:T(8,128)(2,1)S(1)}, u32[]{:S(2)}, u32[]{:S(2)}) collective-permute-start(bf16[2,256,128]{2,1,0:T(8,128)(2,1)S(1)} %get-tuple-element.15.refs_0_), channel_id=1, source_target_pairs={{0,16},{8,24},{16,32},{24,40},{32,48},{40,56},{48,0},{56,8},{1,17}... | collective-permute-start | bytes 393224 | tf_op jit(solution)/shard_map/ppermute | solution.py:271
  11.4 2.5 %collective-permute-start = (bf16[2,256,128]{2,1,0:T(8,128)(2,1)S(1)}, bf16[2,256,128]{2,1,0:T(8,128)(2,1)S(1)}, u32[]{:S(2)}, u32[]{:S(2)}) collective-permute-start(bf16[2,256,128]{2,1,0:T(8,128)(2,1)S(1)} %get-tuple-element.15.refs_0_), channel_id=1, source_target_pairs={{0,8},{8,16},{16,24},{24,32},{32,40},{40,48},{48,56},{56,0},{1,9},... | collective-permute-start | bytes 393224 | tf_op jit(solution)/shard_map/ppermute | solution.py:271
  13.9 4.2 %collective-permute-start.3 = (bf16[2,64,128]{2,1,0:T(8,128)(2,1)S(1)}, bf16[2,64,128]{2,1,0:T(8,128)(2,1)S(1)}, u32[]{:S(2)}, u32[]{:S(2)}) collective-permute-start(bf16[2,64,128]{2,1,0:T(8,128)(2,1)S(1)} %get-tuple-element.16), channel_id=1, source_target_pairs={{0,32},{8,40},{16,48},{24,56},{32,0},{40,8},{48,16},{56,24},{1,33}... | collective-permute-start | bytes 98312 | tf_op jit(solution)/shard_map/ppermute | solution.py:270
  18.1 21.8 %all-to-all-start = ((s32[8,2,8]{2,1,0:T(2,128)}), s32[8,2,8]{2,1,0:T(2,128)S(1)}, u32[]{:S(2)}, u32[]{:S(2)}) async-start(s32[8,2,8]{2,1,0:T(2,128)} %get-tuple-element.13), calls=%async_computation | async-start | bytes 16384 | tf_op jit(solution)/shard_map/all_to_all | solution.py:20
  39.9 1.0 second.1
  40.9 6.7 %all-to-all-done.routes_ref = s32[8,2,8]{2,1,0:T(2,128)S(1)} async-done(((s32[8,2,8]{2,1,0:T(2,128)}), s32[8,2,8]{2,1,0:T(2,128)S(1)}, u32[]{:S(2)}, u32[]{:S(2)}) %all-to-all-start) | async-done | bytes 544 | tf_op jit(solution)/shard_map/all_to_all | solution.py:20
  47.6 0.0 collective-permute-done.3.refs_4_
  47.6 0.0 collective-permute-done.2.refs_3_
  47.6 0.0 collective-permute-done.1.refs_2_
  47.6 0.0 collective-permute-done.refs_1_
  47.6 1.1 attend.1
  48.7 12.5 %all_to_all.15.x_ref = bf16[8,24,512]{2,1,0:T(8,128)(2,1)S(1)} all-to-all(bf16[8,24,512]{2,1,0:T(8,128)(2,1)S(1)} %attend.1), channel_id=1, replica_groups=mesh['dp'=16,'seq'=8,'expert'=8] {'expert'}, dimensions={0} | all-to-all | bytes 393216 | tf_op jit(solution)/shard_map/all_to_all | solution.py:20
  61.2 0.2 pack.1
  61.4 29.4 %all-gather.2 = s16[192,4224]{1,0:T(8,128)(2,1)S(1)} all-gather(s16[24,4224]{1,0:T(8,128)(2,1)S(1)} %pack.1), channel_id=2, replica_groups=mesh['dp'=16,'seq'=8,'expert'=8] {'seq'}, dimensions={0}, use_global_device_ids=true | all-gather | bytes 1824768 | tf_op jit(solution)/shard_map/all_gather | solution.py:291
  90.7 4.5 %project.1 = bf16[192,896]{1,0:T(8,128)(2,1)S(1)} custom-call(s16[8,24,4224]{2,1,0:T(8,128)(2,1)S(1)} %bitcast.4, bf16[1,4096,896]{2,1,0:T(8,128)(2,1)} %w_ref.1), custom_call_target="tpu_custom_call" | custom-call | tf_op jit(solution)/shard_map/project/pallas_call | solution.py:292
  95.2 0.2 reshape.10
  95.4 20.1 %all_to_all.16 = bf16[64,3,896]{2,1,0:T(4,128)(2,1)S(1)} all-to-all(bf16[64,3,896]{2,1,0:T(4,128)(2,1)S(1)} %reshape.10), channel_id=1, replica_groups=mesh['dp'=16,'seq'=8,'expert'=8] {'seq','expert'}, dimensions={0} | all-to-all | bytes 688128 | tf_op jit(solution)/shard_map/all_to_all | solution.py:20
  115.5 0.3 reshape.11.back_ref
  115.8 1.0 mix.1
Async XLA Ops:
  1.5 46.1 %collective-permute-start.2 = (bf16[2,256,128]{2,1,0:T(8,128)(2,1)S(1)}, bf16[2,256,128]{2,1,0:T(8,128)(2,1)S(1)}, u32[]{:S(2)}, u32[]{:S(2)}) collective-permute-start(bf16[2,256,128]{2,1,0:T(8,128)(2,1)S(1)} %get-tuple-element.15.refs_0_), channel_id=1, source_target_pairs={{0,24},{8,32},{16,40},{24,48},{32,56},{40,0},{48,8},{56,16},{1,25}... | collective-permute-start | bytes 393224 | tf_op jit(solution)/shard_map/ppermute | solution.py:271
  6.8 40.8 %collective-permute-start.1 = (bf16[2,256,128]{2,1,0:T(8,128)(2,1)S(1)}, bf16[2,256,128]{2,1,0:T(8,128)(2,1)S(1)}, u32[]{:S(2)}, u32[]{:S(2)}) collective-permute-start(bf16[2,256,128]{2,1,0:T(8,128)(2,1)S(1)} %get-tuple-element.15.refs_0_), channel_id=1, source_target_pairs={{0,16},{8,24},{16,32},{24,40},{32,48},{40,56},{48,0},{56,8},{1,17}... | collective-permute-start | bytes 393224 | tf_op jit(solution)/shard_map/ppermute | solution.py:271
  11.4 36.2 %collective-permute-start = (bf16[2,256,128]{2,1,0:T(8,128)(2,1)S(1)}, bf16[2,256,128]{2,1,0:T(8,128)(2,1)S(1)}, u32[]{:S(2)}, u32[]{:S(2)}) collective-permute-start(bf16[2,256,128]{2,1,0:T(8,128)(2,1)S(1)} %get-tuple-element.15.refs_0_), channel_id=1, source_target_pairs={{0,8},{8,16},{16,24},{24,32},{32,40},{40,48},{48,56},{56,0},{1,9},... | collective-permute-start | bytes 393224 | tf_op jit(solution)/shard_map/ppermute | solution.py:271
  13.9 33.7 %collective-permute-start.3 = (bf16[2,64,128]{2,1,0:T(8,128)(2,1)S(1)}, bf16[2,64,128]{2,1,0:T(8,128)(2,1)S(1)}, u32[]{:S(2)}, u32[]{:S(2)}) collective-permute-start(bf16[2,64,128]{2,1,0:T(8,128)(2,1)S(1)} %get-tuple-element.16), channel_id=1, source_target_pairs={{0,32},{8,40},{16,48},{24,56},{32,0},{40,8},{48,16},{56,24},{1,33}... | collective-permute-start | bytes 98312 | tf_op jit(solution)/shard_map/ppermute | solution.py:270
  18.1 29.5 %all-to-all-start = ((s32[8,2,8]{2,1,0:T(2,128)}), s32[8,2,8]{2,1,0:T(2,128)S(1)}, u32[]{:S(2)}, u32[]{:S(2)}) async-start(s32[8,2,8]{2,1,0:T(2,128)} %get-tuple-element.13), calls=%async_computation | async-start | bytes 16384 | tf_op jit(solution)/shard_map/all_to_all | solution.py:20

commit v6 on v5

--- a/solution.py
+++ b/solution.py
@@ -6,6 +6,7 @@
 from jax.experimental import pallas as pl
 from jax.experimental.pallas import tpu as pltpu
 from jax.sharding import PartitionSpec as P
+
 
 HD = 128
 LONGEST = 1024
@@ -28,18 +29,20 @@
         copy.wait()
 
 
-def first(keys_ref, values_ref, routes_ref, kv_ref, last_ref, message_ref, routes_vmem, sems):
-    shard_len, q_rows = keys_ref.shape[0], last_ref.shape[1]
-    end = pl.ds(shard_len - q_rows, q_rows)
+def first(keys_ref, values_ref, routes_ref, kv_ref, message_ref, routes_vmem, sems):
     pairs = [
         (keys_ref, kv_ref.at[0]),
         (values_ref, kv_ref.at[1]),
-        (keys_ref.at[end], last_ref.at[0]),
-        (values_ref.at[end], last_ref.at[1]),
         (routes_ref, routes_vmem),
     ]
     fetch(pairs, sems)
     message_ref[...] = jnp.broadcast_to(routes_vmem[...][None], message_ref.shape)
+
+
+def forward(near_ref, far_ref, out_ref):
+    rows = out_ref.shape[1] - near_ref.shape[1]
+    out_ref[:, :rows] = far_ref[:, far_ref.shape[1] - rows :]
+    out_ref[:, rows:] = near_ref[...]
 
 
 def second(
@@ -221,7 +224,8 @@
     capacity = 3
     tok_count = routes.shape[0]
     per_expert = expert_count * capacity
-    reach = -(-(LONGEST - 1) // shard_len)
+    reach = LONGEST + shard_len
+    reach = reach - (shard_len - q_rows)
 
     heads = width // HD
     keys, values, queries, lengths, routes, gates = (
@@ -229,18 +233,17 @@
         for x in (keys, values, queries, lengths.reshape(1, -1), routes.T, gates.T)
     )
     hbm = pl.BlockSpec(memory_space=pltpu.HBM)
-    kv_own, kv_last, message = pl.pallas_call(
+    kv_own, message = pl.pallas_call(
         first,
         out_shape=(
             jax.ShapeDtypeStruct((2, shard_len, HD), BF16),
-            jax.ShapeDtypeStruct((2, q_rows, HD), BF16),
             jax.ShapeDtypeStruct((expert_count, 2, tok_count), jnp.int32),
         ),
         in_specs=[hbm] * 3,
-        out_specs=(VMEM,) * 3,
+        out_specs=(VMEM,) * 2,
         scratch_shapes=[
             pltpu.VMEM(routes.shape, jnp.int32),
-            pltpu.SemaphoreType.DMA((5,)),
+            pltpu.SemaphoreType.DMA((3,)),
         ],
         compiler_params=pltpu.CompilerParams(vmem_limit_bytes=8 << 20),
         name="first",
@@ -266,9 +269,19 @@
         cost_estimate=pl.CostEstimate(flops=4_000_000, bytes_accessed=200_000, transcendentals=0),
         name="second",
     )(queries, lengths, routes, gates)
-    ring = [[(i, (i + d) % seq_count) for i in range(seq_count)] for d in range(reach + 1)]
-    last = lax.ppermute(kv_last, "seq", ring[reach])
-    parts = [kv_own] + [lax.ppermute(kv_own, "seq", ring[d]) for d in range(1, reach)] + [last]
+    by_one, by_two = ([(i, (i + d) % seq_count) for i in range(seq_count)] for d in (1, 2))
+    far = lax.ppermute(kv_own, "seq", by_two)
+    near = lax.ppermute(kv_own, "seq", by_one)
+    beyond = pl.pallas_call(
+        forward,
+        out_shape=jax.ShapeDtypeStruct((2, reach - 3 * shard_len, HD), BF16),
+        in_specs=[VMEM] * 2,
+        out_specs=VMEM,
+        compiler_params=pltpu.CompilerParams(vmem_limit_bytes=8 << 20),
+        name="forward",
+    )(near, far)
+    beyond = lax.ppermute(beyond, "seq", by_two)
+    parts = [kv_own, near, far, beyond]
     row_routes = exchange(message, "expert")
 
     outgoing = pl.pallas_call(
@@ -324,6 +337,7 @@
         P(("dp", "seq", "expert"), None),
         P("expert", None, "seq"),
     )
+
     return jax.shard_map(
         shards,
         mesh=mesh,

time: 118 us -> 114 us (0.966)
  starting transfers between devices: 38.3 us -> 28.1 us
  waiting for transfers between devices: 6.69 us -> 13.8 us
    ppermute x4 -> x3, waiting for transfers between devices: 0.01 us -> 7.12 us  [the longest x1 4.07 us: shards(): far = lax.ppermute(kv_own, 'seq', by_two)]
    ppermute x4 -> x3, starting transfers between devices: 16.5 us -> 11 us  [the longest x1 4.33 us: shards(): far = lax.ppermute(kv_own, 'seq', by_two)]
    all_to_all x1, starting transfers between devices: 21.8 us -> 17 us  [exchange(): return lax.all_to_all(x, axis, split_axis=0, concat_axis=0, tiled=True)]
  transfers between devices with their start and end apart: 5 -> 4, of which waited for: 1 -> 3; matrix products, arithmetic and copies ran while one was open for 0% -> 0% of each run, Pallas kernels for 1% -> 1%
where the time goes in v6:
time: 114 us; the launch traced here: 113 us
  blocking collectives  61.6 us (54%)
  starting transfers between devices  28.1 us (25%)
  waiting for transfers between devices  13.8 us (12%)
  Pallas kernels  9.3 us (8%)
    all_to_all x2, blocking collectives, exchange(): return lax.all_to_all(x, axis, split_axis=0, concat_axis=0, tiled=True)  32.5 us
    all_gather x1, blocking collectives, shards(): incoming = lax.all_gather(packed, 'seq')  29.1 us
    all_to_all x1, starting transfers between devices, exchange(): return lax.all_to_all(x, axis, split_axis=0, concat_axis=0, tiled=True)  17 us
    all_to_all x1, waiting for transfers between devices, exchange(): return lax.all_to_all(x, axis, split_axis=0, concat_axis=0, tiled=True)  6.68 us
    pallas_call x1, Pallas kernels, shards(): pl.pallas_call(functools.partial(project, expert_count), out_shape=jax.Sh...  4.49 us
    ppermute x1, starting transfers between devices, shards(): far = lax.ppermute(kv_own, 'seq', by_two)  4.33 us
    ppermute x1, waiting for transfers between devices, shards(): far = lax.ppermute(kv_own, 'seq', by_two)  4.07 us
    ppermute x1, starting transfers between devices, shards(): near = lax.ppermute(kv_own, 'seq', by_one)  3.4 us
  transfers between devices with their start and end apart: 4, of which 3 were waited for; matrix products, arithmetic and copies ran while one was open for 0% of the time, Pallas kernels for 1%

profile of v6, /device:TPU:112, one launch (start us, length us, event | category | flops | bytes accessed | tf_op | source)
XLA Modules:
  0.0 113.2 jit_solution(3048187133882498762)
XLA Ops:
  0.0 1.5 %first.1 = (bf16[2,256,128]{2,1,0:T(8,128)(2,1)S(1)}, s32[8,2,8]{2,1,0:T(2,128)}) custom-call(bf16[256,128]{1,0:T(8,128)(2,1)} %keys_ref.1, bf16[256,128]{1,0:T(8,128)(2,1)} %values_ref.1, s32[2,8]{1,0:T(2,128)} %bitcast.5), custom_call_target="tpu_custom_call" | custom-call | tf_op jit(solution)/shard_map/first/pallas_call | solution.py:236
  1.5 4.3 %collective-permute-start.1 = (bf16[2,256,128]{2,1,0:T(8,128)(2,1)S(1)}, bf16[2,256,128]{2,1,0:T(8,128)(2,1)S(1)}, u32[]{:S(2)}, u32[]{:S(2)}) collective-permute-start(bf16[2,256,128]{2,1,0:T(8,128)(2,1)S(1)} %get-tuple-element.14.refs_0_), channel_id=1, source_target_pairs={{0,16},{8,24},{16,32},{24,40},{32,48},{40,56},{48,0},{56,8},{1,17}... | collective-permute-start | bytes 393224 | tf_op jit(solution)/shard_map/ppermute | solution.py:273
  5.8 3.4 %collective-permute-start = (bf16[2,256,128]{2,1,0:T(8,128)(2,1)S(1)}, bf16[2,256,128]{2,1,0:T(8,128)(2,1)S(1)}, u32[]{:S(2)}, u32[]{:S(2)}) collective-permute-start(bf16[2,256,128]{2,1,0:T(8,128)(2,1)S(1)} %get-tuple-element.14.refs_0_), channel_id=1, source_target_pairs={{0,8},{8,16},{16,24},{24,32},{32,40},{40,48},{48,56},{56,0},{1,9},... | collective-permute-start | bytes 393224 | tf_op jit(solution)/shard_map/ppermute | solution.py:274
  9.2 4.1 %collective-permute-done.1.far_ref.refs_2_ = bf16[2,256,128]{2,1,0:T(8,128)(2,1)S(1)} collective-permute-done((bf16[2,256,128]{2,1,0:T(8,128)(2,1)S(1)}, bf16[2,256,128]{2,1,0:T(8,128)(2,1)S(1)}, u32[]{:S(2)}, u32[]{:S(2)}) %collective-permute-start.1) | collective-permute-done | bytes 131104 | tf_op jit(solution)/shard_map/ppermute | solution.py:273
  13.3 3.0 %collective-permute-done.near_ref.refs_1_ = bf16[2,256,128]{2,1,0:T(8,128)(2,1)S(1)} collective-permute-done((bf16[2,256,128]{2,1,0:T(8,128)(2,1)S(1)}, bf16[2,256,128]{2,1,0:T(8,128)(2,1)S(1)}, u32[]{:S(2)}, u32[]{:S(2)}) %collective-permute-start) | collective-permute-done | bytes 131104 | tf_op jit(solution)/shard_map/ppermute | solution.py:274
  16.4 3.3 %collective-permute-start.2 = (bf16[2,320,128]{2,1,0:T(8,128)(2,1)S(1)}, bf16[2,320,128]{2,1,0:T(8,128)(2,1)S(1)}, u32[]{:S(2)}, u32[]{:S(2)}) collective-permute-start(bf16[2,320,128]{2,1,0:T(8,128)(2,1)S(1)} %forward.1), channel_id=1, source_target_pairs={{0,16},{8,24},{16,32},{24,40},{32,48},{40,56},{48,0},{56,8},{1,17}... | collective-permute-start | bytes 491528 | tf_op jit(solution)/shard_map/ppermute | solution.py:283
  19.7 17.0 %all-to-all-start = ((s32[8,2,8]{2,1,0:T(2,128)}), s32[8,2,8]{2,1,0:T(2,128)S(1)}, u32[]{:S(2)}, u32[]{:S(2)}) async-start(s32[8,2,8]{2,1,0:T(2,128)} %get-tuple-element.12), calls=%async_computation | async-start | bytes 16384 | tf_op jit(solution)/shard_map/all_to_all | solution.py:21
  36.7 1.0 second.1
  37.8 6.7 %all-to-all-done.routes_ref = s32[8,2,8]{2,1,0:T(2,128)S(1)} async-done(((s32[8,2,8]{2,1,0:T(2,128)}), s32[8,2,8]{2,1,0:T(2,128)S(1)}, u32[]{:S(2)}, u32[]{:S(2)}) %all-to-all-start) | async-done | bytes 544 | tf_op jit(solution)/shard_map/all_to_all | solution.py:21
  44.4 0.0 collective-permute-done.2.refs_3_
  44.4 1.1 attend.1
  45.5 12.2 %all_to_all.15.x_ref = bf16[8,24,512]{2,1,0:T(8,128)(2,1)S(1)} all-to-all(bf16[8,24,512]{2,1,0:T(8,128)(2,1)S(1)} %attend.1), channel_id=1, replica_groups=mesh['dp'=16,'seq'=8,'expert'=8] {'expert'}, dimensions={0} | all-to-all | bytes 393216 | tf_op jit(solution)/shard_map/all_to_all | solution.py:21
  57.7 0.2 pack.1
  57.9 29.1 %all-gather.2 = s16[192,4224]{1,0:T(8,128)(2,1)S(1)} all-gather(s16[24,4224]{1,0:T(8,128)(2,1)S(1)} %pack.1), channel_id=2, replica_groups=mesh['dp'=16,'seq'=8,'expert'=8] {'seq'}, dimensions={0}, use_global_device_ids=true | all-gather | bytes 1824768 | tf_op jit(solution)/shard_map/all_gather | solution.py:304
  86.9 4.5 %project.1 = bf16[192,896]{1,0:T(8,128)(2,1)S(1)} custom-call(s16[8,24,4224]{2,1,0:T(8,128)(2,1)S(1)} %bitcast.4, bf16[1,4096,896]{2,1,0:T(8,128)(2,1)} %w_ref.1), custom_call_target="tpu_custom_call" | custom-call | tf_op jit(solution)/shard_map/project/pallas_call | solution.py:305
  91.4 0.2 reshape.10
  91.6 20.3 %all_to_all.16 = bf16[64,3,896]{2,1,0:T(4,128)(2,1)S(1)} all-to-all(bf16[64,3,896]{2,1,0:T(4,128)(2,1)S(1)} %reshape.10), channel_id=1, replica_groups=mesh['dp'=16,'seq'=8,'expert'=8] {'seq','expert'}, dimensions={0} | all-to-all | bytes 688128 | tf_op jit(solution)/shard_map/all_to_all | solution.py:21
  111.9 0.3 reshape.11.back_ref
  112.2 1.0 mix.1
  (1 shorter events, 0.0 us)
Async XLA Ops:
  1.5 11.8 %collective-permute-start.1 = (bf16[2,256,128]{2,1,0:T(8,128)(2,1)S(1)}, bf16[2,256,128]{2,1,0:T(8,128)(2,1)S(1)}, u32[]{:S(2)}, u32[]{:S(2)}) collective-permute-start(bf16[2,256,128]{2,1,0:T(8,128)(2,1)S(1)} %get-tuple-element.14.refs_0_), channel_id=1, source_target_pairs={{0,16},{8,24},{16,32},{24,40},{32,48},{40,56},{48,0},{56,8},{1,17}... | collective-permute-start | bytes 393224 | tf_op jit(solution)/shard_map/ppermute | solution.py:273
  5.8 10.5 %collective-permute-start = (bf16[2,256,128]{2,1,0:T(8,128)(2,1)S(1)}, bf16[2,256,128]{2,1,0:T(8,128)(2,1)S(1)}, u32[]{:S(2)}, u32[]{:S(2)}) collective-permute-start(bf16[2,256,128]{2,1,0:T(8,128)(2,1)S(1)} %get-tuple-element.14.refs_0_), channel_id=1, source_target_pairs={{0,8},{8,16},{16,24},{24,32},{32,40},{40,48},{48,56},{56,0},{1,9},... | collective-permute-start | bytes 393224 | tf_op jit(solution)/shard_map/ppermute | solution.py:274
  16.4 28.1 %collective-permute-start.2 = (bf16[2,320,128]{2,1,0:T(8,128)(2,1)S(1)}, bf16[2,320,128]{2,1,0:T(8,128)(2,1)S(1)}, u32[]{:S(2)}, u32[]{:S(2)}) collective-permute-start(bf16[2,320,128]{2,1,0:T(8,128)(2,1)S(1)} %forward.1), channel_id=1, source_target_pairs={{0,16},{8,24},{16,32},{24,40},{32,48},{40,56},{48,0},{56,8},{1,17}... | collective-permute-start | bytes 491528 | tf_op jit(solution)/shard_map/ppermute | solution.py:283
  19.7 24.7 %all-to-all-start = ((s32[8,2,8]{2,1,0:T(2,128)}), s32[8,2,8]{2,1,0:T(2,128)S(1)}, u32[]{:S(2)}, u32[]{:S(2)}) async-start(s32[8,2,8]{2,1,0:T(2,128)} %get-tuple-element.12), calls=%async_computation | async-start | bytes 16384 | tf_op jit(solution)/shard_map/all_to_all | solution.py:21

commit v7 on v6

--- a/solution.py
+++ b/solution.py
@@ -102,9 +102,11 @@
     place = lax.broadcasted_iota(jnp.int32, (rows, 1), 0) % q_rows
     qpos = (me + 1) * shard_len - q_rows + place
     scores = []
-    for d, part in enumerate(parts):
+    for d, part in zip((0, 1, 3, 2), parts):
         count = part.shape[1]
         kpos = (me + 1 - d) * shard_len - count + lax.broadcasted_iota(jnp.int32, (1, count), 1)
+        if count > shard_len:
+            kpos = jnp.where(kpos < (me - d) * shard_len, kpos - shard_len, kpos)
         score = lax.dot_general(
             queries, part[0], (((1,), (1,)), ((), ())), preferred_element_type=F32
         )
@@ -269,8 +271,8 @@
         cost_estimate=pl.CostEstimate(flops=4_000_000, bytes_accessed=200_000, transcendentals=0),
         name="second",
     )(queries, lengths, routes, gates)
-    by_one, by_two = ([(i, (i + d) % seq_count) for i in range(seq_count)] for d in (1, 2))
-    far = lax.ppermute(kv_own, "seq", by_two)
+    by_one, by_three = ([(i, (i + d) % seq_count) for i in range(seq_count)] for d in (1, 3))
+    far = lax.ppermute(kv_own, "seq", by_three)
     near = lax.ppermute(kv_own, "seq", by_one)
     beyond = pl.pallas_call(
         forward,
@@ -280,7 +282,7 @@
         compiler_params=pltpu.CompilerParams(vmem_limit_bytes=8 << 20),
         name="forward",
     )(near, far)
-    beyond = lax.ppermute(beyond, "seq", by_two)
+    beyond = lax.ppermute(beyond, "seq", by_one)
     parts = [kv_own, near, far, beyond]
     row_routes = exchange(message, "expert")
 

time: 114 us -> 119 us (1.044)
  starting transfers between devices: 28.1 us -> 32.6 us
  blocking collectives: 61.6 us -> 60 us
  waiting for transfers between devices: 13.8 us -> 15.4 us
    all_to_all x1, starting transfers between devices: 17 us -> 20.5 us  [exchange(): return lax.all_to_all(x, axis, split_axis=0, concat_axis=0, tiled=True)]
    ppermute x2, waiting for transfers between devices: 4.07 us -> 6.48 us  [the longest x1 6.47 us: shards(): far = lax.ppermute(kv_own, 'seq', by_three)]
    ppermute x1, starting transfers between devices: 3.4 us -> 4.61 us  [shards(): near = lax.ppermute(kv_own, 'seq', by_one)]
where the time goes in v7:
time: 119 us; the launch traced here: 118 us
  blocking collectives  60 us (50%)
  starting transfers between devices  32.6 us (27%)
  waiting for transfers between devices  15.4 us (13%)
  Pallas kernels  9.29 us (8%)
    all_to_all x2, blocking collectives, exchange(): return lax.all_to_all(x, axis, split_axis=0, concat_axis=0, tiled=True)  31.6 us
    all_gather x1, blocking collectives, shards(): incoming = lax.all_gather(packed, 'seq')  28.4 us
    all_to_all x1, starting transfers between devices, exchange(): return lax.all_to_all(x, axis, split_axis=0, concat_axis=0, tiled=True)  20.5 us
    all_to_all x1, waiting for transfers between devices, exchange(): return lax.all_to_all(x, axis, split_axis=0, concat_axis=0, tiled=True)  6.68 us
    ppermute x1, waiting for transfers between devices, shards(): far = lax.ppermute(kv_own, 'seq', by_three)  6.47 us
    ppermute x1, starting transfers between devices, shards(): far = lax.ppermute(kv_own, 'seq', by_three)  5.25 us
    ppermute x1, starting transfers between devices, shards(): near = lax.ppermute(kv_own, 'seq', by_one)  4.61 us
    pallas_call x1, Pallas kernels, shards(): pl.pallas_call(functools.partial(project, expert_count), out_shape=jax.Sh...  4.49 us
  transfers between devices with their start and end apart: 4, of which 3 were waited for; matrix products, arithmetic and copies ran while one was open for 0% of the time, Pallas kernels for 1%

profile of v7, /device:TPU:112, one launch (start us, length us, event | category | flops | bytes accessed | tf_op | source)
XLA Modules:
  0.0 117.8 jit_solution(9611129476357308942)
XLA Ops:
  0.0 1.5 %first.1 = (bf16[2,256,128]{2,1,0:T(8,128)(2,1)S(1)}, s32[8,2,8]{2,1,0:T(2,128)}) custom-call(bf16[256,128]{1,0:T(8,128)(2,1)} %keys_ref.1, bf16[256,128]{1,0:T(8,128)(2,1)} %values_ref.1, s32[2,8]{1,0:T(2,128)} %bitcast.5), custom_call_target="tpu_custom_call" | custom-call | tf_op jit(solution)/shard_map/first/pallas_call | solution.py:238
  1.5 5.3 %collective-permute-start.1 = (bf16[2,256,128]{2,1,0:T(8,128)(2,1)S(1)}, bf16[2,256,128]{2,1,0:T(8,128)(2,1)S(1)}, u32[]{:S(2)}, u32[]{:S(2)}) collective-permute-start(bf16[2,256,128]{2,1,0:T(8,128)(2,1)S(1)} %get-tuple-element.14.refs_0_), channel_id=1, source_target_pairs={{0,24},{8,32},{16,40},{24,48},{32,56},{40,0},{48,8},{56,16},{1,25}... | collective-permute-start | bytes 393224 | tf_op jit(solution)/shard_map/ppermute | solution.py:275
  6.8 4.6 %collective-permute-start = (bf16[2,256,128]{2,1,0:T(8,128)(2,1)S(1)}, bf16[2,256,128]{2,1,0:T(8,128)(2,1)S(1)}, u32[]{:S(2)}, u32[]{:S(2)}) collective-permute-start(bf16[2,256,128]{2,1,0:T(8,128)(2,1)S(1)} %get-tuple-element.14.refs_0_), channel_id=1, source_target_pairs={{0,8},{8,16},{16,24},{24,32},{32,40},{40,48},{48,56},{56,0},{1,9},... | collective-permute-start | bytes 393224 | tf_op jit(solution)/shard_map/ppermute | solution.py:276
  11.4 6.5 %collective-permute-done.1.far_ref.refs_2_ = bf16[2,256,128]{2,1,0:T(8,128)(2,1)S(1)} collective-permute-done((bf16[2,256,128]{2,1,0:T(8,128)(2,1)S(1)}, bf16[2,256,128]{2,1,0:T(8,128)(2,1)S(1)}, u32[]{:S(2)}, u32[]{:S(2)}) %collective-permute-start.1) | collective-permute-done | bytes 131104 | tf_op jit(solution)/shard_map/ppermute | solution.py:275
  17.9 2.2 %collective-permute-done.near_ref.refs_1_ = bf16[2,256,128]{2,1,0:T(8,128)(2,1)S(1)} collective-permute-done((bf16[2,256,128]{2,1,0:T(8,128)(2,1)S(1)}, bf16[2,256,128]{2,1,0:T(8,128)(2,1)S(1)}, u32[]{:S(2)}, u32[]{:S(2)}) %collective-permute-start) | collective-permute-done | bytes 131104 | tf_op jit(solution)/shard_map/ppermute | solution.py:276
  20.1 2.2 %collective-permute-start.2 = (bf16[2,320,128]{2,1,0:T(8,128)(2,1)S(1)}, bf16[2,320,128]{2,1,0:T(8,128)(2,1)S(1)}, u32[]{:S(2)}, u32[]{:S(2)}) collective-permute-start(bf16[2,320,128]{2,1,0:T(8,128)(2,1)S(1)} %forward.1), channel_id=1, source_target_pairs={{0,8},{8,16},{16,24},{24,32},{32,40},{40,48},{48,56},{56,0},{1,9},... | collective-permute-start | bytes 491528 | tf_op jit(solution)/shard_map/ppermute | solution.py:285
  22.3 20.5 %all-to-all-start = ((s32[8,2,8]{2,1,0:T(2,128)}), s32[8,2,8]{2,1,0:T(2,128)S(1)}, u32[]{:S(2)}, u32[]{:S(2)}) async-start(s32[8,2,8]{2,1,0:T(2,128)} %get-tuple-element.12), calls=%async_computation | async-start | bytes 16384 | tf_op jit(solution)/shard_map/all_to_all | solution.py:21
  42.8 1.0 second.1
  43.9 6.7 %all-to-all-done.routes_ref = s32[8,2,8]{2,1,0:T(2,128)S(1)} async-done(((s32[8,2,8]{2,1,0:T(2,128)}), s32[8,2,8]{2,1,0:T(2,128)S(1)}, u32[]{:S(2)}, u32[]{:S(2)}) %all-to-all-start) | async-done | bytes 544 | tf_op jit(solution)/shard_map/all_to_all | solution.py:21
  50.6 0.0 collective-permute-done.2.refs_3_
  50.6 1.1 attend.1
  51.7 12.2 %all_to_all.15.x_ref = bf16[8,24,512]{2,1,0:T(8,128)(2,1)S(1)} all-to-all(bf16[8,24,512]{2,1,0:T(8,128)(2,1)S(1)} %attend.1), channel_id=1, replica_groups=mesh['dp'=16,'seq'=8,'expert'=8] {'expert'}, dimensions={0} | all-to-all | bytes 393216 | tf_op jit(solution)/shard_map/all_to_all | solution.py:21
  63.8 0.2 pack.1
  64.0 28.4 %all-gather.2 = s16[192,4224]{1,0:T(8,128)(2,1)S(1)} all-gather(s16[24,4224]{1,0:T(8,128)(2,1)S(1)} %pack.1), channel_id=2, replica_groups=mesh['dp'=16,'seq'=8,'expert'=8] {'seq'}, dimensions={0}, use_global_device_ids=true | all-gather | bytes 1824768 | tf_op jit(solution)/shard_map/all_gather | solution.py:306
  92.4 4.5 %project.1 = bf16[192,896]{1,0:T(8,128)(2,1)S(1)} custom-call(s16[8,24,4224]{2,1,0:T(8,128)(2,1)S(1)} %bitcast.4, bf16[1,4096,896]{2,1,0:T(8,128)(2,1)} %w_ref.1), custom_call_target="tpu_custom_call" | custom-call | tf_op jit(solution)/shard_map/project/pallas_call | solution.py:307
  96.9 0.2 reshape.10
  97.1 19.4 %all_to_all.16 = bf16[64,3,896]{2,1,0:T(4,128)(2,1)S(1)} all-to-all(bf16[64,3,896]{2,1,0:T(4,128)(2,1)S(1)} %reshape.10), channel_id=1, replica_groups=mesh['dp'=16,'seq'=8,'expert'=8] {'seq','expert'}, dimensions={0} | all-to-all | bytes 688128 | tf_op jit(solution)/shard_map/all_to_all | solution.py:21
  116.5 0.3 reshape.11.back_ref
  116.8 1.0 mix.1
  (1 shorter events, 0.0 us)
Async XLA Ops:
  1.5 16.4 %collective-permute-start.1 = (bf16[2,256,128]{2,1,0:T(8,128)(2,1)S(1)}, bf16[2,256,128]{2,1,0:T(8,128)(2,1)S(1)}, u32[]{:S(2)}, u32[]{:S(2)}) collective-permute-start(bf16[2,256,128]{2,1,0:T(8,128)(2,1)S(1)} %get-tuple-element.14.refs_0_), channel_id=1, source_target_pairs={{0,24},{8,32},{16,40},{24,48},{32,56},{40,0},{48,8},{56,16},{1,25}... | collective-permute-start | bytes 393224 | tf_op jit(solution)/shard_map/ppermute | solution.py:275
  6.8 13.3 %collective-permute-start = (bf16[2,256,128]{2,1,0:T(8,128)(2,1)S(1)}, bf16[2,256,128]{2,1,0:T(8,128)(2,1)S(1)}, u32[]{:S(2)}, u32[]{:S(2)}) collective-permute-start(bf16[2,256,128]{2,1,0:T(8,128)(2,1)S(1)} %get-tuple-element.14.refs_0_), channel_id=1, source_target_pairs={{0,8},{8,16},{16,24},{24,32},{32,40},{40,48},{48,56},{56,0},{1,9},... | collective-permute-start | bytes 393224 | tf_op jit(solution)/shard_map/ppermute | solution.py:276
  20.1 30.5 %collective-permute-start.2 = (bf16[2,320,128]{2,1,0:T(8,128)(2,1)S(1)}, bf16[2,320,128]{2,1,0:T(8,128)(2,1)S(1)}, u32[]{:S(2)}, u32[]{:S(2)}) collective-permute-start(bf16[2,320,128]{2,1,0:T(8,128)(2,1)S(1)} %forward.1), channel_id=1, source_target_pairs={{0,8},{8,16},{16,24},{24,32},{32,40},{40,48},{48,56},{56,0},{1,9},... | collective-permute-start | bytes 491528 | tf_op jit(solution)/shard_map/ppermute | solution.py:285
  22.3 28.2 %all-to-all-start = ((s32[8,2,8]{2,1,0:T(2,128)}), s32[8,2,8]{2,1,0:T(2,128)S(1)}, u32[]{:S(2)}, u32[]{:S(2)}) async-start(s32[8,2,8]{2,1,0:T(2,128)} %get-tuple-element.12), calls=%async_computation | async-start | bytes 16384 | tf_op jit(solution)/shard_map/all_to_all | solution.py:21

commit v8 on v6

--- a/solution.py
+++ b/solution.py
@@ -12,6 +12,7 @@
 LONGEST = 1024
 FIXED = 32767
 DIGITS = 8192
+ROUTE_ROWS = 16
 F32 = jnp.float32
 BF16 = jnp.bfloat16
 VMEM = pl.BlockSpec(memory_space=pltpu.VMEM)
@@ -19,6 +20,10 @@
 
 def exchange(x, axis):
     return lax.all_to_all(x, axis, split_axis=0, concat_axis=0, tiled=True)
+
+
+def worked_on():
+    return lax.rem(lax.axis_index("seq") + 1, lax.axis_size("seq"))
 
 
 def fetch(pairs, sems):
@@ -29,41 +34,56 @@
         copy.wait()
 
 
-def first(keys_ref, values_ref, routes_ref, kv_ref, message_ref, routes_vmem, sems):
+def first(keys_ref, values_ref, q_ref, routes_ref, kv_ref, left_ref, routes_vmem, sems):
+    shard_len = keys_ref.shape[0]
+    q_rows = q_ref.shape[0]
+    heads = q_ref.shape[1] // HD
     pairs = [
         (keys_ref, kv_ref.at[0]),
         (values_ref, kv_ref.at[1]),
+        (keys_ref, left_ref.at[pl.ds(0, shard_len)]),
+        (values_ref, left_ref.at[pl.ds(shard_len, shard_len)]),
         (routes_ref, routes_vmem),
     ]
+    for h in range(heads):
+        pairs.append(
+            (
+                q_ref.at[:, pl.ds(h * HD, HD)],
+                left_ref.at[pl.ds(2 * shard_len + h * q_rows, q_rows)],
+            )
+        )
     fetch(pairs, sems)
-    message_ref[...] = jnp.broadcast_to(routes_vmem[...][None], message_ref.shape)
-
-
-def forward(near_ref, far_ref, out_ref):
-    rows = out_ref.shape[1] - near_ref.shape[1]
-    out_ref[:, :rows] = far_ref[:, far_ref.shape[1] - rows :]
-    out_ref[:, rows:] = near_ref[...]
+    at = 2 * shard_len + heads * q_rows
+    size = left_ref.shape[0] - at
+    choices, tokens = routes_vmem.shape
+    left_ref[at:] = jnp.zeros((size, HD), BF16)
+    left_ref[at : at + choices, :tokens] = routes_vmem[...].astype(F32).astype(BF16)
+
+
+def forward(own_ref, near_ref, came_ref, out_ref, message_ref):
+    rows = out_ref.shape[1] - own_ref.shape[1]
+    out_ref[:, :rows] = near_ref[:, near_ref.shape[1] - rows :]
+    out_ref[:, rows:] = own_ref[...]
+    tail = came_ref[came_ref.shape[0] - ROUTE_ROWS :].astype(F32).astype(jnp.int32)
+    _, choices, tokens = message_ref.shape
+    message_ref[...] = jnp.broadcast_to(tail[:choices, :tokens][None], message_ref.shape)
 
 
 def second(
-    shard_len,
-    q_hbm, lengths_hbm, routes_hbm, gates_hbm,
-    heads_ref, begin_ref, selector_ref, column_ref,
-    q_ref, lengths_ref, routes_ref, gates_ref, sems,
+    shard_len, q_rows,
+    lengths_hbm, routes_hbm, gates_hbm,
+    begin_ref, selector_ref, column_ref,
+    lengths_ref, routes_ref, gates_ref, sems,
 ):
     pairs = [
-        (q_hbm, q_ref),
         (lengths_hbm, lengths_ref),
         (routes_hbm, routes_ref),
         (gates_hbm, gates_ref),
     ]
     fetch(pairs, sems)
-    heads, q_rows, _ = heads_ref.shape
-    for h in range(heads):
-        heads_ref[h] = q_ref[:, h * HD : (h + 1) * HD]
     routes = routes_ref[...]
     place = lax.broadcasted_iota(jnp.int32, begin_ref.shape, 0)
-    qpos = (lax.axis_index("seq") + 1) * shard_len - q_rows + place
+    qpos = (worked_on() + 1) * shard_len - q_rows + place
     begin = jnp.zeros(begin_ref.shape, jnp.int32)
     start = jnp.zeros((1, 1), jnp.int32)
     for j in range(lengths_ref.shape[1]):
@@ -91,23 +111,23 @@
         column_ref[k] = jnp.broadcast_to(gate, column_ref.shape[1:])
 
 
-def attend(begin_ref, routes_ref, q_ref, *refs):
-    parts, out_ref = refs[:-1], refs[-1]
-    heads, q_rows, _ = q_ref.shape
-    shard_len = parts[0].shape[1]
-    me = lax.axis_index("seq")
+def attend(begin_ref, routes_ref, came_ref, own_ref, near_ref, beyond_ref, out_ref):
+    shard_len = own_ref.shape[1]
+    q_rows = begin_ref.shape[0]
+    heads = out_ref.shape[2] // HD
+    me = worked_on()
     rows = heads * q_rows
-    queries = q_ref[...].reshape(rows, HD)
+    queries = came_ref[2 * shard_len : 2 * shard_len + rows]
     begin = jnp.concatenate([begin_ref[:, 0:1]] * heads, axis=0)
     place = lax.broadcasted_iota(jnp.int32, (rows, 1), 0) % q_rows
     qpos = (me + 1) * shard_len - q_rows + place
+    parts = [(came_ref[:shard_len], came_ref[shard_len : 2 * shard_len])]
+    parts += [(ref[0], ref[1]) for ref in (own_ref, near_ref, beyond_ref)]
     scores = []
-    for d, part in enumerate(parts):
-        count = part.shape[1]
+    for d, (keys, _) in enumerate(parts):
+        count = keys.shape[0]
         kpos = (me + 1 - d) * shard_len - count + lax.broadcasted_iota(jnp.int32, (1, count), 1)
-        score = lax.dot_general(
-            queries, part[0], (((1,), (1,)), ((), ())), preferred_element_type=F32
-        )
+        score = lax.dot_general(queries, keys, (((1,), (1,)), ((), ())), preferred_element_type=F32)
         allowed = kpos >= begin
         if d == 0:
             allowed = allowed & (kpos <= qpos)
@@ -115,10 +135,10 @@
     peak = functools.reduce(jnp.maximum, [jnp.max(s, axis=1, keepdims=True) for s in scores])
     total = jnp.zeros((rows, 1), F32)
     acc = jnp.zeros((rows, HD), F32)
-    for score, part in zip(scores, parts):
+    for score, (_, values) in zip(scores, parts):
         weight = jnp.exp((score - peak) * F32(HD**-0.5))
         total = total + jnp.sum(weight, axis=1, keepdims=True)
-        acc = acc + jnp.dot(weight.astype(BF16), part[1], preferred_element_type=F32)
+        acc = acc + jnp.dot(weight.astype(BF16), values, preferred_element_type=F32)
     attended = (acc / total).astype(BF16)
     wide = jnp.concatenate([attended[h * q_rows : (h + 1) * q_rows] for h in range(heads)], axis=1)
 
@@ -183,8 +203,10 @@
         return pltpu.make_async_copy(w_ref.at[0, at], w_vmem.at[at], sems.at[e])
 
     def rows(lo, size):
-        part = [x_ref[s, :, lo : lo + size].astype(jnp.int32) for s in range(seq_count)]
+        part = [x_ref[s - 1, :, lo : lo + size].astype(jnp.int32) for s in order]
         return jnp.concatenate(part, axis=0).astype(F32)
+
+    order = [s or seq_count for s in range(seq_count)]
 
     for e in range(chunks):
         copy(e).start()
@@ -233,65 +255,70 @@
         for x in (keys, values, queries, lengths.reshape(1, -1), routes.T, gates.T)
     )
     hbm = pl.BlockSpec(memory_space=pltpu.HBM)
-    kv_own, message = pl.pallas_call(
+    small = pltpu.CompilerParams(vmem_limit_bytes=8 << 20)
+    left_rows = 2 * shard_len + heads * q_rows + ROUTE_ROWS
+    own, left = pl.pallas_call(
         first,
         out_shape=(
             jax.ShapeDtypeStruct((2, shard_len, HD), BF16),
-            jax.ShapeDtypeStruct((expert_count, 2, tok_count), jnp.int32),
+            jax.ShapeDtypeStruct((left_rows, HD), BF16),
         ),
-        in_specs=[hbm] * 3,
+        in_specs=[hbm] * 4,
         out_specs=(VMEM,) * 2,
         scratch_shapes=[
             pltpu.VMEM(routes.shape, jnp.int32),
-            pltpu.SemaphoreType.DMA((3,)),
+            pltpu.SemaphoreType.DMA((5 + heads,)),
         ],
-        compiler_params=pltpu.CompilerParams(vmem_limit_bytes=8 << 20),
+        compiler_params=small,
         name="first",
-    )(keys, values, routes)
-    q_heads, begin, selectors, columns = pl.pallas_call(
-        functools.partial(second, shard_len),
+    )(keys, values, queries, routes)
+    begin, selectors, columns = pl.pallas_call(
+        functools.partial(second, shard_len, q_rows),
         out_shape=(
-            jax.ShapeDtypeStruct((heads, q_rows, HD), BF16),
             jax.ShapeDtypeStruct((q_rows, HD), jnp.int32),
             jax.ShapeDtypeStruct((2, per_expert, tok_count), BF16),
             jax.ShapeDtypeStruct((2, tok_count, HD), F32),
         ),
-        in_specs=[hbm] * 4,
-        out_specs=(VMEM,) * 4,
+        in_specs=[hbm] * 3,
+        out_specs=(VMEM,) * 3,
         scratch_shapes=[
-            pltpu.VMEM(queries.shape, BF16),
             pltpu.VMEM(lengths.shape, jnp.int32),
             pltpu.VMEM(routes.shape, jnp.int32),
             pltpu.VMEM(gates.shape, F32),
-            pltpu.SemaphoreType.DMA((4,)),
+            pltpu.SemaphoreType.DMA((3,)),
         ],
-        compiler_params=pltpu.CompilerParams(vmem_limit_bytes=8 << 20),
+        compiler_params=small,
         cost_estimate=pl.CostEstimate(flops=4_000_000, bytes_accessed=200_000, transcendentals=0),
         name="second",
-    )(queries, lengths, routes, gates)
-    by_one, by_two = ([(i, (i + d) % seq_count) for i in range(seq_count)] for d in (1, 2))
-    far = lax.ppermute(kv_own, "seq", by_two)
-    near = lax.ppermute(kv_own, "seq", by_one)
-    beyond = pl.pallas_call(
+    )(lengths, routes, gates)
+
+    def shifted(x, by):
+        return lax.ppermute(x, "seq", [(i, (i + by) % seq_count) for i in range(seq_count)])
+
+    came = shifted(left, -1)
+    near = shifted(own, 1)
+    beyond, message = pl.pallas_call(
         forward,
-        out_shape=jax.ShapeDtypeStruct((2, reach - 3 * shard_len, HD), BF16),
-        in_specs=[VMEM] * 2,
-        out_specs=VMEM,
-        compiler_params=pltpu.CompilerParams(vmem_limit_bytes=8 << 20),
+        out_shape=(
+            jax.ShapeDtypeStruct((2, reach - 3 * shard_len, HD), BF16),
+            jax.ShapeDtypeStruct((expert_count, 2, tok_count), jnp.int32),
+        ),
+        in_specs=[VMEM] * 3,
+        out_specs=(VMEM,) * 2,
+        compiler_params=small,
         name="forward",
-    )(near, far)
-    beyond = lax.ppermute(beyond, "seq", by_two)
-    parts = [kv_own, near, far, beyond]
+    )(own, near, came)
+    beyond = shifted(beyond, 2)
     row_routes = exchange(message, "expert")
 
     outgoing = pl.pallas_call(
         attend,
         out_shape=jax.ShapeDtypeStruct((expert_count, per_expert, width), BF16),
-        in_specs=[VMEM] * (3 + len(parts)),
+        in_specs=[VMEM] * 6,
         out_specs=VMEM,
         compiler_params=pltpu.CompilerParams(vmem_limit_bytes=24 << 20),
         name="attend",
-    )(begin, row_routes, q_heads, *parts)
+    )(begin, row_routes, came, own, near, beyond)
     landed = exchange(outgoing, "expert")
     packed = pl.pallas_call(
         pack,

time: 114 us -> 111 us (0.974)
  starting transfers between devices: 28.1 us -> 25.3 us
    ppermute x3, starting transfers between devices: 11 us -> 8.61 us  [shifted(): lax.ppermute(x, 'seq', [(i, (i + by) % seq_count) for i in range(seq_coun...]
  transfers between devices with their start and end apart: 4 -> 4, of which waited for: 3 -> 2; matrix products, arithmetic and copies ran while one was open for 0% -> 0% of each run, Pallas kernels for 1% -> 1%
where the time goes in v8:
time: 111 us
  blocking collectives  62.6 us (56%)
  starting transfers between devices  25.3 us (23%)
  waiting for transfers between devices  13 us (12%)
  Pallas kernels  9.26 us (8%)
    all_to_all x2, blocking collectives, exchange(): return lax.all_to_all(x, axis, split_axis=0, concat_axis=0, tiled=True)  32.5 us
    all_gather x1, blocking collectives, shards(): incoming = lax.all_gather(packed, 'seq')  30.1 us
    all_to_all x1, starting transfers between devices, exchange(): return lax.all_to_all(x, axis, split_axis=0, concat_axis=0, tiled=True)  16.7 us
    ppermute x3, starting transfers between devices, shifted(): lax.ppermute(x, 'seq', [(i, (i + by) % seq_count) for i in range(seq_coun...  8.61 us
    all_to_all x1, waiting for transfers between devices, exchange(): return lax.all_to_all(x, axis, split_axis=0, concat_axis=0, tiled=True)  6.83 us
    ppermute x3, waiting for transfers between devices, shifted(): lax.ppermute(x, 'seq', [(i, (i + by) % seq_count) for i in range(seq_coun...  6.15 us
    pallas_call x1, Pallas kernels, shards(): pl.pallas_call(functools.partial(project, expert_count), out_shape=jax.Sh...  4.49 us
  transfers between devices with their start and end apart: 4, of which 2 were waited for; matrix products, arithmetic and copies ran while one was open for 0% of the time, Pallas kernels for 1%

profile of v8, /device:TPU:112, one launch (start us, length us, event | category | flops | bytes accessed | tf_op | source)
XLA Modules:
  0.0 110.6 jit_solution(4211292029685195516)
XLA Ops:
  0.0 1.0 first.1
  1.0 4.8 %collective-permute-start.1 = (bf16[784,128]{1,0:T(8,128)(2,1)S(1)}, bf16[784,128]{1,0:T(8,128)(2,1)S(1)}, u32[]{:S(2)}, u32[]{:S(2)}) collective-permute-start(bf16[784,128]{1,0:T(8,128)(2,1)S(1)} %get-tuple-element.14), channel_id=1, source_target_pairs={{0,56},{8,0},{16,8},{24,16},{32,24},{40,32},{48,40},{56,48},{1,57}... | collective-permute-start | bytes 602120 | tf_op jit(solution)/shard_map/ppermute | solution.py:296
  5.8 1.9 %collective-permute-start = (bf16[2,256,128]{2,1,0:T(8,128)(2,1)S(1)}, bf16[2,256,128]{2,1,0:T(8,128)(2,1)S(1)}, u32[]{:S(2)}, u32[]{:S(2)}) collective-permute-start(bf16[2,256,128]{2,1,0:T(8,128)(2,1)S(1)} %get-tuple-element.13.own_ref), channel_id=1, source_target_pairs={{0,8},{8,16},{16,24},{24,32},{32,40},{40,48},{48,56},{56,0},{1,9},... | collective-permute-start | bytes 393224 | tf_op jit(solution)/shard_map/ppermute | solution.py:296
  7.7 6.1 %collective-permute-done.near_ref = bf16[2,256,128]{2,1,0:T(8,128)(2,1)S(1)} collective-permute-done((bf16[2,256,128]{2,1,0:T(8,128)(2,1)S(1)}, bf16[2,256,128]{2,1,0:T(8,128)(2,1)S(1)}, u32[]{:S(2)}, u32[]{:S(2)}) %collective-permute-start) | collective-permute-done | bytes 131104 | tf_op jit(solution)/shard_map/ppermute | solution.py:296
  13.9 0.0 collective-permute-done.1.came_ref
  13.9 0.6 forward.1
  14.5 1.9 %collective-permute-start.2 = (bf16[2,320,128]{2,1,0:T(8,128)(2,1)S(1)}, bf16[2,320,128]{2,1,0:T(8,128)(2,1)S(1)}, u32[]{:S(2)}, u32[]{:S(2)}) collective-permute-start(bf16[2,320,128]{2,1,0:T(8,128)(2,1)S(1)} %get-tuple-element.16), channel_id=1, source_target_pairs={{0,16},{8,24},{16,32},{24,40},{32,48},{40,56},{48,0},{56,8},{1,17}... | collective-permute-start | bytes 491528 | tf_op jit(solution)/shard_map/ppermute | solution.py:296
  16.4 16.7 %all-to-all-start = ((s32[8,2,8]{2,1,0:T(2,128)}), s32[8,2,8]{2,1,0:T(2,128)S(1)}, u32[]{:S(2)}, u32[]{:S(2)}) async-start(s32[8,2,8]{2,1,0:T(2,128)} %get-tuple-element.15), calls=%async_computation | async-start | bytes 16384 | tf_op jit(solution)/shard_map/all_to_all | solution.py:22
  33.1 0.9 second.1
  34.0 6.8 %all-to-all-done.routes_ref = s32[8,2,8]{2,1,0:T(2,128)S(1)} async-done(((s32[8,2,8]{2,1,0:T(2,128)}), s32[8,2,8]{2,1,0:T(2,128)S(1)}, u32[]{:S(2)}, u32[]{:S(2)}) %all-to-all-start) | async-done | bytes 544 | tf_op jit(solution)/shard_map/all_to_all | solution.py:22
  40.9 0.0 collective-permute-done.2.beyond_ref
  40.9 1.1 attend.1
  41.9 12.2 %all_to_all.15.x_ref = bf16[8,24,512]{2,1,0:T(8,128)(2,1)S(1)} all-to-all(bf16[8,24,512]{2,1,0:T(8,128)(2,1)S(1)} %attend.1), channel_id=1, replica_groups=mesh['dp'=16,'seq'=8,'expert'=8] {'expert'}, dimensions={0} | all-to-all | bytes 393216 | tf_op jit(solution)/shard_map/all_to_all | solution.py:22
  54.1 0.2 pack.1
  54.3 30.1 %all-gather.2 = s16[192,4224]{1,0:T(8,128)(2,1)S(1)} all-gather(s16[24,4224]{1,0:T(8,128)(2,1)S(1)} %pack.1), channel_id=2, replica_groups=mesh['dp'=16,'seq'=8,'expert'=8] {'seq'}, dimensions={0}, use_global_device_ids=true | all-gather | bytes 1824768 | tf_op jit(solution)/shard_map/all_gather | solution.py:331
  84.4 4.5 %project.1 = bf16[192,896]{1,0:T(8,128)(2,1)S(1)} custom-call(s16[8,24,4224]{2,1,0:T(8,128)(2,1)S(1)} %bitcast.4, bf16[1,4096,896]{2,1,0:T(8,128)(2,1)} %w_ref.1), custom_call_target="tpu_custom_call" | custom-call | tf_op jit(solution)/shard_map/project/pallas_call | solution.py:332
  88.9 0.2 reshape.10
  89.0 20.3 %all_to_all.16 = bf16[64,3,896]{2,1,0:T(4,128)(2,1)S(1)} all-to-all(bf16[64,3,896]{2,1,0:T(4,128)(2,1)S(1)} %reshape.10), channel_id=1, replica_groups=mesh['dp'=16,'seq'=8,'expert'=8] {'seq','expert'}, dimensions={0} | all-to-all | bytes 688128 | tf_op jit(solution)/shard_map/all_to_all | solution.py:22
  109.4 0.3 reshape.11.back_ref
  109.7 1.0 mix.1
Async XLA Ops:
  1.0 12.9 %collective-permute-start.1 = (bf16[784,128]{1,0:T(8,128)(2,1)S(1)}, bf16[784,128]{1,0:T(8,128)(2,1)S(1)}, u32[]{:S(2)}, u32[]{:S(2)}) collective-permute-start(bf16[784,128]{1,0:T(8,128)(2,1)S(1)} %get-tuple-element.14), channel_id=1, source_target_pairs={{0,56},{8,0},{16,8},{24,16},{32,24},{40,32},{48,40},{56,48},{1,57}... | collective-permute-start | bytes 602120 | tf_op jit(solution)/shard_map/ppermute | solution.py:296
  5.8 8.1 %collective-permute-start = (bf16[2,256,128]{2,1,0:T(8,128)(2,1)S(1)}, bf16[2,256,128]{2,1,0:T(8,128)(2,1)S(1)}, u32[]{:S(2)}, u32[]{:S(2)}) collective-permute-start(bf16[2,256,128]{2,1,0:T(8,128)(2,1)S(1)} %get-tuple-element.13.own_ref), channel_id=1, source_target_pairs={{0,8},{8,16},{16,24},{24,32},{32,40},{40,48},{48,56},{56,0},{1,9},... | collective-permute-start | bytes 393224 | tf_op jit(solution)/shard_map/ppermute | solution.py:296
  14.5 26.3 %collective-permute-start.2 = (bf16[2,320,128]{2,1,0:T(8,128)(2,1)S(1)}, bf16[2,320,128]{2,1,0:T(8,128)(2,1)S(1)}, u32[]{:S(2)}, u32[]{:S(2)}) collective-permute-start(bf16[2,320,128]{2,1,0:T(8,128)(2,1)S(1)} %get-tuple-element.16), channel_id=1, source_target_pairs={{0,16},{8,24},{16,32},{24,40},{32,48},{40,56},{48,0},{56,8},{1,17}... | collective-permute-start | bytes 491528 | tf_op jit(solution)/shard_map/ppermute | solution.py:296
  16.4 24.4 %all-to-all-start = ((s32[8,2,8]{2,1,0:T(2,128)}), s32[8,2,8]{2,1,0:T(2,128)S(1)}, u32[]{:S(2)}, u32[]{:S(2)}) async-start(s32[8,2,8]{2,1,0:T(2,128)} %get-tuple-element.15), calls=%async_computation | async-start | bytes 16384 | tf_op jit(solution)/shard_map/all_to_all | solution.py:22

commit v9 on v8

--- a/solution.py
+++ b/solution.py
@@ -12,7 +12,6 @@
 LONGEST = 1024
 FIXED = 32767
 DIGITS = 8192
-ROUTE_ROWS = 16
 F32 = jnp.float32
 BF16 = jnp.bfloat16
 VMEM = pl.BlockSpec(memory_space=pltpu.VMEM)
@@ -34,7 +33,11 @@
         copy.wait()
 
 
-def first(keys_ref, values_ref, q_ref, routes_ref, kv_ref, left_ref, routes_vmem, sems):
+def first(
+    keys_ref, values_ref, q_ref, routes_ref,
+    kv_ref, left_ref, message_ref,
+    routes_vmem, sems,
+):
     shard_len = keys_ref.shape[0]
     q_rows = q_ref.shape[0]
     heads = q_ref.shape[1] // HD
@@ -53,20 +56,13 @@
             )
         )
     fetch(pairs, sems)
-    at = 2 * shard_len + heads * q_rows
-    size = left_ref.shape[0] - at
-    choices, tokens = routes_vmem.shape
-    left_ref[at:] = jnp.zeros((size, HD), BF16)
-    left_ref[at : at + choices, :tokens] = routes_vmem[...].astype(F32).astype(BF16)
-
-
-def forward(own_ref, near_ref, came_ref, out_ref, message_ref):
+    message_ref[...] = jnp.broadcast_to(routes_vmem[...][None], message_ref.shape)
+
+
+def forward(own_ref, near_ref, out_ref):
     rows = out_ref.shape[1] - own_ref.shape[1]
     out_ref[:, :rows] = near_ref[:, near_ref.shape[1] - rows :]
     out_ref[:, rows:] = own_ref[...]
-    tail = came_ref[came_ref.shape[0] - ROUTE_ROWS :].astype(F32).astype(jnp.int32)
-    _, choices, tokens = message_ref.shape
-    message_ref[...] = jnp.broadcast_to(tail[:choices, :tokens][None], message_ref.shape)
 
 
 def second(
@@ -142,8 +138,10 @@
     attended = (acc / total).astype(BF16)
     wide = jnp.concatenate([attended[h * q_rows : (h + 1) * q_rows] for h in range(heads)], axis=1)
 
-    blocks, _, tokens = routes_ref.shape
     experts = out_ref.shape[0]
+    blocks = routes_ref.shape[0] // lax.axis_size("seq")
+    tokens = routes_ref.shape[2]
+    mine = routes_ref[pl.ds(me * blocks, blocks)].astype(F32)
     slots = out_ref.shape[1]
     capacity = slots // blocks
     spread = lax.broadcasted_iota(jnp.int32, (tokens, q_rows), 0) == (
@@ -154,7 +152,7 @@
     expert_id = lax.broadcasted_iota(jnp.int32, (experts, q_rows), 0).astype(F32)
     named = jnp.zeros((experts, q_rows), jnp.bool_)
     for k in range(2):
-        chosen = routes_ref[:, k, :].astype(F32).astype(BF16)
+        chosen = mine[:, k, :].astype(BF16)
         by_block = jnp.dot(chosen, spread.astype(BF16), preferred_element_type=F32)
         flat = jnp.sum(jnp.where(in_block, by_block, 0.0), axis=0, keepdims=True)
         named = named | (flat == expert_id)
@@ -256,15 +254,16 @@
     )
     hbm = pl.BlockSpec(memory_space=pltpu.HBM)
     small = pltpu.CompilerParams(vmem_limit_bytes=8 << 20)
-    left_rows = 2 * shard_len + heads * q_rows + ROUTE_ROWS
-    own, left = pl.pallas_call(
+    left_rows = 2 * shard_len + heads * q_rows
+    own, left, message = pl.pallas_call(
         first,
         out_shape=(
             jax.ShapeDtypeStruct((2, shard_len, HD), BF16),
             jax.ShapeDtypeStruct((left_rows, HD), BF16),
+            jax.ShapeDtypeStruct((seq_count * expert_count, 2, tok_count), jnp.int32),
         ),
         in_specs=[hbm] * 4,
-        out_specs=(VMEM,) * 2,
+        out_specs=(VMEM,) * 3,
         scratch_shapes=[
             pltpu.VMEM(routes.shape, jnp.int32),
             pltpu.SemaphoreType.DMA((5 + heads,)),
@@ -297,19 +296,16 @@
 
     came = shifted(left, -1)
     near = shifted(own, 1)
-    beyond, message = pl.pallas_call(
+    all_routes = exchange(message, ("seq", "expert"))
+    beyond = pl.pallas_call(
         forward,
-        out_shape=(
-            jax.ShapeDtypeStruct((2, reach - 3 * shard_len, HD), BF16),
-            jax.ShapeDtypeStruct((expert_count, 2, tok_count), jnp.int32),
-        ),
-        in_specs=[VMEM] * 3,
-        out_specs=(VMEM,) * 2,
+        out_shape=jax.ShapeDtypeStruct((2, reach - 3 * shard_len, HD), BF16),
+        in_specs=[VMEM] * 2,
+        out_specs=VMEM,
         compiler_params=small,
         name="forward",
-    )(own, near, came)
+    )(own, near)
     beyond = shifted(beyond, 2)
-    row_routes = exchange(message, "expert")
 
     outgoing = pl.pallas_call(
         attend,
@@ -318,7 +314,7 @@
         out_specs=VMEM,
         compiler_params=pltpu.CompilerParams(vmem_limit_bytes=24 << 20),
         name="attend",
-    )(begin, row_routes, came, own, near, beyond)
+    )(begin, all_routes, came, own, near, beyond)
     landed = exchange(outgoing, "expert")
     packed = pl.pallas_call(
         pack,

time: 111 us -> 114 us (1.027)
  starting transfers between devices: 25.3 us -> 32.1 us
  blocking collectives: 62.6 us -> 59.4 us
    all_to_all x1, starting transfers between devices: 16.7 us -> 22 us  [exchange(): return lax.all_to_all(x, axis, split_axis=0, concat_axis=0, tiled=True)]
    ppermute x3, waiting for transfers between devices: 6.15 us -> 1.28 us  [shifted(): lax.ppermute(x, 'seq', [(i, (i + by) % seq_count) for i in range(seq_coun...]
    all_to_all x1, waiting for transfers between devices: 6.83 us -> 11.3 us  [exchange(): return lax.all_to_all(x, axis, split_axis=0, concat_axis=0, tiled=True)]
    all_to_all x2, blocking collectives: 32.5 us -> 30.9 us  [exchange(): return lax.all_to_all(x, axis, split_axis=0, concat_axis=0, tiled=True)]
    ppermute x3, starting transfers between devices: 8.61 us -> 10.2 us  [shifted(): lax.ppermute(x, 'seq', [(i, (i + by) % seq_count) for i in range(seq_coun...]
    all_gather x1, blocking collectives: 30.1 us -> 28.5 us  [shards(): incoming = lax.all_gather(packed, 'seq')]
where the time goes in v9:
time: 114 us
  blocking collectives  59.4 us (52%)
  starting transfers between devices  32.1 us (28%)
  waiting for transfers between devices  12.6 us (11%)
  Pallas kernels  9.31 us (8%)
    all_to_all x2, blocking collectives, exchange(): return lax.all_to_all(x, axis, split_axis=0, concat_axis=0, tiled=True)  30.9 us
    all_gather x1, blocking collectives, shards(): incoming = lax.all_gather(packed, 'seq')  28.5 us
    all_to_all x1, starting transfers between devices, exchange(): return lax.all_to_all(x, axis, split_axis=0, concat_axis=0, tiled=True)  22 us
    all_to_all x1, waiting for transfers between devices, exchange(): return lax.all_to_all(x, axis, split_axis=0, concat_axis=0, tiled=True)  11.3 us
    ppermute x3, starting transfers between devices, shifted(): lax.ppermute(x, 'seq', [(i, (i + by) % seq_count) for i in range(seq_coun...  10.2 us
    pallas_call x1, Pallas kernels, shards(): pl.pallas_call(functools.partial(project, expert_count), out_shape=jax.Sh...  4.49 us
  transfers between devices with their start and end apart: 4, of which 2 were waited for; matrix products, arithmetic and copies ran while one was open for 0% of the time, Pallas kernels for 1%

profile of v9, /device:TPU:112, one launch (start us, length us, event | category | flops | bytes accessed | tf_op | source)
XLA Modules:
  0.0 113.9 jit_solution(4652620902309153958)
XLA Ops:
  0.0 1.7 %first.1 = (bf16[2,256,128]{2,1,0:T(8,128)(2,1)S(1)}, bf16[768,128]{1,0:T(8,128)(2,1)S(1)}, s32[64,2,8]{2,1,0:T(2,128)}) custom-call(bf16[256,128]{1,0:T(8,128)(2,1)} %keys_ref.1, bf16[256,128]{1,0:T(8,128)(2,1)} %values_ref.1, bf16[64,512]{1,0:T(8,128)(2,1)} %q_ref.1, s32[2,8]{1,0:T(2,128)} %bitcast.5), custom_call_target="tpu_custom_call" | custom-call | tf_op jit(solution)/shard_map/first/pallas_call | solution.py:258
  1.7 3.4 %collective-permute-start.1 = (bf16[2,256,128]{2,1,0:T(8,128)(2,1)S(1)}, bf16[2,256,128]{2,1,0:T(8,128)(2,1)S(1)}, u32[]{:S(2)}, u32[]{:S(2)}) collective-permute-start(bf16[2,256,128]{2,1,0:T(8,128)(2,1)S(1)} %get-tuple-element.14.own_ref), channel_id=1, source_target_pairs={{0,8},{8,16},{16,24},{24,32},{32,40},{40,48},{48,56},{56,0},{1,9},... | collective-permute-start | bytes 393224 | tf_op jit(solution)/shard_map/ppermute | solution.py:295
  5.1 3.7 %collective-permute-start = (bf16[768,128]{1,0:T(8,128)(2,1)S(1)}, bf16[768,128]{1,0:T(8,128)(2,1)S(1)}, u32[]{:S(2)}, u32[]{:S(2)}) collective-permute-start(bf16[768,128]{1,0:T(8,128)(2,1)S(1)} %get-tuple-element.13), channel_id=1, source_target_pairs={{0,56},{8,0},{16,8},{24,16},{32,24},{40,32},{48,40},{56,48},{1,57}... | collective-permute-start | bytes 589832 | tf_op jit(solution)/shard_map/ppermute | solution.py:295
  8.7 1.3 %collective-permute-done.1.near_ref = bf16[2,256,128]{2,1,0:T(8,128)(2,1)S(1)} collective-permute-done((bf16[2,256,128]{2,1,0:T(8,128)(2,1)S(1)}, bf16[2,256,128]{2,1,0:T(8,128)(2,1)S(1)}, u32[]{:S(2)}, u32[]{:S(2)}) %collective-permute-start.1) | collective-permute-done | bytes 131104 | tf_op jit(solution)/shard_map/ppermute | solution.py:295
  10.0 3.1 %collective-permute-start.2 = (bf16[2,320,128]{2,1,0:T(8,128)(2,1)S(1)}, bf16[2,320,128]{2,1,0:T(8,128)(2,1)S(1)}, u32[]{:S(2)}, u32[]{:S(2)}) collective-permute-start(bf16[2,320,128]{2,1,0:T(8,128)(2,1)S(1)} %forward.1), channel_id=1, source_target_pairs={{0,16},{8,24},{16,32},{24,40},{32,48},{40,56},{48,0},{56,8},{1,17}... | collective-permute-start | bytes 491528 | tf_op jit(solution)/shard_map/ppermute | solution.py:295
  13.2 22.0 %all-to-all-start = ((s32[64,2,8]{2,1,0:T(2,128)}), s32[64,2,8]{2,1,0:T(2,128)S(1)}, u32[]{:S(2)}, u32[]{:S(2)}) async-start(s32[64,2,8]{2,1,0:T(2,128)} %get-tuple-element.12), calls=%async_computation | async-start | bytes 131072 | tf_op jit(solution)/shard_map/all_to_all | solution.py:21
  35.1 0.9 second.1
  36.0 11.3 %all-to-all-done.routes_ref = s32[64,2,8]{2,1,0:T(2,128)S(1)} async-done(((s32[64,2,8]{2,1,0:T(2,128)}), s32[64,2,8]{2,1,0:T(2,128)S(1)}, u32[]{:S(2)}, u32[]{:S(2)}) %all-to-all-start) | async-done | bytes 4128 | tf_op jit(solution)/shard_map/all_to_all | solution.py:21
  47.4 0.0 collective-permute-done.came_ref
  47.4 0.0 collective-permute-done.2.beyond_ref
  47.4 1.1 attend.1
  48.4 12.2 %all_to_all.15.x_ref = bf16[8,24,512]{2,1,0:T(8,128)(2,1)S(1)} all-to-all(bf16[8,24,512]{2,1,0:T(8,128)(2,1)S(1)} %attend.1), channel_id=1, replica_groups=mesh['dp'=16,'seq'=8,'expert'=8] {'expert'}, dimensions={0} | all-to-all | bytes 393216 | tf_op jit(solution)/shard_map/all_to_all | solution.py:21
  60.6 0.2 pack.1
  60.8 28.5 %all-gather.2 = s16[192,4224]{1,0:T(8,128)(2,1)S(1)} all-gather(s16[24,4224]{1,0:T(8,128)(2,1)S(1)} %pack.1), channel_id=2, replica_groups=mesh['dp'=16,'seq'=8,'expert'=8] {'seq'}, dimensions={0}, use_global_device_ids=true | all-gather | bytes 1824768 | tf_op jit(solution)/shard_map/all_gather | solution.py:327
  89.3 4.5 %project.1 = bf16[192,896]{1,0:T(8,128)(2,1)S(1)} custom-call(s16[8,24,4224]{2,1,0:T(8,128)(2,1)S(1)} %bitcast.4, bf16[1,4096,896]{2,1,0:T(8,128)(2,1)} %w_ref.1), custom_call_target="tpu_custom_call" | custom-call | tf_op jit(solution)/shard_map/project/pallas_call | solution.py:328
  93.8 0.2 reshape.10
  94.0 18.7 %all_to_all.16 = bf16[64,3,896]{2,1,0:T(4,128)(2,1)S(1)} all-to-all(bf16[64,3,896]{2,1,0:T(4,128)(2,1)S(1)} %reshape.10), channel_id=1, replica_groups=mesh['dp'=16,'seq'=8,'expert'=8] {'seq','expert'}, dimensions={0} | all-to-all | bytes 688128 | tf_op jit(solution)/shard_map/all_to_all | solution.py:21
  112.7 0.3 reshape.11.back_ref
  113.0 1.0 mix.1
  (1 shorter events, 0.0 us)
Async XLA Ops:
  1.7 8.3 %collective-permute-start.1 = (bf16[2,256,128]{2,1,0:T(8,128)(2,1)S(1)}, bf16[2,256,128]{2,1,0:T(8,128)(2,1)S(1)}, u32[]{:S(2)}, u32[]{:S(2)}) collective-permute-start(bf16[2,256,128]{2,1,0:T(8,128)(2,1)S(1)} %get-tuple-element.14.own_ref), channel_id=1, source_target_pairs={{0,8},{8,16},{16,24},{24,32},{32,40},{40,48},{48,56},{56,0},{1,9},... | collective-permute-start | bytes 393224 | tf_op jit(solution)/shard_map/ppermute | solution.py:295
  5.1 42.3 %collective-permute-start = (bf16[768,128]{1,0:T(8,128)(2,1)S(1)}, bf16[768,128]{1,0:T(8,128)(2,1)S(1)}, u32[]{:S(2)}, u32[]{:S(2)}) collective-permute-start(bf16[768,128]{1,0:T(8,128)(2,1)S(1)} %get-tuple-element.13), channel_id=1, source_target_pairs={{0,56},{8,0},{16,8},{24,16},{32,24},{40,32},{48,40},{56,48},{1,57}... | collective-permute-start | bytes 589832 | tf_op jit(solution)/shard_map/ppermute | solution.py:295
  10.0 37.3 %collective-permute-start.2 = (bf16[2,320,128]{2,1,0:T(8,128)(2,1)S(1)}, bf16[2,320,128]{2,1,0:T(8,128)(2,1)S(1)}, u32[]{:S(2)}, u32[]{:S(2)}) collective-permute-start(bf16[2,320,128]{2,1,0:T(8,128)(2,1)S(1)} %forward.1), channel_id=1, source_target_pairs={{0,16},{8,24},{16,32},{24,40},{32,48},{40,56},{48,0},{56,8},{1,17}... | collective-permute-start | bytes 491528 | tf_op jit(solution)/shard_map/ppermute | solution.py:295
  13.2 34.2 %all-to-all-start = ((s32[64,2,8]{2,1,0:T(2,128)}), s32[64,2,8]{2,1,0:T(2,128)S(1)}, u32[]{:S(2)}, u32[]{:S(2)}) async-start(s32[64,2,8]{2,1,0:T(2,128)} %get-tuple-element.12), calls=%async_computation | async-start | bytes 131072 | tf_op jit(solution)/shard_map/all_to_all | solution.py:21

commit v10 on v8

--- a/solution.py
+++ b/solution.py
@@ -12,6 +12,7 @@
 LONGEST = 1024
 FIXED = 32767
 DIGITS = 8192
+PEERS = 8
 ROUTE_ROWS = 16
 F32 = jnp.float32
 BF16 = jnp.bfloat16
@@ -145,7 +146,6 @@
     blocks, _, tokens = routes_ref.shape
     experts = out_ref.shape[0]
     slots = out_ref.shape[1]
-    capacity = slots // blocks
     spread = lax.broadcasted_iota(jnp.int32, (tokens, q_rows), 0) == (
         lax.broadcasted_iota(jnp.int32, (tokens, q_rows), 1) % tokens
     )
@@ -163,7 +163,7 @@
     earlier = (r // tokens == c // tokens) & (r < c)
     ahead = jnp.dot(named.astype(BF16), earlier.astype(BF16), preferred_element_type=F32)
     token_block = lax.broadcasted_iota(jnp.int32, (experts, q_rows), 1) // tokens
-    slot = jnp.where(named, ahead + (token_block * capacity).astype(F32), F32(-1))
+    slot = jnp.where(named, ahead * F32(blocks) + token_block.astype(F32), F32(-1))
     slot_id = lax.broadcasted_iota(jnp.int32, (slots, q_rows), 0).astype(F32)
     selector = jnp.concatenate(
         [(slot_id == slot[e : e + 1, :]).astype(F32) for e in range(experts)], axis=0
@@ -212,7 +212,7 @@
         copy(e).start()
     factor = rows(depth, HD)
     factor = factor[:, 0:1] * F32(1 / DIGITS) * jnp.exp2(factor[:, 1:2])
-    acc = jnp.zeros(out_ref.shape, F32)
+    acc = jnp.zeros((seq_count * x_ref.shape[1], w_vmem.shape[1]), F32)
     for e in range(chunks):
         x = rows(e * chunk, chunk).astype(BF16)
         copy(e).wait()
@@ -220,21 +220,34 @@
             x, w_vmem[e * chunk : (e + 1) * chunk], preferred_element_type=F32
         )
     upper = acc * factor
-    out_ref[...] = (upper / (1.0 + jnp.exp(-upper))).astype(BF16)
+    act = (upper / (1.0 + jnp.exp(-upper))).reshape(-1, PEERS, upper.shape[1])
+    tiles = upper.shape[1] // HD
+    parts = [act[:, :, j * HD : (j + 1) * HD] for j in range(tiles)]
+    parts += [jnp.zeros_like(parts[0])] * (PEERS - tiles)
+    turned = jnp.swapaxes(jnp.stack(parts, axis=1), 1, 2).astype(BF16)
+    slots = out_ref.shape[1] // PEERS
+    for s in range(seq_count):
+        for c in range(slots):
+            at = pl.ds(c * PEERS, PEERS)
+            out_ref[s * PEERS : (s + 1) * PEERS, at] = turned[s * slots + c]
 
 
 def mix(back_ref, selector_ref, column_ref, out_ref):
-    units = back_ref.shape[2]
-    for s in range(back_ref.shape[0]):
+    seq_count = back_ref.shape[0] // PEERS
+    units = out_ref.shape[1] // seq_count
+    tiles = units // HD
+    rows = selector_ref.shape[1]
+    for s in range(seq_count):
+        back = back_ref[s * PEERS : (s + 1) * PEERS].astype(F32)
+        back = jnp.swapaxes(back.reshape(rows // PEERS, PEERS, PEERS, HD), 1, 2)
+        wide = [back[:, j].reshape(rows, HD) for j in range(tiles)]
+        wide = jnp.concatenate(wide, axis=1).astype(BF16)
         both = F32(0)
         for k in range(2):
-            rows = lax.dot_general(
-                selector_ref[k],
-                back_ref[s],
-                (((0,), (0,)), ((), ())),
-                preferred_element_type=F32,
+            picked = lax.dot_general(
+                selector_ref[k], wide, (((0,), (0,)), ((), ())), preferred_element_type=F32
             )
-            both = both + rows * column_ref[k, :, 0:1]
+            both = both + picked * column_ref[k, :, 0:1]
         out_ref[:, s * units : (s + 1) * units] = both.astype(BF16)
 
 
@@ -331,7 +344,7 @@
     incoming = lax.all_gather(packed, "seq")
     act = pl.pallas_call(
         functools.partial(project, expert_count),
-        out_shape=jax.ShapeDtypeStruct((seq_count * per_expert, w_up.shape[2]), BF16),
+        out_shape=jax.ShapeDtypeStruct((seq_count * expert_count, per_expert, HD), BF16),
         in_specs=[VMEM, pl.BlockSpec(memory_space=pltpu.HBM)],
         out_specs=VMEM,
         scratch_shapes=[
@@ -341,12 +354,10 @@
         compiler_params=pltpu.CompilerParams(vmem_limit_bytes=32 << 20),
         name="project",
     )(incoming, pltpu.with_memory_space_constraint(w_up, pltpu.HBM))
-    ff_local = act.shape[1]
-    back = exchange(act.reshape(seq_count * expert_count, capacity, ff_local), ("seq", "expert"))
-    back = back.reshape(seq_count, per_expert, ff_local)
+    back = exchange(act, ("seq", "expert"))
     return pl.pallas_call(
         mix,
-        out_shape=jax.ShapeDtypeStruct((tok_count, seq_count * ff_local), BF16),
+        out_shape=jax.ShapeDtypeStruct((tok_count, seq_count * w_up.shape[2]), BF16),
         in_specs=[VMEM] * 3,
         out_specs=VMEM,
         compiler_params=pltpu.CompilerParams(vmem_limit_bytes=16 << 20),

time: 111 us -> 110 us (level)
  no operation moved by 1% of the time
where the time goes in v10:
time: 110 us
  blocking collectives  62.2 us (57%)
  starting transfers between devices  25.3 us (23%)
  waiting for transfers between devices  13 us (12%)
  Pallas kernels  9.42 us (9%)
    all_to_all x2, blocking collectives, exchange(): return lax.all_to_all(x, axis, split_axis=0, concat_axis=0, tiled=True)  32.1 us
    all_gather x1, blocking collectives, shards(): incoming = lax.all_gather(packed, 'seq')  30.1 us
    all_to_all x1, starting transfers between devices, exchange(): return lax.all_to_all(x, axis, split_axis=0, concat_axis=0, tiled=True)  16.7 us
    ppermute x3, starting transfers between devices, shifted(): lax.ppermute(x, 'seq', [(i, (i + by) % seq_count) for i in range(seq_coun...  8.61 us
    all_to_all x1, waiting for transfers between devices, exchange(): return lax.all_to_all(x, axis, split_axis=0, concat_axis=0, tiled=True)  6.83 us
    ppermute x3, waiting for transfers between devices, shifted(): lax.ppermute(x, 'seq', [(i, (i + by) % seq_count) for i in range(seq_coun...  6.15 us
    pallas_call x1, Pallas kernels, shards(): pl.pallas_call(functools.partial(project, expert_count), out_shape=jax.Sh...  4.64 us
  transfers between devices with their start and end apart: 4, of which 2 were waited for; matrix products, arithmetic and copies ran while one was open for 0% of the time, Pallas kernels for 1%

profile of v10, /device:TPU:112, one launch (start us, length us, event | category | flops | bytes accessed | tf_op | source)
XLA Modules:
  0.0 110.0 jit_solution(5673966016916240507)
XLA Ops:
  0.0 1.0 first.1
  1.0 4.8 %collective-permute-start.1 = (bf16[784,128]{1,0:T(8,128)(2,1)S(1)}, bf16[784,128]{1,0:T(8,128)(2,1)S(1)}, u32[]{:S(2)}, u32[]{:S(2)}) collective-permute-start(bf16[784,128]{1,0:T(8,128)(2,1)S(1)} %get-tuple-element.14), channel_id=1, source_target_pairs={{0,56},{8,0},{16,8},{24,16},{32,24},{40,32},{48,40},{56,48},{1,57}... | collective-permute-start | bytes 602120 | tf_op jit(solution)/shard_map/ppermute | solution.py:309
  5.8 1.9 %collective-permute-start = (bf16[2,256,128]{2,1,0:T(8,128)(2,1)S(1)}, bf16[2,256,128]{2,1,0:T(8,128)(2,1)S(1)}, u32[]{:S(2)}, u32[]{:S(2)}) collective-permute-start(bf16[2,256,128]{2,1,0:T(8,128)(2,1)S(1)} %get-tuple-element.13.own_ref), channel_id=1, source_target_pairs={{0,8},{8,16},{16,24},{24,32},{32,40},{40,48},{48,56},{56,0},{1,9},... | collective-permute-start | bytes 393224 | tf_op jit(solution)/shard_map/ppermute | solution.py:309
  7.7 6.1 %collective-permute-done.near_ref = bf16[2,256,128]{2,1,0:T(8,128)(2,1)S(1)} collective-permute-done((bf16[2,256,128]{2,1,0:T(8,128)(2,1)S(1)}, bf16[2,256,128]{2,1,0:T(8,128)(2,1)S(1)}, u32[]{:S(2)}, u32[]{:S(2)}) %collective-permute-start) | collective-permute-done | bytes 131104 | tf_op jit(solution)/shard_map/ppermute | solution.py:309
  13.9 0.0 collective-permute-done.1.came_ref
  13.9 0.6 forward.1
  14.5 1.9 %collective-permute-start.2 = (bf16[2,320,128]{2,1,0:T(8,128)(2,1)S(1)}, bf16[2,320,128]{2,1,0:T(8,128)(2,1)S(1)}, u32[]{:S(2)}, u32[]{:S(2)}) collective-permute-start(bf16[2,320,128]{2,1,0:T(8,128)(2,1)S(1)} %get-tuple-element.16), channel_id=1, source_target_pairs={{0,16},{8,24},{16,32},{24,40},{32,48},{40,56},{48,0},{56,8},{1,17}... | collective-permute-start | bytes 491528 | tf_op jit(solution)/shard_map/ppermute | solution.py:309
  16.4 16.7 %all-to-all-start = ((s32[8,2,8]{2,1,0:T(2,128)}), s32[8,2,8]{2,1,0:T(2,128)S(1)}, u32[]{:S(2)}, u32[]{:S(2)}) async-start(s32[8,2,8]{2,1,0:T(2,128)} %get-tuple-element.15), calls=%async_computation | async-start | bytes 16384 | tf_op jit(solution)/shard_map/all_to_all | solution.py:23
  33.1 0.9 second.1
  34.0 6.8 %all-to-all-done.routes_ref = s32[8,2,8]{2,1,0:T(2,128)S(1)} async-done(((s32[8,2,8]{2,1,0:T(2,128)}), s32[8,2,8]{2,1,0:T(2,128)S(1)}, u32[]{:S(2)}, u32[]{:S(2)}) %all-to-all-start) | async-done | bytes 544 | tf_op jit(solution)/shard_map/all_to_all | solution.py:23
  40.9 0.0 collective-permute-done.2.beyond_ref
  40.9 1.1 attend.1
  41.9 12.2 %all_to_all.15.x_ref = bf16[8,24,512]{2,1,0:T(8,128)(2,1)S(1)} all-to-all(bf16[8,24,512]{2,1,0:T(8,128)(2,1)S(1)} %attend.1), channel_id=1, replica_groups=mesh['dp'=16,'seq'=8,'expert'=8] {'expert'}, dimensions={0} | all-to-all | bytes 393216 | tf_op jit(solution)/shard_map/all_to_all | solution.py:23
  54.1 0.2 pack.1
  54.3 30.1 %all-gather.2 = s16[192,4224]{1,0:T(8,128)(2,1)S(1)} all-gather(s16[24,4224]{1,0:T(8,128)(2,1)S(1)} %pack.1), channel_id=2, replica_groups=mesh['dp'=16,'seq'=8,'expert'=8] {'seq'}, dimensions={0}, use_global_device_ids=true | all-gather | bytes 1824768 | tf_op jit(solution)/shard_map/all_gather | solution.py:344
  84.4 4.6 %project.1 = bf16[64,24,128]{2,1,0:T(8,128)(2,1)S(1)} custom-call(s16[8,24,4224]{2,1,0:T(8,128)(2,1)S(1)} %bitcast.4, bf16[1,4096,896]{2,1,0:T(8,128)(2,1)} %w_ref.1), custom_call_target="tpu_custom_call" | custom-call | tf_op jit(solution)/shard_map/project/pallas_call | solution.py:345
  89.0 20.0 %all_to_all.16.back_ref = bf16[64,24,128]{2,1,0:T(8,128)(2,1)S(1)} all-to-all(bf16[64,24,128]{2,1,0:T(8,128)(2,1)S(1)} %project.1), channel_id=1, replica_groups=mesh['dp'=16,'seq'=8,'expert'=8] {'seq','expert'}, dimensions={0} | all-to-all | bytes 786432 | tf_op jit(solution)/shard_map/all_to_all | solution.py:23
  109.0 1.0 mix.1
Async XLA Ops:
  1.0 12.9 %collective-permute-start.1 = (bf16[784,128]{1,0:T(8,128)(2,1)S(1)}, bf16[784,128]{1,0:T(8,128)(2,1)S(1)}, u32[]{:S(2)}, u32[]{:S(2)}) collective-permute-start(bf16[784,128]{1,0:T(8,128)(2,1)S(1)} %get-tuple-element.14), channel_id=1, source_target_pairs={{0,56},{8,0},{16,8},{24,16},{32,24},{40,32},{48,40},{56,48},{1,57}... | collective-permute-start | bytes 602120 | tf_op jit(solution)/shard_map/ppermute | solution.py:309
  5.8 8.1 %collective-permute-start = (bf16[2,256,128]{2,1,0:T(8,128)(2,1)S(1)}, bf16[2,256,128]{2,1,0:T(8,128)(2,1)S(1)}, u32[]{:S(2)}, u32[]{:S(2)}) collective-permute-start(bf16[2,256,128]{2,1,0:T(8,128)(2,1)S(1)} %get-tuple-element.13.own_ref), channel_id=1, source_target_pairs={{0,8},{8,16},{16,24},{24,32},{32,40},{40,48},{48,56},{56,0},{1,9},... | collective-permute-start | bytes 393224 | tf_op jit(solution)/shard_map/ppermute | solution.py:309
  14.5 26.3 %collective-permute-start.2 = (bf16[2,320,128]{2,1,0:T(8,128)(2,1)S(1)}, bf16[2,320,128]{2,1,0:T(8,128)(2,1)S(1)}, u32[]{:S(2)}, u32[]{:S(2)}) collective-permute-start(bf16[2,320,128]{2,1,0:T(8,128)(2,1)S(1)} %get-tuple-element.16), channel_id=1, source_target_pairs={{0,16},{8,24},{16,32},{24,40},{32,48},{40,56},{48,0},{56,8},{1,17}... | collective-permute-start | bytes 491528 | tf_op jit(solution)/shard_map/ppermute | solution.py:309
  16.4 24.4 %all-to-all-start = ((s32[8,2,8]{2,1,0:T(2,128)}), s32[8,2,8]{2,1,0:T(2,128)S(1)}, u32[]{:S(2)}, u32[]{:S(2)}) async-start(s32[8,2,8]{2,1,0:T(2,128)} %get-tuple-element.15), calls=%async_computation | async-start | bytes 16384 | tf_op jit(solution)/shard_map/all_to_all | solution.py:23

commit v11 on v10

--- a/solution.py
+++ b/solution.py
@@ -61,10 +61,13 @@
     left_ref[at : at + choices, :tokens] = routes_vmem[...].astype(F32).astype(BF16)
 
 
-def forward(own_ref, near_ref, came_ref, out_ref, message_ref):
+def forward(own_ref, near_ref, out_ref):
     rows = out_ref.shape[1] - own_ref.shape[1]
     out_ref[:, :rows] = near_ref[:, near_ref.shape[1] - rows :]
     out_ref[:, rows:] = own_ref[...]
+
+
+def spread(came_ref, message_ref):
     tail = came_ref[came_ref.shape[0] - ROUTE_ROWS :].astype(F32).astype(jnp.int32)
     _, choices, tokens = message_ref.shape
     message_ref[...] = jnp.broadcast_to(tail[:choices, :tokens][None], message_ref.shape)
@@ -308,20 +311,25 @@
     def shifted(x, by):
         return lax.ppermute(x, "seq", [(i, (i + by) % seq_count) for i in range(seq_count)])
 
+    near = shifted(own, 1)
     came = shifted(left, -1)
-    near = shifted(own, 1)
-    beyond, message = pl.pallas_call(
+    beyond = pl.pallas_call(
         forward,
-        out_shape=(
-            jax.ShapeDtypeStruct((2, reach - 3 * shard_len, HD), BF16),
-            jax.ShapeDtypeStruct((expert_count, 2, tok_count), jnp.int32),
-        ),
-        in_specs=[VMEM] * 3,
-        out_specs=(VMEM,) * 2,
+        out_shape=jax.ShapeDtypeStruct((2, reach - 3 * shard_len, HD), BF16),
+        in_specs=[VMEM] * 2,
+        out_specs=VMEM,
         compiler_params=small,
         name="forward",
-    )(own, near, came)
+    )(own, near)
     beyond = shifted(beyond, 2)
+    message = pl.pallas_call(
+        spread,
+        out_shape=jax.ShapeDtypeStruct((expert_count, 2, tok_count), jnp.int32),
+        in_specs=[VMEM],
+        out_specs=VMEM,
+        compiler_params=small,
+        name="spread",
+    )(came)
     row_routes = exchange(message, "expert")
 
     outgoing = pl.pallas_call(

time: 110 us -> 108 us (0.982)
  waiting for transfers between devices: 13 us -> 8.38 us
  starting transfers between devices: 25.3 us -> 26.9 us
    ppermute x3, waiting for transfers between devices: 6.15 us -> 1.54 us  [shifted(): lax.ppermute(x, 'seq', [(i, (i + by) % seq_count) for i in range(seq_coun...]
    ppermute x3, starting transfers between devices: 8.61 us -> 10.2 us  [shifted(): lax.ppermute(x, 'seq', [(i, (i + by) % seq_count) for i in range(seq_coun...]
    all_to_all x2, blocking collectives: 32.1 us -> 33.7 us  [exchange(): return lax.all_to_all(x, axis, split_axis=0, concat_axis=0, tiled=True)]
  transfers between devices with their start and end apart: 4 -> 4, of which waited for: 2 -> 3; matrix products, arithmetic and copies ran while one was open for 0% -> 0% of each run, Pallas kernels for 1% -> 1%
where the time goes in v11:
time: 108 us
  blocking collectives  63.2 us (59%)
  starting transfers between devices  26.9 us (25%)
  Pallas kernels  9.43 us (9%)
  waiting for transfers between devices  8.38 us (8%)
    all_to_all x2, blocking collectives, exchange(): return lax.all_to_all(x, axis, split_axis=0, concat_axis=0, tiled=True)  33.7 us
    all_gather x1, blocking collectives, shards(): incoming = lax.all_gather(packed, 'seq')  29.6 us
    all_to_all x1, starting transfers between devices, exchange(): return lax.all_to_all(x, axis, split_axis=0, concat_axis=0, tiled=True)  16.7 us
    ppermute x3, starting transfers between devices, shifted(): lax.ppermute(x, 'seq', [(i, (i + by) % seq_count) for i in range(seq_coun...  10.2 us
    all_to_all x1, waiting for transfers between devices, exchange(): return lax.all_to_all(x, axis, split_axis=0, concat_axis=0, tiled=True)  6.83 us
    pallas_call x1, Pallas kernels, shards(): pl.pallas_call(functools.partial(project, expert_count), out_shape=jax.Sh...  4.65 us
  transfers between devices with their start and end apart: 4, of which 3 were waited for; matrix products, arithmetic and copies ran while one was open for 0% of the time, Pallas kernels for 1%

profile of v11, /device:TPU:112, one launch (start us, length us, event | category | flops | bytes accessed | tf_op | source)
XLA Modules:
  0.0 108.0 jit_solution(8708541317503243255)
XLA Ops:
  0.0 1.0 first.1
  1.0 3.4 %collective-permute-start.1 = (bf16[2,256,128]{2,1,0:T(8,128)(2,1)S(1)}, bf16[2,256,128]{2,1,0:T(8,128)(2,1)S(1)}, u32[]{:S(2)}, u32[]{:S(2)}) collective-permute-start(bf16[2,256,128]{2,1,0:T(8,128)(2,1)S(1)} %get-tuple-element.12.own_ref), channel_id=1, source_target_pairs={{0,8},{8,16},{16,24},{24,32},{32,40},{40,48},{48,56},{56,0},{1,9},... | collective-permute-start | bytes 393224 | tf_op jit(solution)/shard_map/ppermute | solution.py:312
  4.4 3.7 %collective-permute-start = (bf16[784,128]{1,0:T(8,128)(2,1)S(1)}, bf16[784,128]{1,0:T(8,128)(2,1)S(1)}, u32[]{:S(2)}, u32[]{:S(2)}) collective-permute-start(bf16[784,128]{1,0:T(8,128)(2,1)S(1)} %get-tuple-element.11), channel_id=1, source_target_pairs={{0,56},{8,0},{16,8},{24,16},{32,24},{40,32},{48,40},{56,48},{1,57}... | collective-permute-start | bytes 602120 | tf_op jit(solution)/shard_map/ppermute | solution.py:312
  8.1 1.3 %collective-permute-done.1.near_ref = bf16[2,256,128]{2,1,0:T(8,128)(2,1)S(1)} collective-permute-done((bf16[2,256,128]{2,1,0:T(8,128)(2,1)S(1)}, bf16[2,256,128]{2,1,0:T(8,128)(2,1)S(1)}, u32[]{:S(2)}, u32[]{:S(2)}) %collective-permute-start.1) | collective-permute-done | bytes 131104 | tf_op jit(solution)/shard_map/ppermute | solution.py:312
  9.4 3.1 %collective-permute-start.2 = (bf16[2,320,128]{2,1,0:T(8,128)(2,1)S(1)}, bf16[2,320,128]{2,1,0:T(8,128)(2,1)S(1)}, u32[]{:S(2)}, u32[]{:S(2)}) collective-permute-start(bf16[2,320,128]{2,1,0:T(8,128)(2,1)S(1)} %forward.1), channel_id=1, source_target_pairs={{0,16},{8,24},{16,32},{24,40},{32,48},{40,56},{48,0},{56,8},{1,17}... | collective-permute-start | bytes 491528 | tf_op jit(solution)/shard_map/ppermute | solution.py:312
  12.5 0.3 collective-permute-done.came_ref
  12.8 0.6 spread.1
  13.4 16.7 %all-to-all-start = ((s32[8,2,8]{2,1,0:T(2,128)}), s32[8,2,8]{2,1,0:T(2,128)S(1)}, u32[]{:S(2)}, u32[]{:S(2)}) async-start(s32[8,2,8]{2,1,0:T(2,128)} %spread.1), calls=%async_computation | async-start | bytes 16384 | tf_op jit(solution)/shard_map/all_to_all | solution.py:23
  30.1 0.9 second.1
  31.0 6.8 %all-to-all-done.routes_ref = s32[8,2,8]{2,1,0:T(2,128)S(1)} async-done(((s32[8,2,8]{2,1,0:T(2,128)}), s32[8,2,8]{2,1,0:T(2,128)S(1)}, u32[]{:S(2)}, u32[]{:S(2)}) %all-to-all-start) | async-done | bytes 544 | tf_op jit(solution)/shard_map/all_to_all | solution.py:23
  37.8 0.0 collective-permute-done.2.beyond_ref
  37.8 1.1 %attend.1 = bf16[8,24,512]{2,1,0:T(8,128)(2,1)S(1)} custom-call(s32[64,128]{1,0:T(8,128)S(1)} %get-tuple-element.10.begin_ref, s32[8,2,8]{2,1,0:T(2,128)S(1)} %all-to-all-done.routes_ref, bf16[784,128]{1,0:T(8,128)(2,1)S(1)} %collective-permute-done.came_ref, bf16[2,256,128]{2,1,0:T(8,128)(2,1)S(1)} %get-tuple-element.12.own_ref, ...), custom_call_target="tpu_custom_call" | custom-call | tf_op jit(solution)/shard_map/attend/pallas_call | solution.py:335
  38.9 12.2 %all_to_all.15.x_ref = bf16[8,24,512]{2,1,0:T(8,128)(2,1)S(1)} all-to-all(bf16[8,24,512]{2,1,0:T(8,128)(2,1)S(1)} %attend.1), channel_id=1, replica_groups=mesh['dp'=16,'seq'=8,'expert'=8] {'expert'}, dimensions={0} | all-to-all | bytes 393216 | tf_op jit(solution)/shard_map/all_to_all | solution.py:23
  51.1 0.2 pack.1
  51.3 29.6 %all-gather.2 = s16[192,4224]{1,0:T(8,128)(2,1)S(1)} all-gather(s16[24,4224]{1,0:T(8,128)(2,1)S(1)} %pack.1), channel_id=2, replica_groups=mesh['dp'=16,'seq'=8,'expert'=8] {'seq'}, dimensions={0}, use_global_device_ids=true | all-gather | bytes 1824768 | tf_op jit(solution)/shard_map/all_gather | solution.py:352
  80.8 4.7 %project.1 = bf16[64,24,128]{2,1,0:T(8,128)(2,1)S(1)} custom-call(s16[8,24,4224]{2,1,0:T(8,128)(2,1)S(1)} %bitcast.4, bf16[1,4096,896]{2,1,0:T(8,128)(2,1)} %w_ref.1), custom_call_target="tpu_custom_call" | custom-call | tf_op jit(solution)/shard_map/project/pallas_call | solution.py:353
  85.5 21.5 %all_to_all.16.back_ref = bf16[64,24,128]{2,1,0:T(8,128)(2,1)S(1)} all-to-all(bf16[64,24,128]{2,1,0:T(8,128)(2,1)S(1)} %project.1), channel_id=1, replica_groups=mesh['dp'=16,'seq'=8,'expert'=8] {'seq','expert'}, dimensions={0} | all-to-all | bytes 786432 | tf_op jit(solution)/shard_map/all_to_all | solution.py:23
  107.0 1.0 mix.1
  (1 shorter events, 0.0 us)
Async XLA Ops:
  1.0 8.3 %collective-permute-start.1 = (bf16[2,256,128]{2,1,0:T(8,128)(2,1)S(1)}, bf16[2,256,128]{2,1,0:T(8,128)(2,1)S(1)}, u32[]{:S(2)}, u32[]{:S(2)}) collective-permute-start(bf16[2,256,128]{2,1,0:T(8,128)(2,1)S(1)} %get-tuple-element.12.own_ref), channel_id=1, source_target_pairs={{0,8},{8,16},{16,24},{24,32},{32,40},{40,48},{48,56},{56,0},{1,9},... | collective-permute-start | bytes 393224 | tf_op jit(solution)/shard_map/ppermute | solution.py:312
  4.4 8.3 %collective-permute-start = (bf16[784,128]{1,0:T(8,128)(2,1)S(1)}, bf16[784,128]{1,0:T(8,128)(2,1)S(1)}, u32[]{:S(2)}, u32[]{:S(2)}) collective-permute-start(bf16[784,128]{1,0:T(8,128)(2,1)S(1)} %get-tuple-element.11), channel_id=1, source_target_pairs={{0,56},{8,0},{16,8},{24,16},{32,24},{40,32},{48,40},{56,48},{1,57}... | collective-permute-start | bytes 602120 | tf_op jit(solution)/shard_map/ppermute | solution.py:312
  9.4 28.4 %collective-permute-start.2 = (bf16[2,320,128]{2,1,0:T(8,128)(2,1)S(1)}, bf16[2,320,128]{2,1,0:T(8,128)(2,1)S(1)}, u32[]{:S(2)}, u32[]{:S(2)}) collective-permute-start(bf16[2,320,128]{2,1,0:T(8,128)(2,1)S(1)} %forward.1), channel_id=1, source_target_pairs={{0,16},{8,24},{16,32},{24,40},{32,48},{40,56},{48,0},{56,8},{1,17}... | collective-permute-start | bytes 491528 | tf_op jit(solution)/shard_map/ppermute | solution.py:312
  13.4 24.4 %all-to-all-start = ((s32[8,2,8]{2,1,0:T(2,128)}), s32[8,2,8]{2,1,0:T(2,128)S(1)}, u32[]{:S(2)}, u32[]{:S(2)}) async-start(s32[8,2,8]{2,1,0:T(2,128)} %spread.1), calls=%async_computation | async-start | bytes 16384 | tf_op jit(solution)/shard_map/all_to_all | solution.py:23

commit v12 on v11

--- a/solution.py
+++ b/solution.py
@@ -115,10 +115,10 @@
         column_ref[k] = jnp.broadcast_to(gate, column_ref.shape[1:])
 
 
-def attend(begin_ref, routes_ref, came_ref, own_ref, near_ref, beyond_ref, out_ref):
+def attend(begin_ref, came_ref, own_ref, near_ref, beyond_ref, out_ref):
     shard_len = own_ref.shape[1]
     q_rows = begin_ref.shape[0]
-    heads = out_ref.shape[2] // HD
+    heads = out_ref.shape[1] // HD
     me = worked_on()
     rows = heads * q_rows
     queries = came_ref[2 * shard_len : 2 * shard_len + rows]
@@ -144,8 +144,12 @@
         total = total + jnp.sum(weight, axis=1, keepdims=True)
         acc = acc + jnp.dot(weight.astype(BF16), values, preferred_element_type=F32)
     attended = (acc / total).astype(BF16)
-    wide = jnp.concatenate([attended[h * q_rows : (h + 1) * q_rows] for h in range(heads)], axis=1)
-
+    for h in range(heads):
+        out_ref[:, h * HD : (h + 1) * HD] = attended[h * q_rows : (h + 1) * q_rows]
+
+
+def select(wide_ref, routes_ref, out_ref):
+    q_rows = wide_ref.shape[0]
     blocks, _, tokens = routes_ref.shape
     experts = out_ref.shape[0]
     slots = out_ref.shape[1]
@@ -171,7 +175,7 @@
     selector = jnp.concatenate(
         [(slot_id == slot[e : e + 1, :]).astype(F32) for e in range(experts)], axis=0
     ).astype(BF16)
-    picked = jnp.dot(selector, wide, preferred_element_type=F32)
+    picked = jnp.dot(selector, wide_ref[...], preferred_element_type=F32)
     out_ref[...] = picked.reshape(out_ref.shape).astype(BF16)
 
 
@@ -288,7 +292,7 @@
         compiler_params=small,
         name="first",
     )(keys, values, queries, routes)
-    begin, selectors, columns = pl.pallas_call(
+    bounds = pl.pallas_call(
         functools.partial(second, shard_len, q_rows),
         out_shape=(
             jax.ShapeDtypeStruct((q_rows, HD), jnp.int32),
@@ -307,6 +311,7 @@
         cost_estimate=pl.CostEstimate(flops=4_000_000, bytes_accessed=200_000, transcendentals=0),
         name="second",
     )(lengths, routes, gates)
+    begin, selectors, columns = bounds
 
     def shifted(x, by):
         return lax.ppermute(x, "seq", [(i, (i + by) % seq_count) for i in range(seq_count)])
@@ -332,14 +337,25 @@
     )(came)
     row_routes = exchange(message, "expert")
 
+    attended = pl.pallas_call(
+        attend,
+        out_shape=jax.ShapeDtypeStruct((q_rows, width), BF16),
+        in_specs=[VMEM] * 5,
+        out_specs=VMEM,
+        compiler_params=pltpu.CompilerParams(vmem_limit_bytes=24 << 20),
+        cost_estimate=pl.CostEstimate(
+            flops=4 * heads * q_rows * reach * HD, bytes_accessed=0, transcendentals=0
+        ),
+        name="attend",
+    )(begin, came, own, near, beyond)
     outgoing = pl.pallas_call(
-        attend,
+        select,
         out_shape=jax.ShapeDtypeStruct((expert_count, per_expert, width), BF16),
-        in_specs=[VMEM] * 6,
-        out_specs=VMEM,
-        compiler_params=pltpu.CompilerParams(vmem_limit_bytes=24 << 20),
-        name="attend",
-    )(begin, row_routes, came, own, near, beyond)
+        in_specs=[VMEM] * 2,
+        out_specs=VMEM,
+        compiler_params=small,
+        name="select",
+    )(attended, row_routes)
     landed = exchange(outgoing, "expert")
     packed = pl.pallas_call(
         pack,

time: 108 us -> 108 us (level)
    all_to_all x2, blocking collectives: 33.7 us -> 32.3 us  [exchange(): return lax.all_to_all(x, axis, split_axis=0, concat_axis=0, tiled=True)]
  transfers between devices with their start and end apart: 4 -> 4, of which waited for: 3 -> 2; matrix products, arithmetic and copies ran while one was open for 0% -> 0% of each run, Pallas kernels for 1% -> 2%
where the time goes in v12:
time: 108 us
  blocking collectives  62.8 us (58%)
  starting transfers between devices  26.9 us (25%)
  Pallas kernels  9.57 us (9%)
  waiting for transfers between devices  8.21 us (8%)
    all_to_all x2, blocking collectives, exchange(): return lax.all_to_all(x, axis, split_axis=0, concat_axis=0, tiled=True)  32.3 us
    all_gather x1, blocking collectives, shards(): incoming = lax.all_gather(packed, 'seq')  30.5 us
    all_to_all x1, starting transfers between devices, exchange(): return lax.all_to_all(x, axis, split_axis=0, concat_axis=0, tiled=True)  16.8 us
    ppermute x3, starting transfers between devices, shifted(): lax.ppermute(x, 'seq', [(i, (i + by) % seq_count) for i in range(seq_coun...  10.2 us
    all_to_all x1, waiting for transfers between devices, exchange(): return lax.all_to_all(x, axis, split_axis=0, concat_axis=0, tiled=True)  6.93 us
    pallas_call x1, Pallas kernels, shards(): pl.pallas_call(functools.partial(project, expert_count), out_shape=jax.Sh...  4.64 us
  transfers between devices with their start and end apart: 4, of which 2 were waited for; matrix products, arithmetic and copies ran while one was open for 0% of the time, Pallas kernels for 2%

profile of v12, /device:TPU:112, one launch (start us, length us, event | category | flops | bytes accessed | tf_op | source)
XLA Modules:
  0.0 107.6 jit_solution(8553009732546955928)
XLA Ops:
  0.0 1.0 first.1
  1.0 3.4 %collective-permute-start.1 = (bf16[2,256,128]{2,1,0:T(8,128)(2,1)S(1)}, bf16[2,256,128]{2,1,0:T(8,128)(2,1)S(1)}, u32[]{:S(2)}, u32[]{:S(2)}) collective-permute-start(bf16[2,256,128]{2,1,0:T(8,128)(2,1)S(1)} %get-tuple-element.12.own_ref), channel_id=1, source_target_pairs={{0,8},{8,16},{16,24},{24,32},{32,40},{40,48},{48,56},{56,0},{1,9},... | collective-permute-start | bytes 393224 | tf_op jit(solution)/shard_map/ppermute | solution.py:317
  4.4 3.7 %collective-permute-start = (bf16[784,128]{1,0:T(8,128)(2,1)S(1)}, bf16[784,128]{1,0:T(8,128)(2,1)S(1)}, u32[]{:S(2)}, u32[]{:S(2)}) collective-permute-start(bf16[784,128]{1,0:T(8,128)(2,1)S(1)} %get-tuple-element.11), channel_id=1, source_target_pairs={{0,56},{8,0},{16,8},{24,16},{32,24},{40,32},{48,40},{56,48},{1,57}... | collective-permute-start | bytes 602120 | tf_op jit(solution)/shard_map/ppermute | solution.py:317
  8.1 1.3 %collective-permute-done.1.near_ref = bf16[2,256,128]{2,1,0:T(8,128)(2,1)S(1)} collective-permute-done((bf16[2,256,128]{2,1,0:T(8,128)(2,1)S(1)}, bf16[2,256,128]{2,1,0:T(8,128)(2,1)S(1)}, u32[]{:S(2)}, u32[]{:S(2)}) %collective-permute-start.1) | collective-permute-done | bytes 131104 | tf_op jit(solution)/shard_map/ppermute | solution.py:317
  9.4 3.1 %collective-permute-start.2 = (bf16[2,320,128]{2,1,0:T(8,128)(2,1)S(1)}, bf16[2,320,128]{2,1,0:T(8,128)(2,1)S(1)}, u32[]{:S(2)}, u32[]{:S(2)}) collective-permute-start(bf16[2,320,128]{2,1,0:T(8,128)(2,1)S(1)} %forward.1), channel_id=1, source_target_pairs={{0,16},{8,24},{16,32},{24,40},{32,48},{40,56},{48,0},{56,8},{1,17}... | collective-permute-start | bytes 491528 | tf_op jit(solution)/shard_map/ppermute | solution.py:317
  12.5 0.9 second.1
  13.4 0.0 collective-permute-done.came_ref
  13.4 0.6 spread.1
  14.0 16.8 %all-to-all-start = ((s32[8,2,8]{2,1,0:T(2,128)}), s32[8,2,8]{2,1,0:T(2,128)S(1)}, u32[]{:S(2)}, u32[]{:S(2)}) async-start(s32[8,2,8]{2,1,0:T(2,128)} %spread.1), calls=%async_computation | async-start | bytes 16384 | tf_op jit(solution)/shard_map/all_to_all | solution.py:23
  30.8 0.0 collective-permute-done.2.beyond_ref
  30.8 0.8 attend.1.wide_ref
  31.6 6.9 %all-to-all-done.routes_ref = s32[8,2,8]{2,1,0:T(2,128)S(1)} async-done(((s32[8,2,8]{2,1,0:T(2,128)}), s32[8,2,8]{2,1,0:T(2,128)S(1)}, u32[]{:S(2)}, u32[]{:S(2)}) %all-to-all-start) | async-done | bytes 544 | tf_op jit(solution)/shard_map/all_to_all | solution.py:23
  38.5 0.4 select.1
  39.0 12.2 %all_to_all.15.x_ref = bf16[8,24,512]{2,1,0:T(8,128)(2,1)S(1)} all-to-all(bf16[8,24,512]{2,1,0:T(8,128)(2,1)S(1)} %select.1), channel_id=1, replica_groups=mesh['dp'=16,'seq'=8,'expert'=8] {'expert'}, dimensions={0} | all-to-all | bytes 393216 | tf_op jit(solution)/shard_map/all_to_all | solution.py:23
  51.2 0.2 pack.1
  51.3 30.5 %all-gather.2 = s16[192,4224]{1,0:T(8,128)(2,1)S(1)} all-gather(s16[24,4224]{1,0:T(8,128)(2,1)S(1)} %pack.1), channel_id=2, replica_groups=mesh['dp'=16,'seq'=8,'expert'=8] {'seq'}, dimensions={0}, use_global_device_ids=true | all-gather | bytes 1824768 | tf_op jit(solution)/shard_map/all_gather | solution.py:368
  81.9 4.6 %project.1 = bf16[64,24,128]{2,1,0:T(8,128)(2,1)S(1)} custom-call(s16[8,24,4224]{2,1,0:T(8,128)(2,1)S(1)} %bitcast.4, bf16[1,4096,896]{2,1,0:T(8,128)(2,1)} %w_ref.1), custom_call_target="tpu_custom_call" | custom-call | tf_op jit(solution)/shard_map/project/pallas_call | solution.py:369
  86.5 20.1 %all_to_all.16.back_ref = bf16[64,24,128]{2,1,0:T(8,128)(2,1)S(1)} all-to-all(bf16[64,24,128]{2,1,0:T(8,128)(2,1)S(1)} %project.1), channel_id=1, replica_groups=mesh['dp'=16,'seq'=8,'expert'=8] {'seq','expert'}, dimensions={0} | all-to-all | bytes 786432 | tf_op jit(solution)/shard_map/all_to_all | solution.py:23
  106.6 1.0 mix.1
  (1 shorter events, 0.0 us)
Async XLA Ops:
  1.0 8.3 %collective-permute-start.1 = (bf16[2,256,128]{2,1,0:T(8,128)(2,1)S(1)}, bf16[2,256,128]{2,1,0:T(8,128)(2,1)S(1)}, u32[]{:S(2)}, u32[]{:S(2)}) collective-permute-start(bf16[2,256,128]{2,1,0:T(8,128)(2,1)S(1)} %get-tuple-element.12.own_ref), channel_id=1, source_target_pairs={{0,8},{8,16},{16,24},{24,32},{32,40},{40,48},{48,56},{56,0},{1,9},... | collective-permute-start | bytes 393224 | tf_op jit(solution)/shard_map/ppermute | solution.py:317
  4.4 9.0 %collective-permute-start = (bf16[784,128]{1,0:T(8,128)(2,1)S(1)}, bf16[784,128]{1,0:T(8,128)(2,1)S(1)}, u32[]{:S(2)}, u32[]{:S(2)}) collective-permute-start(bf16[784,128]{1,0:T(8,128)(2,1)S(1)} %get-tuple-element.11), channel_id=1, source_target_pairs={{0,56},{8,0},{16,8},{24,16},{32,24},{40,32},{48,40},{56,48},{1,57}... | collective-permute-start | bytes 602120 | tf_op jit(solution)/shard_map/ppermute | solution.py:317
  9.4 21.4 %collective-permute-start.2 = (bf16[2,320,128]{2,1,0:T(8,128)(2,1)S(1)}, bf16[2,320,128]{2,1,0:T(8,128)(2,1)S(1)}, u32[]{:S(2)}, u32[]{:S(2)}) collective-permute-start(bf16[2,320,128]{2,1,0:T(8,128)(2,1)S(1)} %forward.1), channel_id=1, source_target_pairs={{0,16},{8,24},{16,32},{24,40},{32,48},{40,56},{48,0},{56,8},{1,17}... | collective-permute-start | bytes 491528 | tf_op jit(solution)/shard_map/ppermute | solution.py:317
  14.0 24.5 %all-to-all-start = ((s32[8,2,8]{2,1,0:T(2,128)}), s32[8,2,8]{2,1,0:T(2,128)S(1)}, u32[]{:S(2)}, u32[]{:S(2)}) async-start(s32[8,2,8]{2,1,0:T(2,128)} %spread.1), calls=%async_computation | async-start | bytes 16384 | tf_op jit(solution)/shard_map/all_to_all | solution.py:23

commit v13 on v12

--- a/solution.py
+++ b/solution.py
@@ -95,7 +95,7 @@
         start = start + lengths_ref[:, j : j + 1]
     begin_ref[...] = begin
 
-    _, rows, tokens = selector_ref.shape
+    rows, tokens = selector_ref.shape[0], selector_ref.shape[1] // 2
     capacity = 3
     row = lax.broadcasted_iota(jnp.int32, (rows, tokens), 0)
     named = [routes[k : k + 1, :] == row // capacity for k in range(2)]
@@ -109,7 +109,8 @@
         lax.broadcasted_iota(jnp.int32, (tokens, tokens), 1)
     )
     for k in range(2):
-        selector_ref[k] = (named[k] & right).astype(F32).astype(BF16)
+        chosen = (named[k] & right).astype(F32).astype(BF16)
+        selector_ref[:, k * tokens : (k + 1) * tokens] = chosen
         gate = jnp.where(diagonal, gates_ref[k : k + 1, :], F32(0))
         gate = jnp.sum(gate, axis=1, keepdims=True)
         column_ref[k] = jnp.broadcast_to(gate, column_ref.shape[1:])
@@ -243,18 +244,17 @@
     seq_count = back_ref.shape[0] // PEERS
     units = out_ref.shape[1] // seq_count
     tiles = units // HD
-    rows = selector_ref.shape[1]
+    rows = selector_ref.shape[0]
+    selectors = selector_ref[...]
     for s in range(seq_count):
         back = back_ref[s * PEERS : (s + 1) * PEERS].astype(F32)
         back = jnp.swapaxes(back.reshape(rows // PEERS, PEERS, PEERS, HD), 1, 2)
         wide = [back[:, j].reshape(rows, HD) for j in range(tiles)]
         wide = jnp.concatenate(wide, axis=1).astype(BF16)
-        both = F32(0)
-        for k in range(2):
-            picked = lax.dot_general(
-                selector_ref[k], wide, (((0,), (0,)), ((), ())), preferred_element_type=F32
-            )
-            both = both + picked * column_ref[k, :, 0:1]
+        picked = lax.dot_general(
+            selectors, wide, (((0,), (0,)), ((), ())), preferred_element_type=F32
+        )
+        both = picked[:PEERS] * column_ref[0, :, 0:1] + picked[PEERS:] * column_ref[1, :, 0:1]
         out_ref[:, s * units : (s + 1) * units] = both.astype(BF16)
 
 
@@ -296,7 +296,7 @@
         functools.partial(second, shard_len, q_rows),
         out_shape=(
             jax.ShapeDtypeStruct((q_rows, HD), jnp.int32),
-            jax.ShapeDtypeStruct((2, per_expert, tok_count), BF16),
+            jax.ShapeDtypeStruct((per_expert, 2 * tok_count), BF16),
             jax.ShapeDtypeStruct((2, tok_count, HD), F32),
         ),
         in_specs=[hbm] * 3,

time: 108 us -> 108 us (level)
  no operation moved by 1% of the time
where the time goes in v13:
time: 108 us
  blocking collectives  62.8 us (58%)
  starting transfers between devices  26.9 us (25%)
  Pallas kernels  9.58 us (9%)
  waiting for transfers between devices  8.21 us (8%)
    all_to_all x2, blocking collectives, exchange(): return lax.all_to_all(x, axis, split_axis=0, concat_axis=0, tiled=True)  32.4 us
    all_gather x1, blocking collectives, shards(): incoming = lax.all_gather(packed, 'seq')  30.5 us
    all_to_all x1, starting transfers between devices, exchange(): return lax.all_to_all(x, axis, split_axis=0, concat_axis=0, tiled=True)  16.8 us
    ppermute x3, starting transfers between devices, shifted(): lax.ppermute(x, 'seq', [(i, (i + by) % seq_count) for i in range(seq_coun...  10.2 us
    all_to_all x1, waiting for transfers between devices, exchange(): return lax.all_to_all(x, axis, split_axis=0, concat_axis=0, tiled=True)  6.93 us
    pallas_call x1, Pallas kernels, shards(): pl.pallas_call(functools.partial(project, expert_count), out_shape=jax.Sh...  4.65 us
  transfers between devices with their start and end apart: 4, of which 2 were waited for; matrix products, arithmetic and copies ran while one was open for 0% of the time, Pallas kernels for 2%

profile of v13, /device:TPU:112, one launch (start us, length us, event | category | flops | bytes accessed | tf_op | source)
XLA Modules:
  0.0 107.6 jit_solution(10913757973140655774)
XLA Ops:
  0.0 1.0 first.1
  1.0 3.4 %collective-permute-start.1 = (bf16[2,256,128]{2,1,0:T(8,128)(2,1)S(1)}, bf16[2,256,128]{2,1,0:T(8,128)(2,1)S(1)}, u32[]{:S(2)}, u32[]{:S(2)}) collective-permute-start(bf16[2,256,128]{2,1,0:T(8,128)(2,1)S(1)} %get-tuple-element.12.own_ref), channel_id=1, source_target_pairs={{0,8},{8,16},{16,24},{24,32},{32,40},{40,48},{48,56},{56,0},{1,9},... | collective-permute-start | bytes 393224 | tf_op jit(solution)/shard_map/ppermute | solution.py:317
  4.4 3.7 %collective-permute-start = (bf16[784,128]{1,0:T(8,128)(2,1)S(1)}, bf16[784,128]{1,0:T(8,128)(2,1)S(1)}, u32[]{:S(2)}, u32[]{:S(2)}) collective-permute-start(bf16[784,128]{1,0:T(8,128)(2,1)S(1)} %get-tuple-element.11), channel_id=1, source_target_pairs={{0,56},{8,0},{16,8},{24,16},{32,24},{40,32},{48,40},{56,48},{1,57}... | collective-permute-start | bytes 602120 | tf_op jit(solution)/shard_map/ppermute | solution.py:317
  8.1 1.3 %collective-permute-done.1.near_ref = bf16[2,256,128]{2,1,0:T(8,128)(2,1)S(1)} collective-permute-done((bf16[2,256,128]{2,1,0:T(8,128)(2,1)S(1)}, bf16[2,256,128]{2,1,0:T(8,128)(2,1)S(1)}, u32[]{:S(2)}, u32[]{:S(2)}) %collective-permute-start.1) | collective-permute-done | bytes 131104 | tf_op jit(solution)/shard_map/ppermute | solution.py:317
  9.4 3.1 %collective-permute-start.2 = (bf16[2,320,128]{2,1,0:T(8,128)(2,1)S(1)}, bf16[2,320,128]{2,1,0:T(8,128)(2,1)S(1)}, u32[]{:S(2)}, u32[]{:S(2)}) collective-permute-start(bf16[2,320,128]{2,1,0:T(8,128)(2,1)S(1)} %forward.1), channel_id=1, source_target_pairs={{0,16},{8,24},{16,32},{24,40},{32,48},{40,56},{48,0},{56,8},{1,17}... | collective-permute-start | bytes 491528 | tf_op jit(solution)/shard_map/ppermute | solution.py:317
  12.5 0.9 second.1
  13.5 0.0 collective-permute-done.came_ref
  13.5 0.6 spread.1
  14.1 16.8 %all-to-all-start = ((s32[8,2,8]{2,1,0:T(2,128)}), s32[8,2,8]{2,1,0:T(2,128)S(1)}, u32[]{:S(2)}, u32[]{:S(2)}) async-start(s32[8,2,8]{2,1,0:T(2,128)} %spread.1), calls=%async_computation | async-start | bytes 16384 | tf_op jit(solution)/shard_map/all_to_all | solution.py:23
  30.8 0.0 collective-permute-done.2.beyond_ref
  30.9 0.8 attend.1.wide_ref
  31.6 6.9 %all-to-all-done.routes_ref = s32[8,2,8]{2,1,0:T(2,128)S(1)} async-done(((s32[8,2,8]{2,1,0:T(2,128)}), s32[8,2,8]{2,1,0:T(2,128)S(1)}, u32[]{:S(2)}, u32[]{:S(2)}) %all-to-all-start) | async-done | bytes 544 | tf_op jit(solution)/shard_map/all_to_all | solution.py:23
  38.6 0.4 select.1
  39.0 12.2 %all_to_all.15.x_ref = bf16[8,24,512]{2,1,0:T(8,128)(2,1)S(1)} all-to-all(bf16[8,24,512]{2,1,0:T(8,128)(2,1)S(1)} %select.1), channel_id=1, replica_groups=mesh['dp'=16,'seq'=8,'expert'=8] {'expert'}, dimensions={0} | all-to-all | bytes 393216 | tf_op jit(solution)/shard_map/all_to_all | solution.py:23
  51.2 0.2 pack.1
  51.4 30.5 %all-gather.2 = s16[192,4224]{1,0:T(8,128)(2,1)S(1)} all-gather(s16[24,4224]{1,0:T(8,128)(2,1)S(1)} %pack.1), channel_id=2, replica_groups=mesh['dp'=16,'seq'=8,'expert'=8] {'seq'}, dimensions={0}, use_global_device_ids=true | all-gather | bytes 1824768 | tf_op jit(solution)/shard_map/all_gather | solution.py:368
  81.8 4.6 %project.1 = bf16[64,24,128]{2,1,0:T(8,128)(2,1)S(1)} custom-call(s16[8,24,4224]{2,1,0:T(8,128)(2,1)S(1)} %bitcast.4, bf16[1,4096,896]{2,1,0:T(8,128)(2,1)} %w_ref.1), custom_call_target="tpu_custom_call" | custom-call | tf_op jit(solution)/shard_map/project/pallas_call | solution.py:369
  86.5 20.2 %all_to_all.16.back_ref = bf16[64,24,128]{2,1,0:T(8,128)(2,1)S(1)} all-to-all(bf16[64,24,128]{2,1,0:T(8,128)(2,1)S(1)} %project.1), channel_id=1, replica_groups=mesh['dp'=16,'seq'=8,'expert'=8] {'seq','expert'}, dimensions={0} | all-to-all | bytes 786432 | tf_op jit(solution)/shard_map/all_to_all | solution.py:23
  106.7 1.0 mix.1
  (1 shorter events, 0.0 us)
Async XLA Ops:
  1.0 8.3 %collective-permute-start.1 = (bf16[2,256,128]{2,1,0:T(8,128)(2,1)S(1)}, bf16[2,256,128]{2,1,0:T(8,128)(2,1)S(1)}, u32[]{:S(2)}, u32[]{:S(2)}) collective-permute-start(bf16[2,256,128]{2,1,0:T(8,128)(2,1)S(1)} %get-tuple-element.12.own_ref), channel_id=1, source_target_pairs={{0,8},{8,16},{16,24},{24,32},{32,40},{40,48},{48,56},{56,0},{1,9},... | collective-permute-start | bytes 393224 | tf_op jit(solution)/shard_map/ppermute | solution.py:317
  4.4 9.0 %collective-permute-start = (bf16[784,128]{1,0:T(8,128)(2,1)S(1)}, bf16[784,128]{1,0:T(8,128)(2,1)S(1)}, u32[]{:S(2)}, u32[]{:S(2)}) collective-permute-start(bf16[784,128]{1,0:T(8,128)(2,1)S(1)} %get-tuple-element.11), channel_id=1, source_target_pairs={{0,56},{8,0},{16,8},{24,16},{32,24},{40,32},{48,40},{56,48},{1,57}... | collective-permute-start | bytes 602120 | tf_op jit(solution)/shard_map/ppermute | solution.py:317
  9.4 21.5 %collective-permute-start.2 = (bf16[2,320,128]{2,1,0:T(8,128)(2,1)S(1)}, bf16[2,320,128]{2,1,0:T(8,128)(2,1)S(1)}, u32[]{:S(2)}, u32[]{:S(2)}) collective-permute-start(bf16[2,320,128]{2,1,0:T(8,128)(2,1)S(1)} %forward.1), channel_id=1, source_target_pairs={{0,16},{8,24},{16,32},{24,40},{32,48},{40,56},{48,0},{56,8},{1,17}... | collective-permute-start | bytes 491528 | tf_op jit(solution)/shard_map/ppermute | solution.py:317
  14.1 24.5 %all-to-all-start = ((s32[8,2,8]{2,1,0:T(2,128)}), s32[8,2,8]{2,1,0:T(2,128)S(1)}, u32[]{:S(2)}, u32[]{:S(2)}) async-start(s32[8,2,8]{2,1,0:T(2,128)} %spread.1), calls=%async_computation | async-start | bytes 16384 | tf_op jit(solution)/shard_map/all_to_all | solution.py:23
